TPU v7x, 128 devices: a whole 4x4x4 slice. The times are simulated.
128 devices in a mesh: dp: 16 (over z, y), fsdp: 8 (over x, core).
Axes of the slice: x: 4, y: 4, z: 4, core: 2. Of those that a mesh axis runs over, the one named last changes fastest.
Arguments:
- x_in: bfloat16 [128, 256, 768], P(('dp', 'fsdp'))
- grad_y: bfloat16 [128, 256, 768], P(('dp', 'fsdp'))
- norm_scale: bfloat16 [2, 768], P(None, 'fsdp')
- w_in: bfloat16 [2, 768, 7040], P(None, 'fsdp')
- w_out: bfloat16 [2, 3840, 768], P(None, 'fsdp')
Outputs:
- output 1: bfloat16 [128, 256, 768], P(('dp', 'fsdp'))
- output 2: bfloat16 [128, 256, 768], P(('dp', 'fsdp'))
- output 3: float32 [2, 768], P(None, 'fsdp')
- output 4: float32 [2, 768, 7040], P(None, 'fsdp')
- output 5: float32 [2, 3840, 768], P(None, 'fsdp')
All inputs are finite; a program needn't handle non-finite values.
Results may differ from a plain program's by a relative error of at most 0.0145081.
Values are sent between devices in bfloat16 or wider.
A program may use at most 1 GiB of HBM per device.

v0:
```python
import functools
import jax
import jax.numpy as jnp
from jax import lax
from jax.experimental import pallas as pl
from jax.experimental.pallas import tpu as pltpu
from jax.sharding import PartitionSpec as P

MESH_ID = pl.DeviceIdType.MESH
BOTH = (1, -1)
AROUND = (1, -1, 2)
PARTS = (True, False)


class Links:
    def __init__(self, send_sems, recv_sems):
        self.send_sems, self.recv_sems = send_sems, recv_sems
        self.slots, self.sent = {}, []

    def _slot(self, key):
        return self.slots.setdefault(key, len(self.slots))

    def send(self, key, src, dst, device):
        slot = self._slot(key)
        copy = pltpu.make_async_remote_copy(
            src_ref=src, dst_ref=dst, send_sem=self.send_sems.at[slot], recv_sem=self.recv_sems.at[slot],
            device_id=device, device_id_type=MESH_ID)
        copy.start()
        self.sent.append(copy)

    def arrive(self, key, landed, device):
        slot = self._slot(key)
        pltpu.make_async_remote_copy(
            src_ref=landed, dst_ref=landed, send_sem=self.send_sems.at[slot], recv_sem=self.recv_sems.at[slot],
            device_id=device, device_id_type=MESH_ID).wait_recv()

    def drain(self):
        for copy in self.sent:
            copy.wait_send()


def rem(a, n):
    return a % n if isinstance(a, int) else lax.rem(a, n)


def chip_position():
    f, d = lax.axis_index("fsdp"), lax.axis_index("dp")
    return f // 2, rem(d, 4), d // 4, rem(f, 2)


def device_at(x, y, z, core):
    return (z * 4 + y, x * 2 + core)


def step(coord, by):
    return rem(coord + 4 + by, 4)


def announce(devices):
    barrier = pltpu.get_barrier_semaphore()
    for device in devices:
        pl.semaphore_signal(barrier, inc=1, device_id=device, device_id_type=MESH_ID)
    pl.semaphore_wait(barrier, len(devices))


def plan(tasks, latency=2.5):
    free, landed, order, now = {}, {}, [], 0.0
    left = list(tasks)
    while left:
        best = None
        for place, (name, rank, start, needs, after, sends) in enumerate(left):
            if all(n[0] in landed for n in needs) and all(n in landed for n in after):
                ready = max([start, now] + [landed[task][i] for task, i in needs])
                best = min(best or (ready, rank, place), (ready, rank, place))
        now, _, place = best
        name, _, _, _, _, sends = left.pop(place)
        order.append(name)
        now += 0.2
        landed[name] = []
        for link, cost in sends:
            free[link] = max(now, free.get(link, 0.0)) + cost
            landed[name].append(free[link] + latency)
    return order


def gather_order(rows_i, cols_i, rows_o, cols_o, starts):
    rate = 23300.0
    tasks = []
    for m in range(4):
        is_in = m % 2 == 0
        edge = cols_i // 128 * 4 // 9 // 2 * 256
        size = {"y": rows_i // 4 * edge, "x": rows_i * (cols_i - 2 * edge)} if is_in else {"y": rows_o // 4 * cols_o // 2}
        size["z"] = size["y"]
        for color in "yzx" if is_in else "yz":
            cost = size[color] / rate
            both = [(("x", by), cost) for by in BOTH]
            spread = [((color, by), cost) for by in BOTH] if color != "x" else []
            tasks.append((("reach", m, color), m, starts[m], [], [], both))
            for i, by in enumerate(BOTH):
                tasks.append((("relay", m, color, by), m, 0.0, [(("reach", m, color), i)], [], [(("x", by), cost / 2)] + spread))
            halves = [(("relay", m, color, by), 0) for by in BOTH]
            tasks.append((("far", m, color), m, 0.0, halves, [], spread))
            if color == "x":
                continue
            for off, source, first in ((-1, ("relay", m, color, 1), 1), (1, ("relay", m, color, -1), 1), (2, ("far", m, color), 0)):
                for i, by in enumerate(BOTH):
                    tasks.append((("pass", m, color, off, by), m, 0.0, [(source, first + i)], [], [((color, by), cost / 2)]))
                halves = [(("pass", m, color, off, by), 0) for by in BOTH]
                tasks.append((("close", m, color, off), m, 0.0, halves, [], []))
        for off in (-1, 1, 2):
            last = [("close", m, color, off) for color in "yz"]
            if is_in:
                last.append(("far", m, "x") if off == 2 else ("relay", m, "x", -off))
            tasks.append((("hand", m, off), m, 0.0, [], last, []))
    return plan(tasks)


def gather_kernel(order, sc_in, wi_in, wo_in, sc_out, wi_a, wo_a, wi_b, wo_b, own_i, own_o, ssem, rsem, lsem):
    x, y, z, core = chip_position()
    here = device_at(x, y, z, core)
    twin = device_at(x, y, z, 1 - core)
    rows_i, cols_i = wi_in.shape[1:]
    rows_o, cols_o = wo_in.shape[1:]
    quarter_i, quarter_o = rows_i // 4, rows_o // 4
    third_i = cols_i // 128 * 4 // 9 // 2 * 256
    half_o = cols_o // 2
    cut_o = quarter_o // 16 * 8 + 8 if quarter_o % 16 else quarter_o // 2
    place = {"x": x, "y": y, "z": z}

    def peer(axis, by):
        moved = dict(place)
        moved[axis] = step(place[axis], by)
        return device_at(moved["x"], moved["y"], moved["z"], core)

    peers = [peer(axis, by) for axis in "xyz" for by in BOTH]
    others = [(lax.axis_index("dp"), lax.rem(lax.axis_index("fsdp") + k, 8)) for k in range(1, 8)]
    announce(others + peers[2:])
    links = Links(ssem, rsem)

    mats = []
    for layer, (wi, wo) in enumerate(((wi_a, wo_a), (wi_b, wo_b))):
        mats.append((wi_in.at[layer], wi, own_i.at[layer], True))
        mats.append((wo_in.at[layer], wo, own_o.at[layer], False))

    def region(is_in, color, q):
        if is_in:
            if color == "x":
                lo, hi = 2 * third_i, cols_i
                rows = (0, rows_i)
            else:
                lo, hi = (0, third_i) if color == "y" else (third_i, 2 * third_i)
                rows = (q * quarter_i, quarter_i)
            mid = lo + ((hi - lo) // 128 + 1) // 2 * 128
            return (rows, (lo, hi - lo)), (rows, (lo, mid - lo)), (rows, (mid, hi - mid))
        cols = (0, half_o) if color == "y" else (half_o, half_o)
        start = q * quarter_o
        return ((start, quarter_o), cols), ((start, cut_o), cols), ((start + cut_o, quarter_o - cut_o), cols)

    def at(ref, lead, area):
        (r, nr), (c, nc) = area
        if not isinstance(r, int):
            r = pl.multiple_of(r, 8)
        return ref.at[(*lead, pl.ds(r, nr), pl.ds(c, nc))]

    def colors(m):
        return "yzx" if mats[m][3] else "yz"

    def reach(m, color):
        src, out, _, is_in = mats[m]
        area = region(is_in, color, place[color])[0]
        for by in BOTH:
            links.send((m, "x1", color, by), at(src, (), area), at(out, (x, core), area), peer("x", by))

    def launch(m, color, off):
        _, out, _, is_in = mats[m]
        block = at(out, (step(x, off), core), region(is_in, color, place[color])[0])
        for by in BOTH:
            links.send((m, "p1", color, off, by), block, block, peer(color, by))

    def relay(m, color, by):
        _, out, _, is_in = mats[m]
        xb = step(x, -by)
        areas = region(is_in, color, place[color])
        links.arrive((m, "x1", color, by), at(out, (xb, core), areas[0]), peer("x", -by))
        part = at(out, (xb, core), areas[1] if by == 1 else areas[2])
        links.send((m, "x2", color, by), part, part, peer("x", by))
        if color != "x":
            launch(m, color, -by)

    def far(m, color):
        _, out, _, is_in = mats[m]
        areas = region(is_in, color, place[color])
        for by in BOTH:
            links.arrive((m, "x2", color, by), at(out, (step(x, 2), core), areas[1] if by == 1 else areas[2]), peer("x", -by))
        if color != "x":
            launch(m, color, 2)

    def pass_on(m, color, off, by):
        _, out, _, is_in = mats[m]
        xb = step(x, off)
        areas = region(is_in, color, step(place[color], -by))
        links.arrive((m, "p1", color, off, by), at(out, (xb, core), areas[0]), peer(color, -by))
        part = at(out, (xb, core), areas[1] if by == 1 else areas[2])
        links.send((m, "p2", color, off, by), part, part, peer(color, by))

    def close(m, color, off):
        _, out, _, is_in = mats[m]
        areas = region(is_in, color, step(place[color], 2))
        for by in BOTH:
            links.arrive((m, "p2", color, off, by), at(out, (step(x, off), core), areas[1] if by == 1 else areas[2]), peer(color, -by))

    def hand(m, off):
        _, out, _, _ = mats[m]
        links.send((m, "d2d", off), out.at[step(x, off), core], out.at[step(x, off), core], twin)

    stages = {"reach": reach, "relay": relay, "far": far, "pass": pass_on, "close": close, "hand": hand}

    loads = []
    for m, (src, out, own, _) in enumerate(mats):
        load = pltpu.make_async_copy(src, own, lsem.at[0, m])
        load.start()
        loads.append(load)
    for k, device in enumerate(others):
        links.send(("sc", k), sc_in, sc_out.at[lax.axis_index("fsdp")], device)
    for m, (src, out, own, _) in enumerate(mats):
        links.send((m, "d2d", 0), src, out.at[x, core], twin)
    stores = []
    for m, (src, out, own, _) in enumerate(mats):
        loads[m].wait()
        store = pltpu.make_async_copy(own, out.at[x, core], lsem.at[1, m])
        store.start()
        stores.append(store)
    own_scale = pltpu.make_async_copy(sc_in, sc_out.at[lax.axis_index("fsdp")], lsem.at[2, 0])
    own_scale.start()
    for kind, *task in order:
        stages[kind](*task)
    for m, (src, out, own, _) in enumerate(mats):
        for off in (0, -1, 1, 2):
            xb = step(x, off)
            links.arrive((m, "d2d", off), out.at[xb, 1 - core], twin)
        stores[m].wait()
    own_scale.wait()
    for k in range(7):
        source = lax.rem(lax.axis_index("fsdp") + 7 - k, 8)
        links.arrive(("sc", k), sc_out.at[source], others[k])
    links.drain()


def gather_weights(scale_tile, w_in, w_out, starts=None, n_copies=320):
    any_space = pl.BlockSpec(memory_space=pl.ANY)
    wi = jax.ShapeDtypeStruct((4, 2, *w_in.shape[1:]), w_in.dtype)
    wo = jax.ShapeDtypeStruct((4, 2, *w_out.shape[1:]), w_out.dtype)
    return pl.pallas_call(
        functools.partial(gather_kernel, gather_order(*w_in.shape[1:], *w_out.shape[1:], starts or (0, 0, 0, 0))),
        out_shape=(jax.ShapeDtypeStruct((8, *scale_tile.shape), scale_tile.dtype), wi, wo, wi, wo),
        in_specs=[any_space] * 3,
        out_specs=[any_space] * 5,
        scratch_shapes=[
            pltpu.VMEM(w_in.shape, w_in.dtype),
            pltpu.VMEM(w_out.shape, w_out.dtype),
            pltpu.SemaphoreType.DMA((n_copies,)),
            pltpu.SemaphoreType.DMA((n_copies,)),
            pltpu.SemaphoreType.DMA((3, 4)),
        ],
        compiler_params=pltpu.CompilerParams(collective_id=0, has_side_effects=True, vmem_limit_bytes=12 * 2 ** 20),
        name="gather_weights",
    )(scale_tile, w_in, w_out)


FLOW_AXES = {"x": "yz", "y": "zx", "z": "xy"}
FLOWS = (("x", 1), ("x", -1), ("z", 1), ("z", -1), ("y", 1), ("y", -1))
GROUPS = (("yz", (0, 1, 2)), ("zy", (3, 4, 5)))


def block_of(ref, is_in, color, b, width, base):
    cols = pl.ds(base, width if color == "z" and is_in else width * (4 if is_in else 1))
    if is_in:
        if color == "x":
            return ref.at[b, :, :, cols]
        if color == "y":
            return ref.at[:, b, :, cols]
        return ref.at[:, :, :, pl.ds(pl.multiple_of(base + b * width, 128) if not isinstance(b, int) else base + b * width, width)]
    if color == "x":
        return ref.at[b, :, :, :, cols]
    if color == "y":
        return ref.at[:, b, :, :, cols]
    return ref.at[:, :, b, :, cols]


def second(ref, is_in, color, b, width):
    if is_in:
        if color == "y":
            return ref.at[:, :, pl.ds(pl.multiple_of(b * width, 128) if not isinstance(b, int) else b * width, width)]
        return ref.at[b]
    return ref.at[:, b] if color == "y" else ref.at[b]


def third(ref, is_in, color, b, width):
    if is_in and color == "x":
        return ref.at[:, pl.ds(pl.multiple_of(b * width, 128) if not isinstance(b, int) else b * width, width)]
    return ref.at[b]


def reduce_kernel(widths, order, *refs):
    n = 2
    ga, gb = refs[0:n], refs[n:2 * n]
    oa, ob = refs[2 * n:3 * n], refs[3 * n:4 * n]
    (wx, wy, wz, wb, rx, ry, rz, rb, sx, sy, sz, sb, tx, ty, tz, tb, fa, fb, ssem, rsem, lsem, osem) = refs[4 * n:]
    x, y, z, core = chip_position()
    place = {"x": x, "y": y, "z": z}
    work = {"x": wx, "y": wy, "z": wz}
    ring1 = {"x": rx, "y": ry, "z": rz}
    ring2 = {"x": sx, "y": sy, "z": sz}
    last = {"x": tx, "y": ty, "z": tz}
    bases = [sum(widths[:k]) * 4 for k in range(6)]

    def peer(axis, by):
        moved = dict(place)
        moved[axis] = step(place[axis], by)
        return device_at(moved["x"], moved["y"], moved["z"], core)

    announce([peer(axis, by) for axis in "xyz" for by in AROUND])
    links = Links(ssem, rsem)
    local = {}

    def buf(table, flat, l, k, slot, is_in):
        color, by = FLOWS[k]
        return table[color].at[l, (1 - by) // 2, slot] if is_in else flat.at[l, k, slot]

    def load(l, k, is_in, b, dst, tag):
        color, _ = FLOWS[k]
        src = block_of((ga if is_in else gb)[l], is_in, color, b, widths[k] if is_in else 128, bases[k] if is_in else 128 * k)
        copy = pltpu.make_async_copy(src, dst, lsem.at[l, k, 0 if is_in else 1, tag])
        copy.start()
        local[l, k, is_in, tag] = copy

    def p1(l, k, s, is_in):
        color, by = FLOWS[k]
        a = place[color]
        width = widths[k] if is_in else 128
        base = bases[k] if is_in else 128 * k
        r = [buf(ring1, rb, l, k, i, is_in) for i in range(3)]
        w = [buf(work, wb, l, k, i, is_in) for i in range(2)]
        if s == 0:
            src = block_of((ga if is_in else gb)[l], is_in, color, step(a, -by), width, base)
            links.send((l, k, is_in, "p1", 0), src, r[0], peer(color, by))
            load(l, k, is_in, step(a, -2 * by), w[1], 0)
            load(l, k, is_in, step(a, -3 * by), w[0], 1)
            return
        mine = (None, w[1], w[0], r[0])[s]
        links.arrive((l, k, is_in, "p1", s - 1), r[s - 1], peer(color, -by))
        local[l, k, is_in, s - 1].wait()
        add_into(mine, r[s - 1])
        if s < 3:
            links.send((l, k, is_in, "p1", s), mine, r[s], peer(color, by))
            if s == 1:
                load(l, k, is_in, a, r[0], 2)
        else:
            p2(l, k, 0, is_in)

    def p2(l, k, s, is_in):
        color, by = FLOWS[k]
        axis = FLOW_AXES[color][0]
        a = place[axis]
        width = widths[k] if is_in else 128
        total = buf(ring1, rb, l, k, 0, is_in)
        r = [buf(ring2, sb, l, k, i, is_in) for i in range(3)]
        mine = second(total, is_in, color, step(a, -by * (1 + s)), width)
        if s:
            links.arrive((l, k, is_in, "p2", s - 1), r[s - 1], peer(axis, -by))
            add_into(mine, r[s - 1])
        if s < 3:
            links.send((l, k, is_in, "p2", s), mine, r[s], peer(axis, by))
        else:
            axis = FLOW_AXES[color][1]
            for slot, o in enumerate(AROUND):
                part = third(mine, is_in, color, step(place[axis], o), width)
                links.send((l, k, is_in, "p3", o), part, buf(last, tb, l, k, slot, is_in), peer(axis, o))

    def final(l, k, is_in):
        return (fa.at[l, :, pl.ds(sum(widths[:k]), widths[k])] if is_in else fb.at[l, :, pl.ds(128 * k, 128)])

    def p3(l, k, is_in):
        color, by = FLOWS[k]
        axis2, axis3 = FLOW_AXES[color]
        width = widths[k] if is_in else 128
        t = [buf(last, tb, l, k, i, is_in) for i in range(3)]
        for slot, o in enumerate(AROUND):
            links.arrive((l, k, is_in, "p3", o), t[slot], peer(axis3, -o))
        mine = third(second(buf(ring1, rb, l, k, 0, is_in), is_in, color, place[axis2], width), is_in, color, place[axis3], width)
        final(l, k, is_in)[...] = (mine[...] + t[0][...]) + (t[1][...] + t[2][...])

    def pieces(l, g, p, q):
        _, flows = GROUPS[g]
        out = []
        for k in flows:
            lo = bases[k] + q * widths[k]
            lo = lo if isinstance(lo, int) else pl.multiple_of(lo, 128)
            out.append(oa[l].at[p, :, pl.ds(lo, widths[k])])
        out.append(ob[l].at[p, q, :, pl.ds(128 * flows[0], 128 * len(flows))])
        return out

    def fronts(l, g):
        _, flows = GROUPS[g]
        out = [fa.at[l, :, pl.ds(sum(widths[:k]), widths[k])] for k in flows]
        out.append(fb.at[l, :, pl.ds(128 * flows[0], 128 * len(flows))])
        return out

    def line(l, g, at2, part):
        order2, flows = GROUPS[g]
        along = slice(None) if part is None else pl.ds(2 * part, 2)
        out = []
        for k in flows:
            if order2 == "yz":
                lo = bases[k] + at2 * widths[k]
                lo = lo if isinstance(lo, int) else pl.multiple_of(lo, 128)
                out.append(oa[l].at[along, :, pl.ds(lo, widths[k])])
            else:
                span = 4 * widths[k] if part is None else 2 * widths[k]
                out.append(oa[l].at[at2, :, pl.ds(bases[k] + (part or 0) * 2 * widths[k], span)])
        cols = pl.ds(128 * flows[0], 128 * len(flows))
        out.append(ob[l].at[along, at2, :, cols] if order2 == "yz" else ob[l].at[at2, along, :, cols])
        return out

    def ag(l, g, s, is_in):
        first, then = GROUPS[g][0]
        own = [place[first], place[then]]
        mine = range(3) if is_in else (3,)

        def spot(i, j):
            return pieces(l, g, i, j) if first == "y" else pieces(l, g, j, i)

        forward = (1, 1, -1, -1) if g == 0 else (1, 1, 1, -1)
        if s == 0:
            src, dst = fronts(l, g), spot(own[0], own[1])
            for i in mine:
                for by in BOTH:
                    links.send((l, g, "a1", i, by), src[i], dst[i], peer(first, by))
                copy = pltpu.make_async_copy(src[i], dst[i], osem.at[l, g, i])
                copy.start()
                local[l, g, i] = copy
        elif s == 1:
            for by in BOTH:
                landed = spot(step(own[0], -by), own[1])
                for i in mine:
                    links.arrive((l, g, "a1", i, by), landed[i], peer(first, -by))
                    if forward[i] == by:
                        links.send((l, g, "b1", i), landed[i], landed[i], peer(first, by))
        elif s == 2:
            landed = spot(step(own[0], 2), own[1])
            part = line(l, g, own[1], None)
            for i in mine:
                local[l, g, i].wait()
                links.arrive((l, g, "b1", i), landed[i], peer(first, -forward[i]))
                for by in BOTH:
                    links.send((l, g, "a2", i, by), part[i], part[i], peer(then, by))
        elif s == 3:
            for by in BOTH:
                at2 = step(own[1], -by)
                whole, half = line(l, g, at2, None), line(l, g, at2, (1 - by) // 2)
                for i in mine:
                    links.arrive((l, g, "a2", i, by), whole[i], peer(then, -by))
                    links.send((l, g, "a3", i, by), half[i], half[i], peer(then, by))
        else:
            at2 = step(own[1], 2)
            for by in BOTH:
                half = line(l, g, at2, (1 - by) // 2)
                for i in mine:
                    links.arrive((l, g, "a3", i, by), half[i], peer(then, -by))

    stages = {"p1": p1, "p2": p2, "p3": lambda l, k, s, is_in: p3(l, k, is_in), "ag": ag}

    for kind, *task in order:
        stages[kind](*task)
    links.drain()


def add_into(dst, src):
    lead = dst.shape[:-2]
    if len(lead) == 2:
        @pl.loop(0, lead[0])
        def _(i):
            for j in range(lead[1]):
                dst[i, j] += src[i, j]
    elif len(lead) == 1:
        @pl.loop(0, lead[0])
        def _(i):
            dst[i] += src[i]
    else:
        dst[...] += src[...]


def reduce_order(widths, rows, rows_b, starts):
    rate = 11650.0
    tasks = []
    for l in range(2):
        for is_in in PARTS:
            for k, (color, by) in enumerate(FLOWS):
                axes = color + FLOW_AXES[color]
                full = 16 * (rows * widths[k] if is_in else rows_b * 128) / rate
                chain = [("p1", l, k, s, is_in) for s in range(4)] + [("p2", l, k, s, is_in) for s in (1, 2, 3)] + [("p3", l, k, 0, is_in)]
                sends = [[((axes[0], by), full)]] * 3 + [[((axes[1], by), full / 4)]] * 3
                sends += [[((axes[2], o), full / 16) for o in (1, -1, 1)], []]
                for i, task in enumerate(chain):
                    needs = [(chain[i - 1], j) for j in range(len(sends[i - 1]))] if i else []
                    tasks.append((task, (l, i - 8), starts[is_in][l] if i == 0 else 0.0, needs, [], sends[i]))
            for g, ((first, then), flows) in enumerate(GROUPS):
                piece = sum(rows * widths[k] if is_in else rows_b * 128 for k in flows) / rate
                for s, (axis, n) in enumerate(((first, 1), (first, 0.5), (then, 4), (then, 2), (None, 0))):
                    needs = [(("ag", l, g, s - 1, is_in), j) for j in (0, 1)] if s else []
                    after = [] if s else [("p3", l, k, 0, is_in) for k in flows]
                    sends = [((axis, by), piece * n) for by in BOTH] if axis else []
                    tasks.append((("ag", l, g, s, is_in), (l, s - 5), 0.0, needs, after, sends))
    return plan(tasks)


def reduce_gradients(ga, gb, widths=(384, 384, 256, 256, 256, 256), starts=None):
    any_space = pl.BlockSpec(memory_space=pl.ANY)
    rows = ga[0].shape[2]
    rows_b = gb[0].shape[3]
    cols = 4 * sum(widths)
    f32 = jnp.float32
    wx, wz, wy = widths[0], widths[2], widths[4]

    def buffers(slots, whole):
        a = {"x": (4, rows, 4 * wx), "y": (4, rows, 4 * wy), "z": (4, 4, rows, wz)}
        b = {"x": (rows, 4 * wx), "y": (4, rows, wy), "z": (4, rows, wz)}
        c = {"x": (rows, wx), "y": (rows, wy), "z": (rows, wz)}
        flat = ((4, 4), (4,), ())[whole]
        per = (a, b, c)[whole]
        return [pltpu.VMEM((2, 2, slots, *per[color]), f32) for color in "xyz"] + [
            pltpu.VMEM((2, 6, slots, *flat, rows_b, 128), f32)]

    oa = jax.ShapeDtypeStruct((4, rows, cols), f32)
    ob = jax.ShapeDtypeStruct((4, 4, rows_b, 768), f32)
    outs = pl.pallas_call(
        functools.partial(reduce_kernel, widths, reduce_order(widths, rows, rows_b, starts or {True: (0, 40), False: (0, 60)})),
        out_shape=(oa, oa, ob, ob),
        in_specs=[any_space] * 4,
        out_specs=[any_space] * 4,
        scratch_shapes=[
            *buffers(2, 0), *buffers(3, 0), *buffers(3, 1), *buffers(3, 2),
            pltpu.VMEM((2, rows, sum(widths)), f32), pltpu.VMEM((2, rows_b, 768), f32),
            pltpu.SemaphoreType.DMA((400,)), pltpu.SemaphoreType.DMA((400,)),
            pltpu.SemaphoreType.DMA((2, 6, 2, 3)), pltpu.SemaphoreType.DMA((2, 2, 4)),
        ],
        compiler_params=pltpu.CompilerParams(collective_id=1, has_side_effects=True, vmem_limit_bytes=60 * 2 ** 20),
        name="reduce_gradients",
    )(*ga, *gb)
    return outs[:2], outs[2:]


def rotary_tables(seq_len, head_dim):
    half_dim = head_dim // 2
    inv_freq = 10000.0 ** (-(jnp.arange(half_dim, dtype=jnp.float32) * 2.0 / head_dim))
    angles = jnp.arange(seq_len, dtype=jnp.float32)[:, None] * inv_freq[None, :]
    return jnp.cos(angles), jnp.sin(angles)


def rotate(vectors, cos_tab, sin_tab):
    half_dim = vectors.shape[-1] // 2
    lo_half = vectors[..., :half_dim]
    hi_half = vectors[..., half_dim:]
    return jnp.concatenate([lo_half * cos_tab - hi_half * sin_tab, hi_half * cos_tab + lo_half * sin_tab], axis=-1)


def layer_norm(hidden, gain_vec):
    hid_f32 = hidden.astype(jnp.float32)
    centered = hid_f32 - jnp.mean(hid_f32, axis=-1, keepdims=True)
    variance = jnp.mean(centered * centered, axis=-1, keepdims=True)
    return (centered * lax.rsqrt(variance + 1e-6) * gain_vec).astype(jnp.bfloat16)


def mix_block(projected, model_dim, ff_dim, head_dim):
    n_batch, seq_len, _ = projected.shape
    n_heads = model_dim // head_dim
    kv_end = model_dim + 2 * head_dim
    queries = projected[..., :model_dim].reshape(n_batch, seq_len, n_heads, head_dim).astype(jnp.float32) * head_dim ** -0.5
    key_vec = projected[..., model_dim:model_dim + head_dim].astype(jnp.float32)
    val_vec = projected[..., model_dim + head_dim:kv_end]
    gate_act = projected[..., kv_end:kv_end + ff_dim].astype(jnp.float32)
    up_act = projected[..., kv_end + ff_dim:].astype(jnp.float32)
    cos_tab, sin_tab = rotary_tables(seq_len, head_dim)
    q_rot = rotate(queries, cos_tab[:, None, :], sin_tab[:, None, :]).astype(jnp.bfloat16)
    k_rot = rotate(key_vec, cos_tab, sin_tab).astype(jnp.bfloat16)
    scores = jnp.einsum("crie,cle->cirl", q_rot, k_rot, preferred_element_type=jnp.float32)
    positions = jnp.arange(seq_len)
    scores = jnp.where(positions[:, None] >= positions[None, :], scores, -1e30)
    attn_probs = jax.nn.softmax(scores, axis=-1).astype(jnp.bfloat16)
    attn_out = jnp.einsum("cirl,cle->crie", attn_probs, val_vec, preferred_element_type=jnp.float32)
    attn_out = attn_out.astype(jnp.bfloat16).reshape(n_batch, seq_len, model_dim)
    mlp_out = (jax.nn.silu(gate_act) * up_act).astype(jnp.bfloat16)
    return jnp.concatenate([attn_out, mlp_out], axis=-1)


def solution(mesh):
    fsdp_size = mesh.shape["fsdp"]
    batch_spec = P(("dp", "fsdp"), None, None)
    scale_spec = P(None, "fsdp")
    weight_spec = P(None, "fsdp", None)
    twins = [(f, f ^ 1) for f in range(fsdp_size)]

    def swap(value):
        return lax.ppermute(value, "fsdp", twins)

    def device_step(x_in, grad_y, norm_scale, w_in, w_out):
        n_layers = w_in.shape[0]
        seq_len, model_dim = x_in.shape[1:]
        proj_dim = w_in.shape[2]
        ff_dim = w_out.shape[1] * fsdp_size - model_dim
        head_dim = (proj_dim - model_dim - 2 * ff_dim) // 2
        core = lax.rem(lax.axis_index("fsdp"), 2)
        rows, rows_out = norm_scale.shape[1], w_out.shape[1]
        scale_tile = jnp.pad(norm_scale.astype(jnp.float32), ((0, 8 - n_layers), (0, 128 - rows)))
        scales, *gathered = gather_weights(scale_tile, w_in, w_out)
        scale_full = scales[:, :n_layers, :rows].transpose(1, 0, 2).reshape(n_layers, model_dim)
        w_in_full = [gathered[0].reshape(model_dim, -1), gathered[2].reshape(model_dim, -1)]
        w_out_full = [gathered[1].reshape(-1, model_dim), gathered[3].reshape(-1, model_dim)]
        mix_fn = functools.partial(mix_block, model_dim=model_dim, ff_dim=ff_dim, head_dim=head_dim)

        def split(value, which):
            parts = value.reshape(seq_len, 4, 2, -1)
            return lax.dynamic_index_in_dim(parts, which, 2, keepdims=False)

        saved_acts = []
        hidden = x_in
        for layer_idx in range(n_layers):
            normed = layer_norm(hidden, scale_full[layer_idx])
            projected = jnp.einsum("bsd,de->bse", normed, w_in_full[layer_idx], preferred_element_type=jnp.float32).astype(jnp.bfloat16)
            mixed_out = mix_fn(projected)
            block_out = jnp.einsum("bsf,fd->bsd", mixed_out, w_out_full[layer_idx], preferred_element_type=jnp.float32)
            saved_acts.append((hidden, normed, projected, mixed_out))
            hidden = (hidden.astype(jnp.float32) + block_out).astype(jnp.bfloat16)
        grad_hidden = grad_y
        in_parts = [None] * n_layers
        out_parts = [None] * n_layers
        for layer_idx in reversed(range(n_layers)):
            layer_in, normed, projected, mixed_out = saved_acts[layer_idx]
            grad_mixed = jnp.einsum("bsd,fd->bsf", grad_hidden, w_out_full[layer_idx], preferred_element_type=jnp.float32).astype(jnp.bfloat16)
            grad_proj = jax.vjp(mix_fn, projected)[1](grad_mixed)[0]
            grad_normed = jnp.einsum("bse,de->bsd", grad_proj, w_in_full[layer_idx], preferred_element_type=jnp.float32).astype(jnp.bfloat16)
            grad_in, part_scale = jax.vjp(layer_norm, layer_in, scale_full[layer_idx])[1](grad_normed)

            def pair(value):
                return jnp.concatenate([split(value, core), swap(split(value, 1 - core))], axis=0)

            def both(value):
                return jnp.concatenate([value, swap(value)], axis=0)

            rows_pair = pair(normed[0]).reshape(2 * seq_len, -1)
            cols_pair = jnp.pad(both(grad_proj[0]), ((0, 0), (0, 128)))
            part_in = lax.dot_general(rows_pair, cols_pair, (((0,), (0,)), ((), ())), preferred_element_type=jnp.float32)
            in_parts[layer_idx] = part_in.reshape(4, 4, rows // 4, proj_dim + 128)
            mixed_pair = jnp.pad(pair(mixed_out[0]), ((0, 0), (0, 0), (0, 32))).reshape(2 * seq_len, -1)
            part_out = lax.dot_general(mixed_pair, both(grad_hidden[0]), (((0,), (0,)), ((), ())), preferred_element_type=jnp.float32)
            part_out = part_out.reshape(4, rows_out + 32, model_dim)
            scale_blocks = part_scale.reshape(4, 2, rows)
            scale_pair = lax.dynamic_index_in_dim(scale_blocks, core, 1) + swap(lax.dynamic_index_in_dim(scale_blocks, 1 - core, 1))
            part_out = lax.dynamic_update_slice(part_out, scale_pair, (0, rows_out, 0))
            out_parts[layer_idx] = part_out.reshape(4, 4, 4, (rows_out + 32) // 16, model_dim)
            grad_hidden = (grad_hidden.astype(jnp.float32) + grad_in.astype(jnp.float32)).astype(jnp.bfloat16)
        in_sums, out_sums = reduce_gradients(in_parts[::-1], out_parts[::-1])
        in_grads = jnp.stack([g.reshape(rows, -1)[:, :proj_dim] for g in in_sums[::-1]])
        out_rows = [g.reshape(-1, model_dim) for g in out_sums[::-1]]
        out_grads = jnp.stack([g[:rows_out] for g in out_rows])
        scale_grads = jnp.stack([g[rows_out, :rows] for g in out_rows])
        return hidden, grad_hidden, scale_grads, in_grads, out_grads

    return jax.shard_map(
        device_step,
        mesh=mesh,
        in_specs=(batch_spec, batch_spec, scale_spec, weight_spec, weight_spec),
        out_specs=(batch_spec, batch_spec, scale_spec, weight_spec, weight_spec),
        check_vma=False,
    )
```

profile of v0, /device:TPU:0, one launch (start us, length us, event | category | flops | bytes accessed | tf_op | source)
XLA Modules:
  0.0 476.0 jit_solution(15130154467489851625)
XLA Ops:
  5.1 75.2 %gather_weights.1 = (f32[8,8,128]{2,1,0:T(8,128)S(1)}, bf16[4,2,96,7040]{3,2,1,0:T(8,128)(2,1)S(1)}, bf16[4,2,480,768]{3,2,1,0:T(8,128)(2,1)S(1)}, bf16[4,2,96,7...) custom-call(f32[8,128]{1,0:T(8,128)S(1)} %pad_convert_fusion.sc_in, bf16[2,96,7040]{2,1,0:T(8,128)(2,1)S(1)} %copy-done, ...), custom_call_target="tpu_custom_call" | custom-call | tf_op jit(solution)/shard_map/gather_weights/pallas_call | solution.py:253
  80.3 4.0 copy-done.2
  84.3 4.0 copy-done.3
  88.3 2.5 copy-done.4
  90.9 2.5 copy-done.5
  94.5 7.6 %fusion.4 = bf16[1,256,7040]{2,1,0:T(8,128)(2,1)S(1)} fusion(bf16[768,7040]{1,0:T(8,128)(2,1)} %bitcast.457, bf16[1,256,768]{2,1,0:T(8,128)(2,1)S(1)} %fusion.181), kind=kOutput, calls=%fused_computation.7 | convolution fusion | flops 2770042880 | bytes 14811136 | tf_op jit(solution)/shard_map/bsd,de->bse/dot_general | solution.py:629
  111.1 4.5 fusion.243
  118.8 7.5 %fusion.5 = bf16[1,256,7040]{2,1,0:T(8,128)(2,1)S(1)} fusion(bf16[768,7040]{1,0:T(8,128)(2,1)} %bitcast.459, bf16[1,256,768]{2,1,0:T(8,128)(2,1)S(1)} %multiply_convert_fusion.2), kind=kOutput, calls=%fused_computation.8 | convolution fusion | flops 2770042880 | bytes 14811136 | tf_op jit(solution)/shard_map/bsd,de->bse/dot_general | solution.py:629
  126.4 3.0 fusion.22
  129.5 3.6 fusion.32
  138.2 1.9 copy.48
  140.1 2.1 fusion.40
  147.6 1.9 copy.54
  151.2 4.1 add_bitcast_fusion.1
  155.5 9.0 %fusion.189 = (f32[768]{0:T(1024)}, f32[256]{0:T(256)S(1)}, f32[256,768]{1,0:T(8,128)S(1)}) fusion(f32[1,256,768]{2,1,0:T(8,128)S(1)} %copy-done.13, f32[256]{0:T(256)S(1)} %copy-done.89, f32[256]{0:T(256)S(1)} %copy-done.84, f32[768]{0:T(1024)S(1)} %copy-done.76, bf16[256,7040]{1,0:T(8,128)(2,1)} %add_bitcast_fusion.1, bf16[768,7040]{1,0:T(8,128)(2,1)} %bitcast.460), kind=kOutput, calls=%fused_computation.188 | convolution fusion | flops 2770009088 | bytes 16000000 | tf_op jit(solution)/shard_map/bse,de->bsd/dot_general | solution.py:641
  172.4 3.3 fusion.49
  181.4 3.0 fusion.41
  185.3 1.9 copy.61
  188.9 3.9 add_bitcast_fusion
  196.1 8.2 %fusion.184 = (f32[256]{0:T(256)S(1)}, f32[256,768]{1,0:T(8,128)S(1)}) fusion(bf16[1,256,768]{2,1,0:T(8,128)(2,1)S(1)} %copy-done.10, f32[768]{0:T(1024)} %copy-done.67, f32[256]{0:T(256)} %copy-done.80, bf16[256,7040]{1,0:T(8,128)(2,1)} %add_bitcast_fusion, bf16[768,7040]{1,0:T(8,128)(2,1)} %bitcast.458), kind=kOutput, calls=%fused_computation.180 | convolution fusion | flops 2769616640 | bytes 15602688 | tf_op jit(solution)/shard_map/bse,de->bsd/dot_general | solution.py:641
  209.4 2.5 fusion.118
  215.4 2.3 copy.64
  219.6 5.3 %fusion.112 = bf16[1,256,768]{2,1,0:T(8,128)(2,1)} fusion(f32[1,256,768]{2,1,0:T(8,128)S(1)} %copy-done.14, bf16[3840,768]{1,0:T(8,128)(2,1)} %bitcast.461, bf16[1,256,3072]{2,1,0:T(8,128)(2,1)S(1)} %copy-done.15, bf16[1,256,768]{2,1,0:T(8,128)(2,1)S(1)} %copy-done.35), kind=kOutput, calls=%fused_computation.136 | convolution fusion | flops 1514274816 | bytes 9043968 | tf_op jit(solution)/shard_map/bsf,fd->bsd/dot_general | solution.py:631
  230.2 2.1 add_convert_fusion
  232.3 2.3 copy.65
  240.4 5.7 %fusion.66 = f32[4,512,768]{2,1,0:T(8,128)} fusion(bf16[256,4,480]{0,2,1:T(8,128)(2,1)} %collective-permute-done.4, bf16[256,4,480]{0,2,1:T(8,128)(2,1)S(1)} %copy-done.36, bf16[256,768]{1,0:T(8,128)(2,1)S(1)} %collective-permute-done.5, bf16[256,768]{1,0:T(8,128)(2,1)} %bitcast.41), kind=kOutput, calls=%fused_computation.98 | convolution fusion | flops 1619525632 | bytes 9043968 | tf_op jit(solution)/shard_map/dot_general | solution.py:655
  247.8 5.7 %fusion.71 = f32[4,512,768]{2,1,0:T(8,128)} fusion(bf16[256,4,480]{0,2,1:T(8,128)(2,1)} %collective-permute-done.7, bf16[256,4,480]{0,2,1:T(8,128)(2,1)S(1)} %get-tuple-element.36, bf16[256,768]{1,0:T(8,128)(2,1)} %collective-permute-done.8, bf16[256,768]{1,0:T(8,128)(2,1)S(1)} %bitcast.482), kind=kOutput, calls=%fused_computation.101 | convolution fusion | flops 1619525632 | bytes 9043968 | tf_op jit(solution)/shard_map/dot_general | solution.py:655
  254.9 7.8 %fusion.8.refs_0_ = f32[4,4,24,7168]{3,2,1,0:T(8,128)} fusion(bf16[4,4,24,512]{3,2,1,0:T(8,128)(2,1)S(1)} %bitcast.489, bf16[256,7040]{1,0:T(8,128)(2,1)} %collective-permute-done.1, bf16[256,7040]{1,0:T(8,128)(2,1)} %add_bitcast_fusion.1), kind=kOutput, calls=%fused_computation.11 | convolution fusion | flops 2844262400 | bytes 18612224 | tf_op jit(solution)/shard_map/dot_general | solution.py:652
  262.7 7.9 %fusion.13.refs_1_ = f32[4,4,24,7168]{3,2,1,0:T(8,128)} fusion(bf16[4,4,24,512]{3,2,1,0:T(8,128)(2,1)S(1)} %bitcast.490, bf16[256,7040]{1,0:T(8,128)(2,1)} %collective-permute-done.3, bf16[256,7040]{1,0:T(8,128)(2,1)} %add_bitcast_fusion), kind=kOutput, calls=%fused_computation.14 | convolution fusion | flops 2844262400 | bytes 18612224 | tf_op jit(solution)/shard_map/dot_general | solution.py:652
  270.6 195.4 %reduce_gradients.1 = (f32[4,24,7168]{2,1,0:T(8,128)}, f32[4,24,7168]{2,1,0:T(8,128)}, f32[4,4,32,768]{3,2,1,0:T(8,128)}, f32[4,4,32,768]{3,2,1,0:T(8,128)}) custom-call(f32[4,4,24,7168]{3,2,1,0:T(8,128)} %fusion.8.refs_0_, f32[4,4,24,7168]{3,2,1,0:T(8,128)} %fusion.13.refs_1_, f32[4,4,4,32,768]{4,3,2,1,0:T(8,128)} %bitcast.472, f32[4,4,4,32,768]{4,3,2,1,0:T(8,128)} %bitcast.471), custom_call_target="tpu_custom_call" | custom-call | tf_op jit(solution)/shard_map/reduce_gradients/pallas_call | solution.py:536
  468.0 2.0 slice_bitcast_fusion.2
  471.0 2.8 pad_maximum_fusion
  (305 shorter events, 78.2 us)
Async XLA Ops:
  5.1 88.4 %copy-start.10 = (bf16[1,256,768]{2,1,0:T(8,128)(2,1)S(1)}, bf16[1,256,768]{2,1,0:T(8,128)(2,1)}, u32[]{:S(2)}) copy-start(bf16[1,256,768]{2,1,0:T(8,128)(2,1)} %param.5) | copy-start | bytes 1179652
  94.2 7.9 %copy-start.28 = (bf16[1,256,768]{2,1,0:T(8,128)(2,1)}, bf16[1,256,768]{2,1,0:T(8,128)(2,1)S(1)}, u32[]{:S(2)}) copy-start(bf16[1,256,768]{2,1,0:T(8,128)(2,1)S(1)} %fusion.181) | copy-start | bytes 1179652
  103.0 8.0 %copy-start.16 = (bf16[1,256,3072]{2,1,0:T(8,128)(2,1)}, bf16[1,256,3072]{2,1,0:T(8,128)(2,1)S(1)}, u32[]{:S(2)}) copy-start(bf16[1,256,3072]{2,1,0:T(8,128)(2,1)S(1)} %fusion.30) | copy-start | bytes 4718596
  103.9 30.3 %copy-start.87 = (f32[32]{0:T(128)}, f32[32]{0:T(128)S(1)}, u32[]{:S(2)}) copy-start(f32[32]{0:T(128)S(1)} %negate_power_fusion) | copy-start | bytes 388
  116.5 9.7 %copy-start.88 = (f32[256]{0:T(256)}, f32[256]{0:T(256)S(1)}, u32[]{:S(2)}) copy-start(f32[256]{0:T(256)S(1)} %fusion.212) | copy-start | bytes 3076
  116.7 9.7 %slice-start = ((s8[5898240]{0:T(1024)(128)(4,1)}), s8[1703936]{0:T(1024)(128)(4,1)S(1)}, s32[]{:S(2)}) async-start(s8[5898240]{0:T(1024)(128)(4,1)} %bitcast.462), calls=%async_computation | async-start | bytes 3407872
  117.7 118.6 %collective-permute-start = (bf16[256,4,96]{0,2,1:T(8,128)(2,1)}, bf16[256,4,96]{0,2,1:T(8,128)(2,1)}, u32[]{:S(2)}, u32[]{:S(2)}) collective-permute-start(bf16[256,4,96]{0,2,1:T(8,128)(2,1)} %get-tuple-element.51), channel_id=1, source_target_pairs={{0,1},{1,0},{2,3},{3,2},{4,5},{5,4},{6,7},{7,6},{8,9},{9,8},{10,11... | collective-permute-start | bytes 589832 | tf_op jit(solution)/shard_map/ppermute | solution.py:604
  118.8 7.6 %slice-start.1 = ((s8[5898240]{0:T(1024)(128)(4,1)}), s8[4194304]{0:T(1024)(128)(4,1)S(1)}, s32[]{:S(2)}) async-start(s8[5898240]{0:T(1024)(128)(4,1)} %bitcast.462), calls=%async_computation.1 | async-start | bytes 8388608
  151.2 15.5 %slice-start.2 = ((s8[5898240]{0:T(1024)(128)(4,1)}), s8[4194304]{0:T(1024)(128)(4,1)S(1)}, s32[]{:S(2)}) async-start(s8[5898240]{0:T(1024)(128)(4,1)} %bitcast.466), calls=%async_computation.2 | async-start | bytes 8388608
  155.3 9.2 %copy-start.73 = (f32[12,256]{1,0:T(8,128)S(1)}, f32[12,256]{1,0:T(8,128)}, u32[]{:S(2)}) copy-start(f32[12,256]{1,0:T(8,128)} %copy-done.72) | copy-start | bytes 36868
  155.3 9.8 %copy-start.93 = (f32[256]{0:T(256)S(1)}, f32[256]{0:T(256)}, u32[]{:S(2)}) copy-start(f32[256]{0:T(256)} %copy-done.92) | copy-start | bytes 3076
  155.3 11.3 %slice-start.3 = ((s8[5898240]{0:T(1024)(128)(4,1)}), s8[1703936]{0:T(1024)(128)(4,1)S(1)}, s32[]{:S(2)}) async-start(s8[5898240]{0:T(1024)(128)(4,1)} %bitcast.466), calls=%async_computation.3 | async-start | bytes 3407872
  155.3 99.6 %collective-permute-start.1 = (bf16[256,7040]{1,0:T(8,128)(2,1)}, bf16[256,7040]{1,0:T(8,128)(2,1)}, u32[]{:S(2)}, u32[]{:S(2)}) collective-permute-start(bf16[256,7040]{1,0:T(8,128)(2,1)} %add_bitcast_fusion.1), channel_id=1, source_target_pairs={{0,1},{1,0},{2,3},{3,2},{4,5},{5,4},{6,7},{7,6},{8,9},{9,8},{10,11... | collective-permute-start | bytes 10813448 | tf_op jit(solution)/shard_map/ppermute | solution.py:604
  192.7 70.0 %collective-permute-start.3 = (bf16[256,7040]{1,0:T(8,128)(2,1)}, bf16[256,7040]{1,0:T(8,128)(2,1)}, u32[]{:S(2)}, u32[]{:S(2)}) collective-permute-start(bf16[256,7040]{1,0:T(8,128)(2,1)} %add_bitcast_fusion), channel_id=1, source_target_pairs={{0,1},{1,0},{2,3},{3,2},{4,5},{5,4},{6,7},{7,6},{8,9},{9,8},{10,11... | collective-permute-start | bytes 10813448 | tf_op jit(solution)/shard_map/ppermute | solution.py:604
  195.7 8.7 %copy-start.91 = (f32[256]{0:T(256)S(1)}, f32[256]{0:T(256)}, u32[]{:S(2)}) copy-start(f32[256]{0:T(256)} %copy-done.90) | copy-start | bytes 3076
  195.7 9.6 %copy-start.68 = (f32[768]{0:T(1024)S(1)}, f32[768]{0:T(1024)}, u32[]{:S(2)}) copy-start(f32[768]{0:T(1024)} %copy-done.67) | copy-start | bytes 9220
  195.7 9.6 %copy-start.78 = (f32[256]{0:T(256)S(1)}, f32[256]{0:T(256)}, u32[]{:S(2)}) copy-start(f32[256]{0:T(256)} %copy-done.77) | copy-start | bytes 3076
  195.7 9.6 %copy-start.81 = (f32[256]{0:T(256)S(1)}, f32[256]{0:T(256)}, u32[]{:S(2)}) copy-start(f32[256]{0:T(256)} %copy-done.80) | copy-start | bytes 3076
  195.7 34.0 %collective-permute-start.6 = (f32[4,1,96]{2,1,0:T(1,128)}, f32[4,1,96]{2,1,0:T(1,128)}, u32[]{:S(2)}, u32[]{:S(2)}) collective-permute-start(f32[4,1,96]{2,1,0:T(1,128)} %constant_dynamic-slice_fusion.2), channel_id=1, source_target_pairs={{0,1},{1,0},{2,3},{3,2},{4,5},{5,4},{6,7},{7,6},{8,9},{9,8},{10,11... | collective-permute-start | bytes 4616 | tf_op jit(solution)/shard_map/ppermute | solution.py:604
  209.0 20.8 %collective-permute-start.9 = (f32[4,1,96]{2,1,0:T(1,128)}, f32[4,1,96]{2,1,0:T(1,128)}, u32[]{:S(2)}, u32[]{:S(2)}) collective-permute-start(f32[4,1,96]{2,1,0:T(1,128)} %constant_dynamic-slice_fusion), channel_id=1, source_target_pairs={{0,1},{1,0},{2,3},{3,2},{4,5},{5,4},{6,7},{7,6},{8,9},{9,8},{10,11... | collective-permute-start | bytes 4616 | tf_op jit(solution)/shard_map/ppermute | solution.py:604
  219.6 5.3 %copy-start.11 = (bf16[1,256,3840]{1,2,0:T(8,128)(2,1)S(1)}, bf16[1,256,3840]{1,2,0:T(8,128)(2,1)}, u32[]{:S(2)}) copy-start(bf16[1,256,3840]{1,2,0:T(8,128)(2,1)} %copy.64) | copy-start | bytes 5898244
  224.9 5.3 %copy-start.19 = (f32[256,768]{1,0:T(8,128)S(1)}, f32[256,768]{1,0:T(8,128)}, u32[]{:S(2)}) copy-start(f32[256,768]{1,0:T(8,128)} %copy-done.18) | copy-start | bytes 2359300
  224.9 5.3 %copy-start.69 = (f32[768]{0:T(1024)S(1)}, f32[768]{0:T(1024)}, u32[]{:S(2)}) copy-start(f32[768]{0:T(1024)} %copy-done.67) | copy-start | bytes 9220
  224.9 5.3 %copy-start.79 = (f32[256]{0:T(256)S(1)}, f32[256]{0:T(256)}, u32[]{:S(2)}) copy-start(f32[256]{0:T(256)} %copy-done.77) | copy-start | bytes 3076
  229.7 6.8 %collective-permute-start.2 = (bf16[256,4,96]{0,2,1:T(8,128)(2,1)}, bf16[256,4,96]{0,2,1:T(8,128)(2,1)S(1)}, u32[]{:S(2)}, u32[]{:S(2)}) collective-permute-start(bf16[256,4,96]{0,2,1:T(8,128)(2,1)} %get-tuple-element.49), channel_id=1, source_target_pairs={{0,1},{1,0},{2,3},{3,2},{4,5},{5,4},{6,7},{7,6},{8,9},{9,8},{10,11... | collective-permute-start | bytes 589832 | tf_op jit(solution)/shard_map/ppermute | solution.py:604
  229.8 10.6 %collective-permute-start.4 = (bf16[256,4,480]{0,2,1:T(8,128)(2,1)}, bf16[256,4,480]{0,2,1:T(8,128)(2,1)}, u32[]{:S(2)}, u32[]{:S(2)}) collective-permute-start(bf16[256,4,480]{0,2,1:T(8,128)(2,1)} %get-tuple-element.39), channel_id=1, source_target_pairs={{0,1},{1,0},{2,3},{3,2},{4,5},{5,4},{6,7},{7,6},{8,9},{9,8},{10,11... | collective-permute-start | bytes 2949128 | tf_op jit(solution)/shard_map/ppermute | solution.py:604
  232.3 5.3 %copy-start.86 = (f32[4,2,96]{2,1,0:T(2,128)S(1)}, f32[4,2,96]{2,1,0:T(2,128)}, u32[]{:S(2)}) copy-start(f32[4,2,96]{2,1,0:T(2,128)} %reshape.635) | copy-start | bytes 9220
  232.3 6.0 %copy-start.53 = (bf16[256,4,1,96]{0,3,2,1:T(8,128)(2,1)S(1)}, bf16[256,4,1,96]{0,3,2,1:T(8,128)(2,1)}, u32[]{:S(2)}) copy-start(bf16[256,4,1,96]{0,3,2,1:T(8,128)(2,1)} %get-tuple-element.50) | copy-start | bytes 589828
  234.5 5.9 %copy-start.36 = (bf16[256,4,480]{0,2,1:T(8,128)(2,1)S(1)}, bf16[256,4,480]{0,2,1:T(8,128)(2,1)}, u32[]{:S(2)}) copy-start(bf16[256,4,480]{0,2,1:T(8,128)(2,1)} %get-tuple-element.38) | copy-start | bytes 2949124
  236.3 3.0 collective-permute-start.5
  236.5 11.3 %collective-permute-start.7 = (bf16[256,4,480]{0,2,1:T(8,128)(2,1)S(1)}, bf16[256,4,480]{0,2,1:T(8,128)(2,1)}, u32[]{:S(2)}, u32[]{:S(2)}) collective-permute-start(bf16[256,4,480]{0,2,1:T(8,128)(2,1)S(1)} %get-tuple-element.37), channel_id=1, source_target_pairs={{0,1},{1,0},{2,3},{3,2},{4,5},{5,4},{6,7},{7,6},{8,9},{9,8},{10,11... | collective-permute-start | bytes 2949128 | tf_op jit(solution)/shard_map/ppermute | solution.py:604
  239.3 8.6 %collective-permute-start.8 = (bf16[256,768]{1,0:T(8,128)(2,1)S(1)}, bf16[256,768]{1,0:T(8,128)(2,1)}, u32[]{:S(2)}, u32[]{:S(2)}) collective-permute-start(bf16[256,768]{1,0:T(8,128)(2,1)S(1)} %bitcast.481), channel_id=1, source_target_pairs={{0,1},{1,0},{2,3},{3,2},{4,5},{5,4},{6,7},{7,6},{8,9},{9,8},{10,11... | collective-permute-start | bytes 1179656 | tf_op jit(solution)/shard_map/ppermute | solution.py:604
  (78 other events, 197.7 us)
where the time goes:
time: 486 us; the launch traced here: 476 us
  Pallas kernels  271 us (56%)
  matrix products  95.3 us (20%)
  local copies, waits for them, and re-layouts  58.4 us (12%)
  other arithmetic  45.5 us (9%)
    pallas_call x1, Pallas kernels, reduce_gradients(): pl.pallas_call(functools.partial(reduce_kernel, widths, reduce_order(widt...  195 us
    pallas_call x1, Pallas kernels, gather_weights(): pl.pallas_call(functools.partial(gather_kernel, gather_order(*w_in.shape[...  75.2 us
    unnamed x200, local copies, waits for them, and re-layouts  23.3 us
    dot_general x2, matrix products, device_step(): jnp.einsum('bse,de->bsd', grad_proj, w_in_full[layer_idx], preferred_elem...  17.2 us
    dot_general x2, matrix products, device_step(): lax.dot_general(rows_pair, cols_pair, (((0,), (0,)), ((), ())), preferred...  15.7 us
    dot_general x2, matrix products, device_step(): jnp.einsum('bsd,de->bse', normed, w_in_full[layer_idx], preferred_element...  15.1 us
    dot_general x6, matrix products, mix_block(): jnp.einsum('cirl,cle->crie', attn_probs, val_vec, preferred_element_type=...  12.4 us
    dot_general x2, matrix products, device_step(): lax.dot_general(mixed_pair, both(grad_hidden[0]), (((0,), (0,)), ((), ())...  11.4 us
  transfers between devices with their start and end apart: 10, of which 0 were waited for; matrix products, arithmetic and copies ran while one was open for 28% of the time, Pallas kernels for 0%

commit v1 on v0

v1 whole, which is shorter than its diff:
```python
import functools
import jax
import jax.numpy as jnp
from jax import lax
from jax.experimental import pallas as pl
from jax.experimental.pallas import tpu as pltpu
from jax.sharding import PartitionSpec as P

MESH_ID = pl.DeviceIdType.MESH
BOTH = (1, -1)
AROUND = (1, -1, 2)
PARTS = (True, False)
ALL = ...
LANE, WIDE, STRIP, HEAD = 128, 256, 512, 64
ROW, BAND, SIDE, PAIR = 8, 32, 4, 2


class Links:
    def __init__(self, send_sems, recv_sems):
        self.send_sems, self.recv_sems = send_sems, recv_sems
        self.slots, self.sent = {}, []

    def _slot(self, key):
        return self.slots.setdefault(key, len(self.slots))

    def send(self, key, src, dst, device):
        slot = self._slot(key)
        copy = pltpu.make_async_remote_copy(
            src_ref=src, dst_ref=dst, send_sem=self.send_sems.at[slot], recv_sem=self.recv_sems.at[slot],
            device_id=device, device_id_type=MESH_ID)
        copy.start()
        self.sent.append(copy)

    def arrive(self, key, landed, device):
        slot = self._slot(key)
        pltpu.make_async_remote_copy(
            src_ref=landed, dst_ref=landed, send_sem=self.send_sems.at[slot], recv_sem=self.recv_sems.at[slot],
            device_id=device, device_id_type=MESH_ID).wait_recv()

    def drain(self):
        for copy in self.sent:
            copy.wait_send()
        self.sent.clear()


def rem(a, n):
    return a % n if isinstance(a, int) else lax.rem(a, n)


def chip_position():
    f, d = lax.axis_index("fsdp"), lax.axis_index("dp")
    return f // PAIR, rem(d, SIDE), d // SIDE, rem(f, PAIR)


def device_at(x, y, z, core):
    return (z * SIDE + y, x * PAIR + core)


def step(coord, by):
    return rem(coord + SIDE + by, SIDE)


def announce(devices):
    barrier = pltpu.get_barrier_semaphore()
    for device in devices:
        pl.semaphore_signal(barrier, inc=1, device_id=device, device_id_type=MESH_ID)
    pl.semaphore_wait(barrier, len(devices))


def plan(tasks, latency=2.5):
    free, landed, order, now = {}, {}, [], 0.0
    left = list(tasks)
    while left:
        best = None
        for place, (name, rank, start, needs, after, sends) in enumerate(left):
            if all(n[0] in landed for n in needs) and all(n in landed for n in after):
                ready = max([start, now] + [landed[task][i] for task, i in needs])
                best = min(best or (ready, rank, place), (ready, rank, place))
        now, _, place = best
        name, _, _, _, _, sends = left.pop(place)
        order.append(name)
        now += 0.2
        landed[name] = []
        for link, cost in sends:
            free[link] = max(now, free.get(link, 0.0)) + cost
            landed[name].append(free[link] + latency)
    return order


def gather_order(rows_i, cols_i, rows_o, cols_o, starts):
    rate = 23300.0
    tasks = []
    for m in range(SIDE):
        is_in = m % PAIR == 0
        edge = cols_i // LANE * SIDE // 9 // PAIR * WIDE
        size = {"y": rows_i // SIDE * edge, "x": rows_i * (cols_i - PAIR * edge)} if is_in else {"y": rows_o // SIDE * cols_o // PAIR}
        size["z"] = size["y"]
        for color in "yzx" if is_in else "yz":
            cost = size[color] / rate
            both = [(("x", by), cost) for by in BOTH]
            spread = [((color, by), cost) for by in BOTH] if color != "x" else []
            tasks.append((("reach", m, color), m, starts[m], [], [], both))
            for i, by in enumerate(BOTH):
                tasks.append((("relay", m, color, by), m, 0.0, [(("reach", m, color), i)], [], [(("x", by), cost / PAIR)] + spread))
            halves = [(("relay", m, color, by), 0) for by in BOTH]
            tasks.append((("far", m, color), m, 0.0, halves, [], spread))
            if color == "x":
                continue
            for off, source, first in ((-1, ("relay", m, color, 1), 1), (1, ("relay", m, color, -1), 1), (PAIR, ("far", m, color), 0)):
                for i, by in enumerate(BOTH):
                    tasks.append((("pass", m, color, off, by), m, 0.0, [(source, first + i)], [], [((color, by), cost / PAIR)]))
                halves = [(("pass", m, color, off, by), 0) for by in BOTH]
                tasks.append((("close", m, color, off), m, 0.0, halves, [], []))
        for off in (-1, 1, PAIR):
            last = [("close", m, color, off) for color in "yz"]
            if is_in:
                last.append(("far", m, "x") if off == PAIR else ("relay", m, "x", -off))
            tasks.append((("hand", m, off), m, 0.0, [], last, []))
    return plan(tasks)


def gather_kernel(order, sc_in, wi_in, wo_in, sc_out, wi_a, wo_a, wi_b, wo_b, own_i, own_o, ssem, rsem, lsem):
    x, y, z, core = chip_position()
    here = device_at(x, y, z, core)
    twin = device_at(x, y, z, 1 - core)
    rows_i, cols_i = wi_in.shape[1:]
    rows_o, cols_o = wo_in.shape[1:]
    quarter_i, quarter_o = rows_i // SIDE, rows_o // SIDE
    third_i = cols_i // LANE * SIDE // 9 // PAIR * WIDE
    half_o = cols_o // PAIR
    cut_o = quarter_o // 16 * ROW + ROW if quarter_o % 16 else quarter_o // PAIR
    place = {"x": x, "y": y, "z": z}

    def peer(axis, by):
        moved = dict(place)
        moved[axis] = step(place[axis], by)
        return device_at(moved["x"], moved["y"], moved["z"], core)

    peers = [peer(axis, by) for axis in "xyz" for by in BOTH]
    others = [(lax.axis_index("dp"), lax.rem(lax.axis_index("fsdp") + k, ROW)) for k in range(1, ROW)]
    announce(others + peers[PAIR:])
    links = Links(ssem, rsem)

    mats = []
    for layer, (wi, wo) in enumerate(((wi_a, wo_a), (wi_b, wo_b))):
        mats.append((wi_in.at[layer], wi, own_i.at[layer], True))
        mats.append((wo_in.at[layer], wo, own_o.at[layer], False))

    def region(is_in, color, q):
        if is_in:
            if color == "x":
                lo, hi = PAIR * third_i, cols_i
                rows = (0, rows_i)
            else:
                lo, hi = (0, third_i) if color == "y" else (third_i, PAIR * third_i)
                rows = (q * quarter_i, quarter_i)
            mid = lo + ((hi - lo) // LANE + 1) // PAIR * LANE
            return (rows, (lo, hi - lo)), (rows, (lo, mid - lo)), (rows, (mid, hi - mid))
        cols = (0, half_o) if color == "y" else (half_o, half_o)
        start = q * quarter_o
        return ((start, quarter_o), cols), ((start, cut_o), cols), ((start + cut_o, quarter_o - cut_o), cols)

    def at(ref, lead, area):
        (r, nr), (c, nc) = area
        if not isinstance(r, int):
            r = pl.multiple_of(r, ROW)
        return ref.at[(*lead, pl.ds(r, nr), pl.ds(c, nc))]

    def colors(m):
        return "yzx" if mats[m][3] else "yz"

    def reach(m, color):
        src, out, _, is_in = mats[m]
        area = region(is_in, color, place[color])[0]
        for by in BOTH:
            links.send((m, "x1", color, by), at(src, (), area), at(out, (x, core), area), peer("x", by))

    def launch(m, color, off):
        _, out, _, is_in = mats[m]
        block = at(out, (step(x, off), core), region(is_in, color, place[color])[0])
        for by in BOTH:
            links.send((m, "p1", color, off, by), block, block, peer(color, by))

    def relay(m, color, by):
        _, out, _, is_in = mats[m]
        xb = step(x, -by)
        areas = region(is_in, color, place[color])
        links.arrive((m, "x1", color, by), at(out, (xb, core), areas[0]), peer("x", -by))
        part = at(out, (xb, core), areas[1] if by == 1 else areas[PAIR])
        links.send((m, "x2", color, by), part, part, peer("x", by))
        if color != "x":
            launch(m, color, -by)

    def far(m, color):
        _, out, _, is_in = mats[m]
        areas = region(is_in, color, place[color])
        for by in BOTH:
            links.arrive((m, "x2", color, by), at(out, (step(x, PAIR), core), areas[1] if by == 1 else areas[PAIR]), peer("x", -by))
        if color != "x":
            launch(m, color, PAIR)

    def pass_on(m, color, off, by):
        _, out, _, is_in = mats[m]
        xb = step(x, off)
        areas = region(is_in, color, step(place[color], -by))
        links.arrive((m, "p1", color, off, by), at(out, (xb, core), areas[0]), peer(color, -by))
        part = at(out, (xb, core), areas[1] if by == 1 else areas[PAIR])
        links.send((m, "p2", color, off, by), part, part, peer(color, by))

    def close(m, color, off):
        _, out, _, is_in = mats[m]
        areas = region(is_in, color, step(place[color], PAIR))
        for by in BOTH:
            links.arrive((m, "p2", color, off, by), at(out, (step(x, off), core), areas[1] if by == 1 else areas[PAIR]), peer(color, -by))

    def hand(m, off):
        _, out, _, _ = mats[m]
        links.send((m, "d2d", off), out.at[step(x, off), core], out.at[step(x, off), core], twin)

    stages = {"reach": reach, "relay": relay, "far": far, "pass": pass_on, "close": close, "hand": hand}

    loads = []
    for m, (src, out, own, _) in enumerate(mats):
        load = pltpu.make_async_copy(src, own, lsem.at[0, m])
        load.start()
        loads.append(load)
    for k, device in enumerate(others):
        links.send(("sc", k), sc_in, sc_out.at[lax.axis_index("fsdp")], device)
    for m, (src, out, own, _) in enumerate(mats):
        links.send((m, "d2d", 0), src, out.at[x, core], twin)
    stores = []
    for m, (src, out, own, _) in enumerate(mats):
        loads[m].wait()
        store = pltpu.make_async_copy(own, out.at[x, core], lsem.at[1, m])
        store.start()
        stores.append(store)
    own_scale = pltpu.make_async_copy(sc_in, sc_out.at[lax.axis_index("fsdp")], lsem.at[PAIR, 0])
    own_scale.start()
    for kind, *task in order:
        stages[kind](*task)
    for m, (src, out, own, _) in enumerate(mats):
        for off in (0, -1, 1, PAIR):
            xb = step(x, off)
            links.arrive((m, "d2d", off), out.at[xb, 1 - core], twin)
        stores[m].wait()
    own_scale.wait()
    for k in range(7):
        source = lax.rem(lax.axis_index("fsdp") + 7 - k, ROW)
        links.arrive(("sc", k), sc_out.at[source], others[k])
    links.drain()


def gather_weights(scale_tile, w_in, w_out, starts=None, n_copies=320):
    any_space = pl.BlockSpec(memory_space=pl.ANY)
    wi = jax.ShapeDtypeStruct((SIDE, PAIR, *w_in.shape[1:]), w_in.dtype)
    wo = jax.ShapeDtypeStruct((SIDE, PAIR, *w_out.shape[1:]), w_out.dtype)
    return pl.pallas_call(
        functools.partial(gather_kernel, gather_order(*w_in.shape[1:], *w_out.shape[1:], starts or (0, 0, 0, 0))),
        out_shape=(jax.ShapeDtypeStruct((ROW, *scale_tile.shape), scale_tile.dtype), wi, wo, wi, wo),
        in_specs=[any_space] * 3,
        out_specs=[any_space] * 5,
        scratch_shapes=[
            pltpu.VMEM(w_in.shape, w_in.dtype),
            pltpu.VMEM(w_out.shape, w_out.dtype),
            pltpu.SemaphoreType.DMA((n_copies,)),
            pltpu.SemaphoreType.DMA((n_copies,)),
            pltpu.SemaphoreType.DMA((3, SIDE)),
        ],
        compiler_params=pltpu.CompilerParams(collective_id=0, has_side_effects=True, vmem_limit_bytes=12 << 20),
        name="gather_weights",
    )(scale_tile, w_in, w_out)


FLOW_AXES = {"x": "yz", "y": "zx", "z": "xy"}
FLOWS = (("x", 1), ("x", -1), ("z", 1), ("z", -1), ("y", 1), ("y", -1))
GROUPS = (("yz", (0, 1, PAIR)), ("zy", (3, SIDE, 5)))


def block_of(ref, is_in, color, b, width, base):
    cols = pl.ds(base, width if color == "z" and is_in else width * (SIDE if is_in else 1))
    if is_in:
        if color == "x":
            return ref.at[b, :, :, cols]
        if color == "y":
            return ref.at[:, b, :, cols]
        return ref.at[:, :, :, pl.ds(pl.multiple_of(base + b * width, LANE) if not isinstance(b, int) else base + b * width, width)]
    if color == "x":
        return ref.at[b, :, :, :, cols]
    if color == "y":
        return ref.at[:, b, :, :, cols]
    return ref.at[:, :, b, :, cols]


def second(ref, is_in, color, b, width):
    if is_in:
        if color == "y":
            return ref.at[:, :, pl.ds(pl.multiple_of(b * width, LANE) if not isinstance(b, int) else b * width, width)]
        return ref.at[b]
    return ref.at[:, b] if color == "y" else ref.at[b]


def third(ref, is_in, color, b, width):
    if is_in and color == "x":
        return ref.at[:, pl.ds(pl.multiple_of(b * width, LANE) if not isinstance(b, int) else b * width, width)]
    return ref.at[b]


def reduce_kernel(widths, order, *refs):
    n = PAIR
    ga, gb = refs[0:n], refs[n:PAIR * n]
    oa, ob = refs[PAIR * n:3 * n], refs[3 * n:SIDE * n]
    (wx, wy, wz, wb, rx, ry, rz, rb, sx, sy, sz, sb, tx, ty, tz, tb, fa, fb, ssem, rsem, lsem, osem) = refs[SIDE * n:]
    x, y, z, core = chip_position()
    place = {"x": x, "y": y, "z": z}
    work = {"x": wx, "y": wy, "z": wz}
    ring1 = {"x": rx, "y": ry, "z": rz}
    ring2 = {"x": sx, "y": sy, "z": sz}
    last = {"x": tx, "y": ty, "z": tz}
    bases = [sum(widths[:k]) * SIDE for k in range(6)]

    def peer(axis, by):
        moved = dict(place)
        moved[axis] = step(place[axis], by)
        return device_at(moved["x"], moved["y"], moved["z"], core)

    announce([peer(axis, by) for axis in "xyz" for by in AROUND])
    links = Links(ssem, rsem)
    local = {}

    def buf(table, flat, l, k, slot, is_in):
        color, by = FLOWS[k]
        return table[color].at[l, (1 - by) // PAIR, slot] if is_in else flat.at[l, k, slot]

    def load(l, k, is_in, b, dst, tag):
        color, _ = FLOWS[k]
        src = block_of((ga if is_in else gb)[l], is_in, color, b, widths[k] if is_in else LANE, bases[k] if is_in else LANE * k)
        copy = pltpu.make_async_copy(src, dst, lsem.at[l, k, 0 if is_in else 1, tag])
        copy.start()
        local[l, k, is_in, tag] = copy

    def p1(l, k, s, is_in):
        color, by = FLOWS[k]
        a = place[color]
        width = widths[k] if is_in else LANE
        base = bases[k] if is_in else LANE * k
        r = [buf(ring1, rb, l, k, i, is_in) for i in range(3)]
        w = [buf(work, wb, l, k, i, is_in) for i in range(PAIR)]
        if s == 0:
            src = block_of((ga if is_in else gb)[l], is_in, color, step(a, -by), width, base)
            links.send((l, k, is_in, "p1", 0), src, r[0], peer(color, by))
            load(l, k, is_in, step(a, -PAIR * by), w[1], 0)
            load(l, k, is_in, step(a, -3 * by), w[0], 1)
            return
        mine = (None, w[1], w[0], r[0])[s]
        links.arrive((l, k, is_in, "p1", s - 1), r[s - 1], peer(color, -by))
        local[l, k, is_in, s - 1].wait()
        add_into(mine, r[s - 1])
        if s < 3:
            links.send((l, k, is_in, "p1", s), mine, r[s], peer(color, by))
            if s == 1:
                load(l, k, is_in, a, r[0], PAIR)
        else:
            p2(l, k, 0, is_in)

    def p2(l, k, s, is_in):
        color, by = FLOWS[k]
        axis = FLOW_AXES[color][0]
        a = place[axis]
        width = widths[k] if is_in else LANE
        total = buf(ring1, rb, l, k, 0, is_in)
        r = [buf(ring2, sb, l, k, i, is_in) for i in range(3)]
        mine = second(total, is_in, color, step(a, -by * (1 + s)), width)
        if s:
            links.arrive((l, k, is_in, "p2", s - 1), r[s - 1], peer(axis, -by))
            add_into(mine, r[s - 1])
        if s < 3:
            links.send((l, k, is_in, "p2", s), mine, r[s], peer(axis, by))
        else:
            axis = FLOW_AXES[color][1]
            for slot, o in enumerate(AROUND):
                part = third(mine, is_in, color, step(place[axis], o), width)
                links.send((l, k, is_in, "p3", o), part, buf(last, tb, l, k, slot, is_in), peer(axis, o))

    def final(l, k, is_in):
        return (fa.at[l, :, pl.ds(sum(widths[:k]), widths[k])] if is_in else fb.at[l, :, pl.ds(LANE * k, LANE)])

    def p3(l, k, is_in):
        color, by = FLOWS[k]
        axis2, axis3 = FLOW_AXES[color]
        width = widths[k] if is_in else LANE
        t = [buf(last, tb, l, k, i, is_in) for i in range(3)]
        for slot, o in enumerate(AROUND):
            links.arrive((l, k, is_in, "p3", o), t[slot], peer(axis3, -o))
        mine = third(second(buf(ring1, rb, l, k, 0, is_in), is_in, color, place[axis2], width), is_in, color, place[axis3], width)
        final(l, k, is_in)[ALL] = (mine[ALL] + t[0][ALL]) + (t[1][ALL] + t[PAIR][ALL])

    def pieces(l, g, p, q):
        _, flows = GROUPS[g]
        out = []
        for k in flows:
            lo = bases[k] + q * widths[k]
            lo = lo if isinstance(lo, int) else pl.multiple_of(lo, LANE)
            out.append(oa[l].at[p, :, pl.ds(lo, widths[k])])
        out.append(ob[l].at[p, q, :, pl.ds(LANE * flows[0], LANE * len(flows))])
        return out

    def fronts(l, g):
        _, flows = GROUPS[g]
        out = [fa.at[l, :, pl.ds(sum(widths[:k]), widths[k])] for k in flows]
        out.append(fb.at[l, :, pl.ds(LANE * flows[0], LANE * len(flows))])
        return out

    def line(l, g, at2, part):
        order2, flows = GROUPS[g]
        along = slice(None) if part is None else pl.ds(PAIR * part, PAIR)
        out = []
        for k in flows:
            if order2 == "yz":
                lo = bases[k] + at2 * widths[k]
                lo = lo if isinstance(lo, int) else pl.multiple_of(lo, LANE)
                out.append(oa[l].at[along, :, pl.ds(lo, widths[k])])
            else:
                span = SIDE * widths[k] if part is None else PAIR * widths[k]
                out.append(oa[l].at[at2, :, pl.ds(bases[k] + (part or 0) * PAIR * widths[k], span)])
        cols = pl.ds(LANE * flows[0], LANE * len(flows))
        out.append(ob[l].at[along, at2, :, cols] if order2 == "yz" else ob[l].at[at2, along, :, cols])
        return out

    def ag(l, g, s, is_in):
        first, then = GROUPS[g][0]
        own = [place[first], place[then]]
        mine = range(3) if is_in else (3,)

        def spot(i, j):
            return pieces(l, g, i, j) if first == "y" else pieces(l, g, j, i)

        forward = (1, 1, -1, -1) if g == 0 else (1, 1, 1, -1)
        if s == 0:
            src, dst = fronts(l, g), spot(own[0], own[1])
            for i in mine:
                for by in BOTH:
                    links.send((l, g, "a1", i, by), src[i], dst[i], peer(first, by))
                copy = pltpu.make_async_copy(src[i], dst[i], osem.at[l, g, i])
                copy.start()
                local[l, g, i] = copy
        elif s == 1:
            for by in BOTH:
                landed = spot(step(own[0], -by), own[1])
                for i in mine:
                    links.arrive((l, g, "a1", i, by), landed[i], peer(first, -by))
                    if forward[i] == by:
                        links.send((l, g, "b1", i), landed[i], landed[i], peer(first, by))
        elif s == PAIR:
            landed = spot(step(own[0], PAIR), own[1])
            part = line(l, g, own[1], None)
            for i in mine:
                local[l, g, i].wait()
                links.arrive((l, g, "b1", i), landed[i], peer(first, -forward[i]))
                for by in BOTH:
                    links.send((l, g, "a2", i, by), part[i], part[i], peer(then, by))
        elif s == 3:
            for by in BOTH:
                at2 = step(own[1], -by)
                whole, half = line(l, g, at2, None), line(l, g, at2, (1 - by) // PAIR)
                for i in mine:
                    links.arrive((l, g, "a2", i, by), whole[i], peer(then, -by))
                    links.send((l, g, "a3", i, by), half[i], half[i], peer(then, by))
        else:
            at2 = step(own[1], PAIR)
            for by in BOTH:
                half = line(l, g, at2, (1 - by) // PAIR)
                for i in mine:
                    links.arrive((l, g, "a3", i, by), half[i], peer(then, -by))

    stages = {"p1": p1, "p2": p2, "p3": lambda l, k, s, is_in: p3(l, k, is_in), "ag": ag}

    for kind, *task in order:
        stages[kind](*task)
    links.drain()


def add_into(dst, src):
    lead = dst.shape[:-PAIR]
    if len(lead) == PAIR:
        @pl.loop(0, lead[0])
        def _(i):
            for j in range(lead[1]):
                dst[i, j] += src[i, j]
    elif len(lead) == 1:
        @pl.loop(0, lead[0])
        def _(i):
            dst[i] += src[i]
    else:
        dst[ALL] += src[ALL]


def reduce_order(widths, rows, rows_b, starts):
    rate = 11650.0
    tasks = []
    for l in range(PAIR):
        for is_in in PARTS:
            for k, (color, by) in enumerate(FLOWS):
                axes = color + FLOW_AXES[color]
                full = 16 * (rows * widths[k] if is_in else rows_b * LANE) / rate
                chain = [("p1", l, k, s, is_in) for s in range(SIDE)] + [("p2", l, k, s, is_in) for s in (1, PAIR, 3)] + [("p3", l, k, 0, is_in)]
                sends = [[((axes[0], by), full)]] * 3 + [[((axes[1], by), full / SIDE)]] * 3
                sends += [[((axes[PAIR], o), full / 16) for o in (1, -1, 1)], []]
                for i, task in enumerate(chain):
                    needs = [(chain[i - 1], j) for j in range(len(sends[i - 1]))] if i else []
                    tasks.append((task, (l, i - ROW), starts[is_in][l] if i == 0 else 0.0, needs, [], sends[i]))
            for g, ((first, then), flows) in enumerate(GROUPS):
                piece = sum(rows * widths[k] if is_in else rows_b * LANE for k in flows) / rate
                for s, (axis, n) in enumerate(((first, 1), (first, 0.5), (then, SIDE), (then, PAIR), (None, 0))):
                    needs = [(("ag", l, g, s - 1, is_in), j) for j in (0, 1)] if s else []
                    after = [] if s else [("p3", l, k, 0, is_in) for k in flows]
                    sends = [((axis, by), piece * n) for by in BOTH] if axis else []
                    tasks.append((("ag", l, g, s, is_in), (l, s - 5), 0.0, needs, after, sends))
    return plan(tasks)


def reduce_gradients(ga, gb, widths=(384, 384, WIDE, WIDE, WIDE, WIDE), starts=None):
    any_space = pl.BlockSpec(memory_space=pl.ANY)
    rows = ga[0].shape[PAIR]
    rows_b = gb[0].shape[3]
    cols = SIDE * sum(widths)
    f32 = jnp.float32
    wx, wz, wy = widths[0], widths[PAIR], widths[SIDE]

    def buffers(slots, whole):
        a = {"x": (SIDE, rows, SIDE * wx), "y": (SIDE, rows, SIDE * wy), "z": (SIDE, SIDE, rows, wz)}
        b = {"x": (rows, SIDE * wx), "y": (SIDE, rows, wy), "z": (SIDE, rows, wz)}
        c = {"x": (rows, wx), "y": (rows, wy), "z": (rows, wz)}
        flat = ((SIDE, SIDE), (SIDE,), ())[whole]
        per = (a, b, c)[whole]
        return [pltpu.VMEM((PAIR, PAIR, slots, *per[color]), f32) for color in "xyz"] + [
            pltpu.VMEM((PAIR, 6, slots, *flat, rows_b, LANE), f32)]

    oa = jax.ShapeDtypeStruct((SIDE, rows, cols), f32)
    ob = jax.ShapeDtypeStruct((SIDE, SIDE, rows_b, 768), f32)
    outs = pl.pallas_call(
        functools.partial(reduce_kernel, widths, reduce_order(widths, rows, rows_b, starts or {True: (0, 40), False: (0, 60)})),
        out_shape=(oa, oa, ob, ob),
        in_specs=[any_space] * SIDE,
        out_specs=[any_space] * SIDE,
        scratch_shapes=[
            *buffers(PAIR, 0), *buffers(3, 0), *buffers(3, 1), *buffers(3, PAIR),
            pltpu.VMEM((PAIR, rows, sum(widths)), f32), pltpu.VMEM((PAIR, rows_b, 768), f32),
            pltpu.SemaphoreType.DMA((400,)), pltpu.SemaphoreType.DMA((400,)),
            pltpu.SemaphoreType.DMA((PAIR, 6, PAIR, 3)), pltpu.SemaphoreType.DMA((PAIR, PAIR, SIDE)),
        ],
        compiler_params=pltpu.CompilerParams(collective_id=1, has_side_effects=True, vmem_limit_bytes=60 << 20),
        name="reduce_gradients",
    )(*ga, *gb)
    return outs[:PAIR], outs[PAIR:]


BF, F32 = jnp.bfloat16, jnp.float32


def product(a, b, contract=((1,), (0,))):
    return lax.dot_general(a, b, (contract, ((), ())), preferred_element_type=F32)


def lanes(start, size):
    return pl.ds(start if isinstance(start, int) else pl.multiple_of(start, LANE), size)


def layers_kernel(x_ref, dy_ref, gain_ref, cos_ref, sin_ref, turn_ref, wi_a, wo_a, wi_b, wo_b,
                  y_ref, gx_ref, ht_a, ht_b, z_a, z_b, mt_a, mt_b, yp_a, yp_b, sc_out,
                  wi, wo, z, om, h, hid, qr, kts, vts, ksl, scores, dscores, pcat, dscat,
                  dot_heads, qt, dht, dkv, omt, ht, dyt, sc, load_sems, own_sems, send_sems, recv_sems):
    seq, dim = x_ref.shape
    ff = (wi_a.shape[1] - dim - LANE) // PAIR
    x, y, zc, core = chip_position()
    twin = device_at(x, y, zc, 1 - core)
    announce([twin])
    links = Links(send_sems, recv_sems)
    stored, used = [], []
    loads = []
    for i, (src, dst) in enumerate(((wi_a, wi.at[0]), (wo_a, wo.at[0]), (wi_b, wi.at[1]), (wo_b, wo.at[1]))):
        copy = pltpu.make_async_copy(src, dst, load_sems.at[i])
        copy.start()
        loads.append(copy)

    def keep(src, dst):
        copy = pltpu.make_async_copy(src, dst, own_sems.at[len(used)])
        copy.start()
        used.append(copy)
        stored.append(copy)

    def settle():
        for copy in stored:
            copy.wait()
        stored.clear()
        links.drain()

    def share(key, src, out, place):
        keep(src, place(out, 0))
        links.send(key, src, place(out, 1), twin)

    z[:, :, wi.shape[PAIR]:] = jnp.zeros((PAIR, seq, z.shape[PAIR] - wi.shape[PAIR]), BF)
    entry = (x_ref, hid.at[0])
    kts[ALL] = jnp.zeros(kts.shape, BF)
    vts[ALL] = jnp.zeros(vts.shape, BF)

    def normalise(l, src):
        @pl.loop(0, seq // BAND)
        def _(r):
            rows = pl.ds(pl.multiple_of(r * BAND, BAND), BAND)
            v = src[rows].astype(F32)
            v = v - jnp.mean(v, axis=-1, keepdims=True)
            var = jnp.mean(v * v, axis=-1, keepdims=True)
            h[l, rows] = (v * lax.rsqrt(var + 1e-6) * gain_ref[l:l + 1]).astype(BF)

    def project(l):
        def part(at, size):
            z[l, :, lanes(at, size)] = product(h[l], wi[l, :, lanes(at, size)]).astype(BF)

        n = wi.shape[PAIR] // STRIP

        @pl.loop(0, n)
        def _(i):
            part(i * STRIP, STRIP)
        part(n * STRIP, wi.shape[PAIR] - n * STRIP)

    def heads(l):
        cos, sin = cos_ref[ALL], sin_ref[ALL]
        for g in range(dim // WIDE):
            q = z[l, :, g * WIDE:(g + 1) * WIDE]
            qr[l, :, g * WIDE:(g + 1) * WIDE] = ((q.astype(F32) * cos + product(q, turn_ref[ALL]) * sin) * 0.125).astype(BF)
        kv = z[l, :, dim:dim + LANE]
        turned = kv.astype(F32) * cos[:, :LANE] + product(kv, turn_ref[:LANE, :LANE]) * sin[:, :LANE]
        first = lax.broadcasted_iota(jnp.int32, turned.shape, 1) < HEAD
        key_lo = jnp.where(first, turned, 0.0)
        val_hi = jnp.where(first, 0.0, kv.astype(F32))
        return key_lo, pltpu.roll(key_lo, HEAD, 1), pltpu.roll(val_hi, HEAD, 1), val_hi

    def slot_rows(ref, lo, hi):
        zero = jnp.zeros((seq, LANE), BF)
        lo, hi = lo.astype(BF), hi.astype(BF)
        for i, (left, right) in enumerate(((lo, zero), (hi, zero), (zero, lo), (zero, hi))):
            ref[i * seq:(i + 1) * seq, :LANE] = left
            ref[i * seq:(i + 1) * seq, LANE:] = right

    def slot_cols(ref, lo):
        flat = lo.T[:HEAD].astype(BF)
        for i in range(SIDE):
            ref[HEAD * i:HEAD * (i + 1), i * seq:(i + 1) * seq] = flat

    def chances(rows, r, i):
        s = scores[rows, i * seq:(i + 1) * seq]
        at = lax.broadcasted_iota(jnp.int32, s.shape, 0) + r * BAND
        s = jnp.where(at >= lax.broadcasted_iota(jnp.int32, s.shape, 1), s, -1e30)
        e = jnp.exp(s - jnp.max(s, axis=-1, keepdims=True))
        return e * (1.0 / jnp.sum(e, axis=-1, keepdims=True))

    def attend(l):
        key_lo, _, val_lo, val_hi = heads(l)
        slot_cols(kts, key_lo)
        slot_rows(ksl, val_lo, val_hi)

        @pl.loop(0, dim // WIDE)
        def _(g):
            cols = lanes(g * WIDE, WIDE)
            scores[ALL] = product(qr[l, :, cols], kts[ALL])

            @pl.loop(0, seq // BAND)
            def _(r):
                rows = pl.ds(pl.multiple_of(r * BAND, BAND), BAND)
                for i in range(SIDE):
                    pcat[rows, i * seq:(i + 1) * seq] = chances(rows, r, i).astype(BF)
            om[:, cols] = product(pcat[ALL], ksl[ALL]).astype(BF)

    def mlp(l):
        @pl.loop(0, seq // BAND)
        def _(r):
            rows = pl.ds(pl.multiple_of(r * BAND, BAND), BAND)

            @pl.loop(0, ff // STRIP)
            def _(i):
                gate = z[l, rows, lanes(dim + LANE + i * STRIP, STRIP)].astype(F32)
                up = z[l, rows, lanes(dim + LANE + ff + i * STRIP, STRIP)].astype(F32)
                om[rows, lanes(dim + i * STRIP, STRIP)] = (gate * jax.nn.sigmoid(gate) * up).astype(BF)

    def put_out(l, dst):
        for n in range(dim // WIDE):
            cols = slice(n * WIDE, (n + 1) * WIDE)
            total = product(om[ALL], wo[l, :, cols])
            dst[:, cols] = (entry[l][:, cols].astype(F32) + total).astype(BF)

    def flip(src, dst, width):
        @pl.loop(0, width // WIDE)
        def _(i):
            dst[pl.ds(pl.multiple_of(i * WIDE, WIDE), WIDE)] = src(i * WIDE).T

    def backward(l, dy):
        flip(lambda at: dy[:, lanes(at, WIDE)], dyt, dim)

        @pl.loop(0, wo.shape[1] // dim)
        def _(n):
            rows = pl.ds(pl.multiple_of(n * dim, dim), dim)
            part = product(wo[l, rows], dyt[ALL]).astype(BF)
            om[:, lanes(n * dim, dim)] = part.T

            @pl.when(n == 0)
            def _():
                dot_heads[ALL] = part

        @pl.loop(0, seq // BAND)
        def _(r):
            rows = pl.ds(pl.multiple_of(r * BAND, BAND), BAND)

            @pl.loop(0, ff // STRIP)
            def _(i):
                gate_at, up_at = lanes(dim + LANE + i * STRIP, STRIP), lanes(dim + LANE + ff + i * STRIP, STRIP)
                gate, up = z[l, rows, gate_at].astype(F32), z[l, rows, up_at].astype(F32)
                d = om[rows, lanes(dim + i * STRIP, STRIP)].astype(F32)
                sig = jax.nn.sigmoid(gate)
                du = d * up
                z[l, rows, gate_at] = (du * sig + du * gate * (sig * (1.0 - sig))).astype(BF)
                z[l, rows, up_at] = (d * (gate * sig)).astype(BF)

        key_lo, key_hi, val_lo, val_hi = heads(l)
        slot_cols(kts, key_lo)
        slot_cols(vts, val_lo)
        slot_rows(ksl, key_lo, key_hi)
        dkv[ALL] = jnp.zeros(dkv.shape, F32)
        flip(lambda at: qr[l, :, lanes(at, WIDE)], qt, dim)

        @pl.loop(0, dim // WIDE)
        def _(g):
            cols = lanes(g * WIDE, WIDE)
            scores[ALL] = product(qr[l, :, cols], kts[ALL])
            dscores[ALL] = product(om[:, cols], vts[ALL])

            @pl.loop(0, seq // BAND)
            def _(r):
                rows = pl.ds(pl.multiple_of(r * BAND, BAND), BAND)
                for i in range(SIDE):
                    at = slice(i * seq, (i + 1) * seq)
                    p = chances(rows, r, i)
                    pcat[rows, at] = p.astype(BF)
                    pd = p * dscores[rows, at].astype(BF).astype(F32)
                    dscat[rows, at] = (pd - p * jnp.sum(pd, axis=-1, keepdims=True)).astype(BF)
            dq = product(dscat[ALL], ksl[ALL]).astype(BF)
            back = dq.astype(F32) * cos_ref[ALL] - product(dq, turn_ref[ALL]) * sin_ref[ALL]
            z[l, :, cols] = (back * 0.125).astype(BF)
            for i in range(SIDE):
                head = pl.ds(pl.multiple_of(g * WIDE + i * HEAD, HEAD), HEAD)
                at = slice(i * seq, (i + 1) * seq)
                dkv[:HEAD] += product(qt[head], dscat[:, at])
                dkv[HEAD:] += product(dot_heads[head], pcat[:, at])

        dkv_t = dkv[ALL].T
        dk = dkv_t.astype(BF)
        turned = dk.astype(F32) * cos_ref[:, :LANE] - product(dk, turn_ref[:LANE, :LANE]) * sin_ref[:, :LANE]
        first = lax.broadcasted_iota(jnp.int32, turned.shape, 1) < HEAD
        z[l, :, dim:dim + LANE] = jnp.where(first, turned, dkv_t).astype(BF)

    def backward_rows(l, dy, dst):
        n, width = wi.shape[PAIR] // 1408, 1408
        for i in range(n):
            at = slice(i * width, (i + 1) * width)
            part = product(wi[l, :, at], z[l, :, at], ((1,), (1,)))
            dht[ALL] = part if i == 0 else dht[ALL] + part
        for i in range(dim // WIDE):
            cols = slice(i * WIDE, (i + 1) * WIDE)
            h[l, :, cols] = dht[cols].T.astype(BF)
        sc[l] = jnp.zeros(sc.shape[1:], F32)

        @pl.loop(0, seq // BAND)
        def _(r):
            rows = pl.ds(pl.multiple_of(r * BAND, BAND), BAND)
            v = entry[l][rows].astype(F32)
            v = v - jnp.mean(v, axis=-1, keepdims=True)
            scale = lax.rsqrt(jnp.mean(v * v, axis=-1, keepdims=True) + 1e-6)
            hat = v * scale
            d = h[l, rows].astype(F32)
            each = (d * hat).reshape(SIDE, ROW, dim)
            sc[l] += (each[0] + each[1]) + (each[PAIR] + each[3])
            d = d * gain_ref[l:l + 1]
            d = scale * (d - jnp.mean(d, axis=-1, keepdims=True) - hat * jnp.mean(d * hat, axis=-1, keepdims=True))
            dst[rows] = (dy[rows].astype(F32) + d.astype(BF).astype(F32)).astype(BF)

    def give_rows(l, name, src, out):
        size = src.shape[0] // ROW
        for b in range(SIDE):
            mine = src.at[pl.ds(pl.multiple_of((PAIR * b + core) * size, BAND), size)]
            other = src.at[pl.ds(pl.multiple_of((PAIR * b + 1 - core) * size, BAND), size)]
            keep(mine, out.at[b, :, pl.ds(0, seq)])
            links.send((name, l, b), other, out.at[b, :, pl.ds(seq, seq)], twin)

    for l in range(PAIR):
        loads[PAIR * l].wait()
        normalise(l, entry[l])
        settle()
        flip(lambda at: h[l, :, lanes(at, WIDE)], ht, dim)
        project(l)
        attend(l)
        mlp(l)
        flip(lambda at: om[:, lanes(at, WIDE)], omt, om.shape[1])
        loads[PAIR * l + 1].wait()
        put_out(l, hid.at[0] if l == 0 else y_ref)
        give_rows(l, "ht", ht, (ht_a, ht_b)[l])
        give_rows(l, "mt", omt, (mt_a, mt_b)[l])
    share(("y", 1), dy_ref, yp_b, lambda out, far: out.at[pl.ds(far * seq, seq)])
    for l, dy, dst in ((1, dy_ref, hid.at[1]), (0, hid.at[1], gx_ref)):
        if l == 0:
            share(("y", 0), dy, yp_a, lambda out, far: out.at[pl.ds(far * seq, seq)])
        backward(l, dy)
        share(("z", l), z.at[l], (z_a, z_b)[l], lambda out, far: out.at[pl.ds(far * seq, seq)])
        backward_rows(l, dy, dst)
        share(("sc", l), sc.at[l], sc_out.at[l], lambda out, far: out.at[far])
    settle()
    for l in range(PAIR):
        for b in range(SIDE):
            links.arrive(("ht", l, b), (ht_a, ht_b)[l].at[b, :, pl.ds(seq, seq)], twin)
            links.arrive(("mt", l, b), (mt_a, mt_b)[l].at[b, :, pl.ds(seq, seq)], twin)
        links.arrive(("y", l), (yp_a, yp_b)[l].at[pl.ds(seq, seq)], twin)
        links.arrive(("z", l), (z_a, z_b)[l].at[pl.ds(seq, seq)], twin)
        links.arrive(("sc", l), sc_out.at[l, 1], twin)


def run_layers(x, dy, gain, cos, sin, turn, weights):
    seq, dim = x.shape
    proj, cat = weights[0].shape[1], weights[1].shape[0]
    wide = proj + LANE
    any_space, vmem = pl.BlockSpec(memory_space=pltpu.HBM), pl.BlockSpec(memory_space=pltpu.VMEM)
    out = lambda *shape, dtype=BF: jax.ShapeDtypeStruct(shape, dtype)
    buffer = lambda *shape, dtype=BF: pltpu.VMEM(shape, dtype)
    pair = PAIR * seq
    return pl.pallas_call(
        layers_kernel,
        out_shape=(out(seq, dim), out(seq, dim), *[out(SIDE, dim // ROW, pair)] * PAIR, *[out(pair, wide)] * PAIR, *[out(SIDE, cat // ROW, pair)] * PAIR,
                   *[out(pair, dim)] * PAIR, out(PAIR, PAIR, ROW, dim, dtype=F32)),
        in_specs=[vmem] * 6 + [any_space] * SIDE,
        out_specs=[vmem] * PAIR + [any_space] * 9,
        scratch_shapes=[
            buffer(PAIR, dim, proj), buffer(PAIR, cat, dim), buffer(PAIR, seq, wide), buffer(seq, cat), buffer(PAIR, seq, dim),
            buffer(PAIR, seq, dim), buffer(PAIR, seq, dim),
            buffer(WIDE, SIDE * seq), buffer(WIDE, SIDE * seq), buffer(SIDE * seq, WIDE),
            buffer(seq, SIDE * seq, dtype=F32), buffer(seq, SIDE * seq, dtype=F32), buffer(seq, SIDE * seq), buffer(seq, SIDE * seq),
            buffer(dim, seq), buffer(dim, seq), buffer(dim, seq, dtype=F32), buffer(LANE, seq, dtype=F32),
            buffer(cat, seq), buffer(dim, seq), buffer(dim, seq), buffer(PAIR, ROW, dim, dtype=F32),
            pltpu.SemaphoreType.DMA((SIDE,)), pltpu.SemaphoreType.DMA((BAND,)), pltpu.SemaphoreType.DMA((BAND,)), pltpu.SemaphoreType.DMA((BAND,)),
        ],
        compiler_params=pltpu.CompilerParams(collective_id=PAIR, has_side_effects=True, vmem_limit_bytes=67043328),
        name="run_layers",
    )(x, dy, gain, cos, sin, turn, *weights)


def rotary_tables(seq_len, head_dim):
    half_dim = head_dim // PAIR
    inv_freq = 10000.0 ** (-(jnp.arange(half_dim, dtype=jnp.float32) * 2.0 / head_dim))
    angles = jnp.arange(seq_len, dtype=jnp.float32)[:, None] * inv_freq[None, :]
    return jnp.cos(angles), jnp.sin(angles)


def solution(mesh):
    fsdp_size = mesh.shape["fsdp"]
    batch_spec = P(("dp", "fsdp"), None, None)
    scale_spec = P(None, "fsdp")
    weight_spec = P(None, "fsdp", None)

    def device_step(x_in, grad_y, norm_scale, w_in, w_out):
        n_layers = w_in.shape[0]
        seq_len, model_dim = x_in.shape[1:]
        proj_dim = w_in.shape[PAIR]
        ff_dim = w_out.shape[1] * fsdp_size - model_dim
        head_dim = (proj_dim - model_dim - PAIR * ff_dim) // PAIR
        rows, rows_out = norm_scale.shape[1], w_out.shape[1]
        scale_tile = jnp.pad(norm_scale.astype(jnp.float32), ((0, ROW - n_layers), (0, LANE - rows)))
        scales, *gathered = gather_weights(scale_tile, w_in, w_out)
        scale_full = scales[:, :n_layers, :rows].transpose(1, 0, PAIR).reshape(n_layers, model_dim)
        cos_tab, sin_tab = rotary_tables(seq_len, head_dim)
        cos_tab, sin_tab = jnp.tile(cos_tab, (1, ROW)), jnp.tile(sin_tab, (1, ROW))
        lane = jnp.arange(WIDE)
        down = lane[:, None] - lane[None, :]
        low = lane[None, :] % head_dim < head_dim // PAIR
        turn = jnp.where(low & (down == BAND), -1.0, jnp.where(~low & (down == -BAND), 1.0, 0.0)).astype(jnp.bfloat16)
        weights = [w.reshape(-1, w.shape[-1]) for w in gathered]
        hidden, grad_hidden, *rest = run_layers(x_in[0], grad_y[0], jnp.pad(scale_full, ((0, ROW - n_layers), (0, 0))), cos_tab, sin_tab, turn, weights)
        h_rows, z_cols, m_rows, y_cols, scale_parts = rest[0:PAIR], rest[PAIR:SIDE], rest[SIDE:6], rest[6:ROW], rest[ROW]
        in_parts, out_parts = [], []
        for l in range(n_layers):
            part_in = jnp.dot(h_rows[l].reshape(SIDE * rows, -1), z_cols[l], preferred_element_type=jnp.float32)
            in_parts.append(part_in.reshape(SIDE, SIDE, rows // SIDE, proj_dim + LANE))
            part_out = jnp.dot(m_rows[l].reshape(SIDE * rows_out, -1), y_cols[l], preferred_element_type=jnp.float32).reshape(SIDE, rows_out, model_dim)
            part_out = jnp.pad(part_out, ((0, 0), (0, BAND), (0, 0)))
            part_scale = jnp.broadcast_to(scale_parts[l].sum((0, 1)), (SIDE, 1, model_dim))
            part_out = lax.dynamic_update_slice(part_out, part_scale, (0, rows_out, 0))
            out_parts.append(part_out.reshape(SIDE, SIDE, SIDE, (rows_out + BAND) // 16, model_dim))
        in_sums, out_sums = reduce_gradients(in_parts[::-1], out_parts[::-1])
        in_grads = jnp.stack([g.reshape(rows, -1)[:, :proj_dim] for g in in_sums[::-1]])
        out_rows = [g.reshape(-1, model_dim) for g in out_sums[::-1]]
        out_grads = jnp.stack([g[:rows_out] for g in out_rows])
        scale_grads = jnp.stack([lax.dynamic_slice(g[rows_out], (lax.axis_index("fsdp") * rows,), (rows,)) for g in out_rows])
        return hidden[None], grad_hidden[None], scale_grads, in_grads, out_grads

    return jax.shard_map(
        device_step,
        mesh=mesh,
        in_specs=(batch_spec, batch_spec, scale_spec, weight_spec, weight_spec),
        out_specs=(batch_spec, batch_spec, scale_spec, weight_spec, weight_spec),
        check_vma=False,
    )
```

time: 486 us -> 426 us (0.88); the launches traced: 476 us -> 426 us
  Pallas kernels: 271 us -> 360 us
  matrix products: 95.3 us -> 22.7 us
  other arithmetic: 45.5 us -> 6.73 us
  local copies, waits for them, and re-layouts: 58.4 us -> 35.1 us
    pallas_call x0 -> x1, Pallas kernels: none -> 89.7 us  [run_layers(): pl.pallas_call(layers_kernel, out_shape=(out(seq, dim), out(seq, dim), *[...]
    dot_general x24 -> x4, matrix products: 95.3 us -> 22.7 us  [the longest x2 17.6 us: device_step(): jnp.dot(h_rows[l].reshape(SIDE * rows, -1), z_cols[l], preferred_element_...]
    convert_element_type x13 -> x1, other arithmetic: 13.6 us -> 0.71 us  [device_step(): jnp.where(low & (down == BAND), -1.0, jnp.where(~low & (down == -BAND), 1...]
    another operation x3 -> x1, other arithmetic: 8.57 us -> 0.57 us  [device_step(): jnp.stack([lax.dynamic_slice(g[rows_out], (lax.axis_index('fsdp') * rows,...]
    reshape x6 -> x1, local copies, waits for them, and re-layouts: 7.86 us -> 0.08 us  [device_step(): scales[:, :n_layers, :rows].transpose(1, 0, PAIR)]
    concatenate x8 -> x0, other arithmetic: 7.46 us -> none  [the longest x2 3.26 us: mix_block(): return jnp.concatenate([attn_out, mlp_out], axis=-1)]
    pad x0 -> x3, local copies, waits for them, and re-layouts: none -> 7.3 us  [the longest x2 6.68 us: device_step(): part_out = jnp.pad(part_out, ((0, 0), (0, BAND), (0, 0)))]
    split x4 -> x0, local copies, waits for them, and re-layouts: 5.37 us -> none  [mix_block(): return jnp.concatenate([attn_out, mlp_out], axis=-1)]
  transfers between devices with their start and end apart: 10 -> 0, of which waited for: 0 -> 0; matrix products, arithmetic and copies ran while one was open for 28% -> 0% of each run, Pallas kernels for 0% -> 0%
where the time goes in v1:
time: 426 us
  Pallas kernels  360 us (85%)
  local copies, waits for them, and re-layouts  35.1 us (8%)
  matrix products  22.7 us (5%)
  other arithmetic  6.73 us (2%)
    pallas_call x1, Pallas kernels, reduce_gradients(): pl.pallas_call(functools.partial(reduce_kernel, widths, reduce_order(widt...  196 us
    pallas_call x1, Pallas kernels, run_layers(): pl.pallas_call(layers_kernel, out_shape=(out(seq, dim), out(seq, dim), *[...  89.7 us
    pallas_call x1, Pallas kernels, gather_weights(): pl.pallas_call(functools.partial(gather_kernel, gather_order(*w_in.shape[...  75.2 us
    unnamed x34, local copies, waits for them, and re-layouts  19.9 us
    dot_general x2, matrix products, device_step(): jnp.dot(h_rows[l].reshape(SIDE * rows, -1), z_cols[l], preferred_element_...  17.6 us

profile of v1, /device:TPU:0, one launch (start us, length us, event | category | flops | bytes accessed | tf_op | source)
XLA Modules:
  0.0 425.8 jit_solution(16206030862138384018)
XLA Ops:
  0.6 0.7 pad_convert_fusion.sc_in
  1.3 1.8 copy-done.4
  3.1 1.4 copy-done.5
  4.4 75.2 %gather_weights.1 = (f32[8,8,128]{2,1,0:T(8,128)S(1)}, bf16[4,2,96,7040]{3,2,1,0:T(8,128)(2,1)S(1)}, bf16[4,2,480,768]{3,2,1,0:T(8,128)(2,1)S(1)}, bf16[4,2,96,7...) custom-call(f32[8,128]{1,0:T(8,128)S(1)} %pad_convert_fusion.sc_in, bf16[2,96,7040]{2,1,0:T(8,128)(2,1)S(1)} %copy-done.4, ...), custom_call_target="tpu_custom_call" | custom-call | tf_op jit(solution)/shard_map/gather_weights/pallas_call | solution.py:257
  79.7 4.1 copy-done
  83.8 4.0 copy-done.1
  87.7 2.5 copy-done.2
  90.2 2.6 copy-done.3
  92.9 0.6 pad.19.gain_ref
  93.5 0.7 select_convert_fusion.turn_ref
  94.5 0.8 copy.12.cos_ref
  95.3 0.8 copy.13.sin_ref
  96.2 89.7 %run_layers.1 = (bf16[256,768]{1,0:T(8,128)(2,1)}, bf16[256,768]{1,0:T(8,128)(2,1)}, bf16[4,96,512]{2,1,0:T(8,128)(2,1)}, bf16[4,96,512]{2,1,0:T(8,128)(2,1)}, b...) custom-call(bf16[256,768]{1,0:T(8,128)(2,1)} %bitcast.62, ...), custom_call_target="tpu_custom_call" | custom-call | tf_op jit(solution)/shard_map/run_layers/pallas_call | solution.py:832
  185.8 3.4 fusion.4
  189.3 3.4 pad.21
  192.7 1.6 dynamic_update_slice.7
  194.3 1.7 fusion.6
  196.0 3.3 pad.20
  199.3 1.6 dynamic_update_slice.6
  200.9 8.9 %fusion.refs_1_ = f32[4,4,24,7168]{3,2,1,0:T(8,128)} fusion(bf16[4,4,24,512]{3,2,1,0:T(8,128)(2,1)S(1)} %bitcast.67, bf16[512,7168]{1,0:T(8,128)(2,1)} %get-tuple-element.35), kind=kOutput, calls=%fused_computation | convolution fusion | flops 2818572288 | bytes 18743296 | tf_op jit(solution)/shard_map/dot_general | solution.py:886
  209.8 8.7 %fusion.2.refs_0_ = f32[4,4,24,7168]{3,2,1,0:T(8,128)} fusion(bf16[4,4,24,512]{3,2,1,0:T(8,128)(2,1)S(1)} %bitcast.66, bf16[512,7168]{1,0:T(8,128)(2,1)} %get-tuple-element.33), kind=kOutput, calls=%fused_computation.2 | convolution fusion | flops 2818572288 | bytes 18743296 | tf_op jit(solution)/shard_map/dot_general | solution.py:886
  218.5 195.5 %reduce_gradients.1 = (f32[4,24,7168]{2,1,0:T(8,128)}, f32[4,24,7168]{2,1,0:T(8,128)}, f32[4,4,32,768]{3,2,1,0:T(8,128)}, f32[4,4,32,768]{3,2,1,0:T(8,128)}) custom-call(f32[4,4,24,7168]{3,2,1,0:T(8,128)} %fusion.2.refs_0_, f32[4,4,24,7168]{3,2,1,0:T(8,128)} %fusion.refs_1_, f32[4,4,4,32,768]{4,3,2,1,0:T(8,128)} %bitcast.53, f32[4,4,4,32,768]{4,3,2,1,0:T(8,128)} %bitcast.52), custom_call_target="tpu_custom_call" | custom-call | tf_op jit(solution)/shard_map/reduce_gradients/pallas_call | solution.py:540
  414.1 1.6 slice_bitcast_fusion.2
  415.6 0.3 copy-done.9
  416.0 1.8 pad_maximum_fusion.1
  417.8 1.0 copy-done.7
  419.0 0.8 copy-done.6
  420.1 2.8 pad_maximum_fusion
  422.9 0.7 slice.37
  423.7 0.6 pad_maximum_fusion.2
  424.3 0.7 copy.20
  425.0 0.7 copy.21
  (40 shorter events, 1.0 us)
Async XLA Ops:
  1.3 1.8 copy-start.4
  3.1 1.4 copy-start.5
  79.7 4.1 copy-start
  83.8 4.0 copy-start.1
  87.7 2.5 copy-start.2
  90.2 2.6 copy-start.3
  189.3 3.4 copy-start.13
  189.3 5.0 %copy-start.8 = (bf16[4,480,512]{2,1,0:T(8,128)(2,1)S(1)}, bf16[4,480,512]{2,1,0:T(8,128)(2,1)}, u32[]{:S(2)}) copy-start(bf16[4,480,512]{2,1,0:T(8,128)(2,1)} %get-tuple-element.36) | copy-start | bytes 5898244
  189.3 5.0 %copy-start.10 = (bf16[512,768]{1,0:T(8,128)(2,1)S(1)}, bf16[512,768]{1,0:T(8,128)(2,1)}, u32[]{:S(2)}) copy-start(bf16[512,768]{1,0:T(8,128)(2,1)} %get-tuple-element.37) | copy-start | bytes 2359300
  196.0 4.9 %copy-start.15 = (bf16[4,96,512]{2,1,0:T(8,128)(2,1)S(1)}, bf16[4,96,512]{2,1,0:T(8,128)(2,1)}, u32[]{:S(2)}) copy-start(bf16[4,96,512]{2,1,0:T(8,128)(2,1)} %get-tuple-element.34) | copy-start | bytes 1179652
  200.9 8.9 %copy-start.14 = (bf16[4,96,512]{2,1,0:T(8,128)(2,1)S(1)}, bf16[4,96,512]{2,1,0:T(8,128)(2,1)}, u32[]{:S(2)}) copy-start(bf16[4,96,512]{2,1,0:T(8,128)(2,1)} %get-tuple-element.32) | copy-start | bytes 1179652
  414.0 1.9 copy-start.9
  416.0 2.8 copy-start.7
  417.8 2.1 copy-start.6
  420.0 4.2 copy-start.12
  420.1 5.0 %copy-start.11 = (bf16[256,768]{1,0:T(8,128)(2,1)S(1)}, bf16[256,768]{1,0:T(8,128)(2,1)}, u32[]{:S(2)}) copy-start(bf16[256,768]{1,0:T(8,128)(2,1)} %get-tuple-element.31) | copy-start | bytes 1179652

commit v2 on v1

--- a/solution.py
+++ b/solution.py
@@ -18,28 +18,24 @@
 class Links:
     def __init__(self, send_sems, recv_sems):
         self.send_sems, self.recv_sems = send_sems, recv_sems
-        self.slots, self.sent = {}, []
-
-    def _slot(self, key):
-        return self.slots.setdefault(key, len(self.slots))
-
-    def send(self, key, src, dst, device):
-        slot = self._slot(key)
+        self.slots, self.batches, self.sent = {}, {}, {}
+
+    def send(self, key, src, dst, device, landing=None, whole=None, batch=None):
+        slot = self.slots.setdefault(landing or key, len(self.slots))
+        leaving = self.batches.setdefault(batch or key, len(self.batches))
         copy = pltpu.make_async_remote_copy(
-            src_ref=src, dst_ref=dst, send_sem=self.send_sems.at[slot], recv_sem=self.recv_sems.at[slot],
+            src_ref=src, dst_ref=dst, send_sem=self.send_sems.at[leaving], recv_sem=self.recv_sems.at[slot],
             device_id=device, device_id_type=MESH_ID)
         copy.start()
-        self.sent.append(copy)
-
-    def arrive(self, key, landed, device):
-        slot = self._slot(key)
-        pltpu.make_async_remote_copy(
-            src_ref=landed, dst_ref=landed, send_sem=self.send_sems.at[slot], recv_sem=self.recv_sems.at[slot],
-            device_id=device, device_id_type=MESH_ID).wait_recv()
+        self.sent[batch or key] = (whole or src, leaving)
+
+    def arrive(self, key, landed):
+        slot = self.slots.setdefault(key, len(self.slots))
+        pltpu.make_async_copy(landed, landed, self.recv_sems.at[slot]).wait()
 
     def drain(self):
-        for copy in self.sent:
-            copy.wait_send()
+        for left, leaving in self.sent.values():
+            pltpu.make_async_copy(left, left, self.send_sems.at[leaving]).wait()
         self.sent.clear()
 
 
@@ -72,17 +68,17 @@
     left = list(tasks)
     while left:
         best = None
-        for place, (name, rank, start, needs, after, sends) in enumerate(left):
+        for place, (name, rank, start, needs, after, _, _) in enumerate(left):
             if all(n[0] in landed for n in needs) and all(n in landed for n in after):
                 ready = max([start, now] + [landed[task][i] for task, i in needs])
                 best = min(best or (ready, rank, place), (ready, rank, place))
         now, _, place = best
-        name, _, _, _, _, sends = left.pop(place)
+        name, _, _, _, _, sends, cost = left.pop(place)
         order.append(name)
-        now += 0.2
+        now += cost
         landed[name] = []
-        for link, cost in sends:
-            free[link] = max(now, free.get(link, 0.0)) + cost
+        for link, time in sends:
+            free[link] = max(now, free.get(link, 0.0)) + time
             landed[name].append(free[link] + latency)
     return order
 
@@ -99,23 +95,23 @@
             cost = size[color] / rate
             both = [(("x", by), cost) for by in BOTH]
             spread = [((color, by), cost) for by in BOTH] if color != "x" else []
-            tasks.append((("reach", m, color), m, starts[m], [], [], both))
+            tasks.append((("reach", m, color), m, starts[m], [], [], both, 0.2))
             for i, by in enumerate(BOTH):
-                tasks.append((("relay", m, color, by), m, 0.0, [(("reach", m, color), i)], [], [(("x", by), cost / PAIR)] + spread))
+                tasks.append((("relay", m, color, by), m, 0.0, [(("reach", m, color), i)], [], [(("x", by), cost / PAIR)] + spread, 0.2))
             halves = [(("relay", m, color, by), 0) for by in BOTH]
-            tasks.append((("far", m, color), m, 0.0, halves, [], spread))
+            tasks.append((("far", m, color), m, 0.0, halves, [], spread, 0.2))
             if color == "x":
                 continue
             for off, source, first in ((-1, ("relay", m, color, 1), 1), (1, ("relay", m, color, -1), 1), (PAIR, ("far", m, color), 0)):
                 for i, by in enumerate(BOTH):
-                    tasks.append((("pass", m, color, off, by), m, 0.0, [(source, first + i)], [], [((color, by), cost / PAIR)]))
+                    tasks.append((("pass", m, color, off, by), m, 0.0, [(source, first + i)], [], [((color, by), cost / PAIR)], 0.2))
                 halves = [(("pass", m, color, off, by), 0) for by in BOTH]
-                tasks.append((("close", m, color, off), m, 0.0, halves, [], []))
+                tasks.append((("close", m, color, off), m, 0.0, halves, [], [], 0.2))
         for off in (-1, 1, PAIR):
             last = [("close", m, color, off) for color in "yz"]
             if is_in:
                 last.append(("far", m, "x") if off == PAIR else ("relay", m, "x", -off))
-            tasks.append((("hand", m, off), m, 0.0, [], last, []))
+            tasks.append((("hand", m, off), m, 0.0, [], last, [], 0.2))
     return plan(tasks)
 
 
@@ -131,10 +127,19 @@
     cut_o = quarter_o // 16 * ROW + ROW if quarter_o % 16 else quarter_o // PAIR
     place = {"x": x, "y": y, "z": z}
 
-    def peer(axis, by):
-        moved = dict(place)
-        moved[axis] = step(place[axis], by)
-        return device_at(moved["x"], moved["y"], moved["z"], core)
+    spots = {(axis, o): step(place[axis], o) for axis in "xyz" for o in range(SIDE)}
+
+    def spot(axis, o):
+        return spots[axis, o % SIDE]
+
+    table = {}
+    for axis in "xyz":
+        for o in range(1, SIDE):
+            moved = {**place, axis: spot(axis, o)}
+            table[axis, o] = device_at(moved["x"], moved["y"], moved["z"], core)
+
+    def peer(axis, o):
+        return table[axis, o % SIDE]
 
     peers = [peer(axis, by) for axis in "xyz" for by in BOTH]
     others = [(lax.axis_index("dp"), lax.rem(lax.axis_index("fsdp") + k, ROW)) for k in range(1, ROW)]
@@ -177,15 +182,15 @@
 
     def launch(m, color, off):
         _, out, _, is_in = mats[m]
-        block = at(out, (step(x, off), core), region(is_in, color, place[color])[0])
+        block = at(out, (spot("x", off), core), region(is_in, color, place[color])[0])
         for by in BOTH:
             links.send((m, "p1", color, off, by), block, block, peer(color, by))
 
     def relay(m, color, by):
         _, out, _, is_in = mats[m]
-        xb = step(x, -by)
+        xb = spot("x", -by)
         areas = region(is_in, color, place[color])
-        links.arrive((m, "x1", color, by), at(out, (xb, core), areas[0]), peer("x", -by))
+        links.arrive((m, "x1", color, by), at(out, (xb, core), areas[0]))
         part = at(out, (xb, core), areas[1] if by == 1 else areas[PAIR])
         links.send((m, "x2", color, by), part, part, peer("x", by))
         if color != "x":
@@ -195,27 +200,27 @@
         _, out, _, is_in = mats[m]
         areas = region(is_in, color, place[color])
         for by in BOTH:
-            links.arrive((m, "x2", color, by), at(out, (step(x, PAIR), core), areas[1] if by == 1 else areas[PAIR]), peer("x", -by))
+            links.arrive((m, "x2", color, by), at(out, (spot("x", PAIR), core), areas[1] if by == 1 else areas[PAIR]))
         if color != "x":
             launch(m, color, PAIR)
 
     def pass_on(m, color, off, by):
         _, out, _, is_in = mats[m]
-        xb = step(x, off)
-        areas = region(is_in, color, step(place[color], -by))
-        links.arrive((m, "p1", color, off, by), at(out, (xb, core), areas[0]), peer(color, -by))
+        xb = spot("x", off)
+        areas = region(is_in, color, spot(color, -by))
+        links.arrive((m, "p1", color, off, by), at(out, (xb, core), areas[0]))
         part = at(out, (xb, core), areas[1] if by == 1 else areas[PAIR])
         links.send((m, "p2", color, off, by), part, part, peer(color, by))
 
     def close(m, color, off):
         _, out, _, is_in = mats[m]
-        areas = region(is_in, color, step(place[color], PAIR))
+        areas = region(is_in, color, spot(color, PAIR))
         for by in BOTH:
-            links.arrive((m, "p2", color, off, by), at(out, (step(x, off), core), areas[1] if by == 1 else areas[PAIR]), peer(color, -by))
+            links.arrive((m, "p2", color, off, by), at(out, (spot("x", off), core), areas[1] if by == 1 else areas[PAIR]))
 
     def hand(m, off):
         _, out, _, _ = mats[m]
-        links.send((m, "d2d", off), out.at[step(x, off), core], out.at[step(x, off), core], twin)
+        links.send((m, "d2d", off), out.at[spot("x", off), core], out.at[spot("x", off), core], twin)
 
     stages = {"reach": reach, "relay": relay, "far": far, "pass": pass_on, "close": close, "hand": hand}
 
@@ -240,18 +245,18 @@
         stages[kind](*task)
     for m, (src, out, own, _) in enumerate(mats):
         for off in (0, -1, 1, PAIR):
-            xb = step(x, off)
-            links.arrive((m, "d2d", off), out.at[xb, 1 - core], twin)
+            xb = spot("x", off)
+            links.arrive((m, "d2d", off), out.at[xb, 1 - core])
         stores[m].wait()
     own_scale.wait()
     for k in range(7):
         source = lax.rem(lax.axis_index("fsdp") + 7 - k, ROW)
-        links.arrive(("sc", k), sc_out.at[source], others[k])
+        links.arrive(("sc", k), sc_out.at[source])
     links.drain()
 
 
 def gather_weights(scale_tile, w_in, w_out, starts=None, n_copies=320):
-    any_space = pl.BlockSpec(memory_space=pl.ANY)
+    any_space = pl.BlockSpec(memory_space=pltpu.HBM)
     wi = jax.ShapeDtypeStruct((SIDE, PAIR, *w_in.shape[1:]), w_in.dtype)
     wo = jax.ShapeDtypeStruct((SIDE, PAIR, *w_out.shape[1:]), w_out.dtype)
     return pl.pallas_call(
@@ -269,289 +274,6 @@
         compiler_params=pltpu.CompilerParams(collective_id=0, has_side_effects=True, vmem_limit_bytes=12 << 20),
         name="gather_weights",
     )(scale_tile, w_in, w_out)
-
-
-FLOW_AXES = {"x": "yz", "y": "zx", "z": "xy"}
-FLOWS = (("x", 1), ("x", -1), ("z", 1), ("z", -1), ("y", 1), ("y", -1))
-GROUPS = (("yz", (0, 1, PAIR)), ("zy", (3, SIDE, 5)))
-
-
-def block_of(ref, is_in, color, b, width, base):
-    cols = pl.ds(base, width if color == "z" and is_in else width * (SIDE if is_in else 1))
-    if is_in:
-        if color == "x":
-            return ref.at[b, :, :, cols]
-        if color == "y":
-            return ref.at[:, b, :, cols]
-        return ref.at[:, :, :, pl.ds(pl.multiple_of(base + b * width, LANE) if not isinstance(b, int) else base + b * width, width)]
-    if color == "x":
-        return ref.at[b, :, :, :, cols]
-    if color == "y":
-        return ref.at[:, b, :, :, cols]
-    return ref.at[:, :, b, :, cols]
-
-
-def second(ref, is_in, color, b, width):
-    if is_in:
-        if color == "y":
-            return ref.at[:, :, pl.ds(pl.multiple_of(b * width, LANE) if not isinstance(b, int) else b * width, width)]
-        return ref.at[b]
-    return ref.at[:, b] if color == "y" else ref.at[b]
-
-
-def third(ref, is_in, color, b, width):
-    if is_in and color == "x":
-        return ref.at[:, pl.ds(pl.multiple_of(b * width, LANE) if not isinstance(b, int) else b * width, width)]
-    return ref.at[b]
-
-
-def reduce_kernel(widths, order, *refs):
-    n = PAIR
-    ga, gb = refs[0:n], refs[n:PAIR * n]
-    oa, ob = refs[PAIR * n:3 * n], refs[3 * n:SIDE * n]
-    (wx, wy, wz, wb, rx, ry, rz, rb, sx, sy, sz, sb, tx, ty, tz, tb, fa, fb, ssem, rsem, lsem, osem) = refs[SIDE * n:]
-    x, y, z, core = chip_position()
-    place = {"x": x, "y": y, "z": z}
-    work = {"x": wx, "y": wy, "z": wz}
-    ring1 = {"x": rx, "y": ry, "z": rz}
-    ring2 = {"x": sx, "y": sy, "z": sz}
-    last = {"x": tx, "y": ty, "z": tz}
-    bases = [sum(widths[:k]) * SIDE for k in range(6)]
-
-    def peer(axis, by):
-        moved = dict(place)
-        moved[axis] = step(place[axis], by)
-        return device_at(moved["x"], moved["y"], moved["z"], core)
-
-    announce([peer(axis, by) for axis in "xyz" for by in AROUND])
-    links = Links(ssem, rsem)
-    local = {}
-
-    def buf(table, flat, l, k, slot, is_in):
-        color, by = FLOWS[k]
-        return table[color].at[l, (1 - by) // PAIR, slot] if is_in else flat.at[l, k, slot]
-
-    def load(l, k, is_in, b, dst, tag):
-        color, _ = FLOWS[k]
-        src = block_of((ga if is_in else gb)[l], is_in, color, b, widths[k] if is_in else LANE, bases[k] if is_in else LANE * k)
-        copy = pltpu.make_async_copy(src, dst, lsem.at[l, k, 0 if is_in else 1, tag])
-        copy.start()
-        local[l, k, is_in, tag] = copy
-
-    def p1(l, k, s, is_in):
-        color, by = FLOWS[k]
-        a = place[color]
-        width = widths[k] if is_in else LANE
-        base = bases[k] if is_in else LANE * k
-        r = [buf(ring1, rb, l, k, i, is_in) for i in range(3)]
-        w = [buf(work, wb, l, k, i, is_in) for i in range(PAIR)]
-        if s == 0:
-            src = block_of((ga if is_in else gb)[l], is_in, color, step(a, -by), width, base)
-            links.send((l, k, is_in, "p1", 0), src, r[0], peer(color, by))
-            load(l, k, is_in, step(a, -PAIR * by), w[1], 0)
-            load(l, k, is_in, step(a, -3 * by), w[0], 1)
-            return
-        mine = (None, w[1], w[0], r[0])[s]
-        links.arrive((l, k, is_in, "p1", s - 1), r[s - 1], peer(color, -by))
-        local[l, k, is_in, s - 1].wait()
-        add_into(mine, r[s - 1])
-        if s < 3:
-            links.send((l, k, is_in, "p1", s), mine, r[s], peer(color, by))
-            if s == 1:
-                load(l, k, is_in, a, r[0], PAIR)
-        else:
-            p2(l, k, 0, is_in)
-
-    def p2(l, k, s, is_in):
-        color, by = FLOWS[k]
-        axis = FLOW_AXES[color][0]
-        a = place[axis]
-        width = widths[k] if is_in else LANE
-        total = buf(ring1, rb, l, k, 0, is_in)
-        r = [buf(ring2, sb, l, k, i, is_in) for i in range(3)]
-        mine = second(total, is_in, color, step(a, -by * (1 + s)), width)
-        if s:
-            links.arrive((l, k, is_in, "p2", s - 1), r[s - 1], peer(axis, -by))
-            add_into(mine, r[s - 1])
-        if s < 3:
-            links.send((l, k, is_in, "p2", s), mine, r[s], peer(axis, by))
-        else:
-            axis = FLOW_AXES[color][1]
-            for slot, o in enumerate(AROUND):
-                part = third(mine, is_in, color, step(place[axis], o), width)
-                links.send((l, k, is_in, "p3", o), part, buf(last, tb, l, k, slot, is_in), peer(axis, o))
-
-    def final(l, k, is_in):
-        return (fa.at[l, :, pl.ds(sum(widths[:k]), widths[k])] if is_in else fb.at[l, :, pl.ds(LANE * k, LANE)])
-
-    def p3(l, k, is_in):
-        color, by = FLOWS[k]
-        axis2, axis3 = FLOW_AXES[color]
-        width = widths[k] if is_in else LANE
-        t = [buf(last, tb, l, k, i, is_in) for i in range(3)]
-        for slot, o in enumerate(AROUND):
-            links.arrive((l, k, is_in, "p3", o), t[slot], peer(axis3, -o))
-        mine = third(second(buf(ring1, rb, l, k, 0, is_in), is_in, color, place[axis2], width), is_in, color, place[axis3], width)
-        final(l, k, is_in)[ALL] = (mine[ALL] + t[0][ALL]) + (t[1][ALL] + t[PAIR][ALL])
-
-    def pieces(l, g, p, q):
-        _, flows = GROUPS[g]
-        out = []
-        for k in flows:
-            lo = bases[k] + q * widths[k]
-            lo = lo if isinstance(lo, int) else pl.multiple_of(lo, LANE)
-            out.append(oa[l].at[p, :, pl.ds(lo, widths[k])])
-        out.append(ob[l].at[p, q, :, pl.ds(LANE * flows[0], LANE * len(flows))])
-        return out
-
-    def fronts(l, g):
-        _, flows = GROUPS[g]
-        out = [fa.at[l, :, pl.ds(sum(widths[:k]), widths[k])] for k in flows]
-        out.append(fb.at[l, :, pl.ds(LANE * flows[0], LANE * len(flows))])
-        return out
-
-    def line(l, g, at2, part):
-        order2, flows = GROUPS[g]
-        along = slice(None) if part is None else pl.ds(PAIR * part, PAIR)
-        out = []
-        for k in flows:
-            if order2 == "yz":
-                lo = bases[k] + at2 * widths[k]
-                lo = lo if isinstance(lo, int) else pl.multiple_of(lo, LANE)
-                out.append(oa[l].at[along, :, pl.ds(lo, widths[k])])
-            else:
-                span = SIDE * widths[k] if part is None else PAIR * widths[k]
-                out.append(oa[l].at[at2, :, pl.ds(bases[k] + (part or 0) * PAIR * widths[k], span)])
-        cols = pl.ds(LANE * flows[0], LANE * len(flows))
-        out.append(ob[l].at[along, at2, :, cols] if order2 == "yz" else ob[l].at[at2, along, :, cols])
-        return out
-
-    def ag(l, g, s, is_in):
-        first, then = GROUPS[g][0]
-        own = [place[first], place[then]]
-        mine = range(3) if is_in else (3,)
-
-        def spot(i, j):
-            return pieces(l, g, i, j) if first == "y" else pieces(l, g, j, i)
-
-        forward = (1, 1, -1, -1) if g == 0 else (1, 1, 1, -1)
-        if s == 0:
-            src, dst = fronts(l, g), spot(own[0], own[1])
-            for i in mine:
-                for by in BOTH:
-                    links.send((l, g, "a1", i, by), src[i], dst[i], peer(first, by))
-                copy = pltpu.make_async_copy(src[i], dst[i], osem.at[l, g, i])
-                copy.start()
-                local[l, g, i] = copy
-        elif s == 1:
-            for by in BOTH:
-                landed = spot(step(own[0], -by), own[1])
-                for i in mine:
-                    links.arrive((l, g, "a1", i, by), landed[i], peer(first, -by))
-                    if forward[i] == by:
-                        links.send((l, g, "b1", i), landed[i], landed[i], peer(first, by))
-        elif s == PAIR:
-            landed = spot(step(own[0], PAIR), own[1])
-            part = line(l, g, own[1], None)
-            for i in mine:
-                local[l, g, i].wait()
-                links.arrive((l, g, "b1", i), landed[i], peer(first, -forward[i]))
-                for by in BOTH:
-                    links.send((l, g, "a2", i, by), part[i], part[i], peer(then, by))
-        elif s == 3:
-            for by in BOTH:
-                at2 = step(own[1], -by)
-                whole, half = line(l, g, at2, None), line(l, g, at2, (1 - by) // PAIR)
-                for i in mine:
-                    links.arrive((l, g, "a2", i, by), whole[i], peer(then, -by))
-                    links.send((l, g, "a3", i, by), half[i], half[i], peer(then, by))
-        else:
-            at2 = step(own[1], PAIR)
-            for by in BOTH:
-                half = line(l, g, at2, (1 - by) // PAIR)
-                for i in mine:
-                    links.arrive((l, g, "a3", i, by), half[i], peer(then, -by))
-
-    stages = {"p1": p1, "p2": p2, "p3": lambda l, k, s, is_in: p3(l, k, is_in), "ag": ag}
-
-    for kind, *task in order:
-        stages[kind](*task)
-    links.drain()
-
-
-def add_into(dst, src):
-    lead = dst.shape[:-PAIR]
-    if len(lead) == PAIR:
-        @pl.loop(0, lead[0])
-        def _(i):
-            for j in range(lead[1]):
-                dst[i, j] += src[i, j]
-    elif len(lead) == 1:
-        @pl.loop(0, lead[0])
-        def _(i):
-            dst[i] += src[i]
-    else:
-        dst[ALL] += src[ALL]
-
-
-def reduce_order(widths, rows, rows_b, starts):
-    rate = 11650.0
-    tasks = []
-    for l in range(PAIR):
-        for is_in in PARTS:
-            for k, (color, by) in enumerate(FLOWS):
-                axes = color + FLOW_AXES[color]
-                full = 16 * (rows * widths[k] if is_in else rows_b * LANE) / rate
-                chain = [("p1", l, k, s, is_in) for s in range(SIDE)] + [("p2", l, k, s, is_in) for s in (1, PAIR, 3)] + [("p3", l, k, 0, is_in)]
-                sends = [[((axes[0], by), full)]] * 3 + [[((axes[1], by), full / SIDE)]] * 3
-                sends += [[((axes[PAIR], o), full / 16) for o in (1, -1, 1)], []]
-                for i, task in enumerate(chain):
-                    needs = [(chain[i - 1], j) for j in range(len(sends[i - 1]))] if i else []
-                    tasks.append((task, (l, i - ROW), starts[is_in][l] if i == 0 else 0.0, needs, [], sends[i]))
-            for g, ((first, then), flows) in enumerate(GROUPS):
-                piece = sum(rows * widths[k] if is_in else rows_b * LANE for k in flows) / rate
-                for s, (axis, n) in enumerate(((first, 1), (first, 0.5), (then, SIDE), (then, PAIR), (None, 0))):
-                    needs = [(("ag", l, g, s - 1, is_in), j) for j in (0, 1)] if s else []
-                    after = [] if s else [("p3", l, k, 0, is_in) for k in flows]
-                    sends = [((axis, by), piece * n) for by in BOTH] if axis else []
-                    tasks.append((("ag", l, g, s, is_in), (l, s - 5), 0.0, needs, after, sends))
-    return plan(tasks)
-
-
-def reduce_gradients(ga, gb, widths=(384, 384, WIDE, WIDE, WIDE, WIDE), starts=None):
-    any_space = pl.BlockSpec(memory_space=pl.ANY)
-    rows = ga[0].shape[PAIR]
-    rows_b = gb[0].shape[3]
-    cols = SIDE * sum(widths)
-    f32 = jnp.float32
-    wx, wz, wy = widths[0], widths[PAIR], widths[SIDE]
-
-    def buffers(slots, whole):
-        a = {"x": (SIDE, rows, SIDE * wx), "y": (SIDE, rows, SIDE * wy), "z": (SIDE, SIDE, rows, wz)}
-        b = {"x": (rows, SIDE * wx), "y": (SIDE, rows, wy), "z": (SIDE, rows, wz)}
-        c = {"x": (rows, wx), "y": (rows, wy), "z": (rows, wz)}
-        flat = ((SIDE, SIDE), (SIDE,), ())[whole]
-        per = (a, b, c)[whole]
-        return [pltpu.VMEM((PAIR, PAIR, slots, *per[color]), f32) for color in "xyz"] + [
-            pltpu.VMEM((PAIR, 6, slots, *flat, rows_b, LANE), f32)]
-
-    oa = jax.ShapeDtypeStruct((SIDE, rows, cols), f32)
-    ob = jax.ShapeDtypeStruct((SIDE, SIDE, rows_b, 768), f32)
-    outs = pl.pallas_call(
-        functools.partial(reduce_kernel, widths, reduce_order(widths, rows, rows_b, starts or {True: (0, 40), False: (0, 60)})),
-        out_shape=(oa, oa, ob, ob),
-        in_specs=[any_space] * SIDE,
-        out_specs=[any_space] * SIDE,
-        scratch_shapes=[
-            *buffers(PAIR, 0), *buffers(3, 0), *buffers(3, 1), *buffers(3, PAIR),
-            pltpu.VMEM((PAIR, rows, sum(widths)), f32), pltpu.VMEM((PAIR, rows_b, 768), f32),
-            pltpu.SemaphoreType.DMA((400,)), pltpu.SemaphoreType.DMA((400,)),
-            pltpu.SemaphoreType.DMA((PAIR, 6, PAIR, 3)), pltpu.SemaphoreType.DMA((PAIR, PAIR, SIDE)),
-        ],
-        compiler_params=pltpu.CompilerParams(collective_id=1, has_side_effects=True, vmem_limit_bytes=60 << 20),
-        name="reduce_gradients",
-    )(*ga, *gb)
-    return outs[:PAIR], outs[PAIR:]
 
 
 BF, F32 = jnp.bfloat16, jnp.float32
@@ -814,11 +536,11 @@
     settle()
     for l in range(PAIR):
         for b in range(SIDE):
-            links.arrive(("ht", l, b), (ht_a, ht_b)[l].at[b, :, pl.ds(seq, seq)], twin)
-            links.arrive(("mt", l, b), (mt_a, mt_b)[l].at[b, :, pl.ds(seq, seq)], twin)
-        links.arrive(("y", l), (yp_a, yp_b)[l].at[pl.ds(seq, seq)], twin)
-        links.arrive(("z", l), (z_a, z_b)[l].at[pl.ds(seq, seq)], twin)
-        links.arrive(("sc", l), sc_out.at[l, 1], twin)
+            links.arrive(("ht", l, b), (ht_a, ht_b)[l].at[b, :, pl.ds(seq, seq)])
+            links.arrive(("mt", l, b), (mt_a, mt_b)[l].at[b, :, pl.ds(seq, seq)])
+        links.arrive(("y", l), (yp_a, yp_b)[l].at[pl.ds(seq, seq)])
+        links.arrive(("z", l), (z_a, z_b)[l].at[pl.ds(seq, seq)])
+        links.arrive(("sc", l), sc_out.at[l, 1])
 
 
 def run_layers(x, dy, gain, cos, sin, turn, weights):
@@ -849,6 +571,344 @@
     )(x, dy, gain, cos, sin, turn, *weights)
 
 
+NEXT_AXES = {"x": "yz", "y": "zx", "z": "xy"}
+IN_CHAINS = [("x", 1)] * 3 + [("x", -1)] * 3 + [("z", 1)] * PAIR + [("z", -1)] * PAIR + [("y", 1)] * PAIR + [("y", -1)] * PAIR
+OUT_CHAINS = [("x", 1), ("x", -1), ("z", 1), ("z", -1), ("y", 1), ("y", -1)]
+CHAINS = [(color, by, True, i) for i, (color, by) in enumerate(IN_CHAINS)] + [(color, by, False, i) for i, (color, by) in enumerate(OUT_CHAINS)]
+GROUPS = [("yz", True, 0, 3, 1), ("yz", True, 3, 3, -1), ("yz", True, 6, PAIR, 1), ("zy", True, ROW, PAIR, -1), ("zy", True, 10, SIDE, 1),
+          ("yz", False, 0, 3, -1), ("zy", False, 3, 3, -1)]
+
+
+def reduce_order(rows, rows_b, starts):
+    rate = 11650.0
+    tasks = []
+    for l in range(PAIR):
+        for b in range(SIDE):
+            tasks.append((("rows", l, b), (9 * l, -9, b), 0.0, [], [], [], 0.9))
+        for c, (color, by, is_in, i) in enumerate(CHAINS):
+            axes = color + NEXT_AXES[color]
+            full = 16 * LANE * (rows if is_in else rows_b) / rate
+            chain = [("p1", l, c, s) for s in range(SIDE)] + [("p2", l, c, s) for s in (1, PAIR, 3)] + [("p3", l, c)]
+            sends = [[((axes[0], by), full)]] * 3 + [[((axes[1], by), full / SIDE)]] * 3
+            sends += [[((axes[PAIR], o), full / 16) for o in (1, -1, 1)], []]
+            turn = sum(e[:PAIR] == (color, by) for e in IN_CHAINS[:i]) if is_in else 3
+            if is_in:
+                before = [("cols", l, c)]
+                tasks.append((before[0], (9 * l, -9, turn), 0.0, [], [], [], 0.7))
+            else:
+                before = [("rows", l, b) for b in range(SIDE)]
+            for j, task in enumerate(chain):
+                needs = [(chain[j - 1], n) for n in range(len(sends[j - 1]))] if j else []
+                start = starts[0][l] + starts[1][l] * turn if j == 0 else 0.0
+                tasks.append((task, (l, j - ROW if j else -10, 0), start, needs, [] if j else before, sends[j], 0.3))
+        for g, ((first, then), is_in, at, n, way) in enumerate(GROUPS):
+            piece = n * LANE * (rows if is_in else rows_b) / rate
+            members = [c for c, e in enumerate(CHAINS) if e[PAIR] == is_in and at <= e[3] < at + n]
+            for s in range(5):
+                needs = []
+                if s:
+                    needs = [(("ag", l, g, s - 1), k) for k in ((0,) if s == PAIR else (0, 1))]
+                sends = ([((first, by), piece) for by in BOTH], [((first, way), piece)], [((then, by), SIDE * piece) for by in BOTH],
+                         [((then, by), PAIR * piece) for by in BOTH], [])[s]
+                after = [] if s else [("p3", l, c) for c in members]
+                tasks.append((("ag", l, g, s), (l, s - 5, 0), 0.0, needs, after, sends, 0.3))
+    return plan(tasks)
+
+
+def reduce_kernel(order, *refs):
+    ht, z, mt, yp, sc = refs[0:PAIR], refs[PAIR:SIDE], refs[SIDE:6], refs[6:ROW], refs[ROW]
+    oa, ob, ga, gb = refs[9], refs[10], refs[11:13], refs[13:15]
+    (wx, wy, wz, wb, rx, ry, rz, rb, sx, sy, sz, sb, tx, ty, tz, tb, fa, fb,
+     hbuf, ybuf, scbuf, zbuf, mbuf, cols_out, rows_out, ssem, rsem, lsem, osem, isem, zsem, msem, gsem, bsem) = refs[15:]
+    x, y, zc, core = chip_position()
+    place = {"x": x, "y": y, "z": zc}
+    work, ring1, ring2 = {"x": wx, "y": wy, "z": wz}, {"x": rx, "y": ry, "z": rz}, {"x": sx, "y": sy, "z": sz}
+    last = {"x": tx, "y": ty, "z": tz}
+    firsts = {color: [e[0] for e in IN_CHAINS].index(color) for color in "xyz"}
+    counts = {color: sum(e[0] == color for e in IN_CHAINS) for color in "xyz"}
+    quarter = z[0].shape[1] // SIDE
+    rows_b = gb[0].shape[3]
+
+    spots = {(axis, o): step(place[axis], o) for axis in "xyz" for o in range(SIDE)}
+
+    def spot(axis, o):
+        return spots[axis, o % SIDE]
+
+    peers = {}
+    for axis in "xyz":
+        for o in range(1, SIDE):
+            moved = {**place, axis: spot(axis, o)}
+            peers[axis, o] = device_at(moved["x"], moved["y"], moved["z"], core)
+
+    def peer(axis, o):
+        return peers[axis, o % SIDE]
+
+    col_order = [task for task in order if task[0] == "cols"]
+    row_order = [task for task in order if task[0] == "rows"]
+    whole = []
+    for l in range(PAIR):
+        for i, (src, dst) in enumerate(((ht[l], hbuf.at[l]), (yp[l], ybuf.at[l]), (sc.at[l], scbuf.at[l]))):
+            copy = pltpu.make_async_copy(src, dst, isem.at[l, i])
+            copy.start()
+            whole.append(copy)
+    pending = {}
+
+    def fetch_cols(n):
+        if n < len(col_order):
+            _, l, c = col_order[n]
+            for q in range(SIDE):
+                copy = pltpu.make_async_copy(z[l].at[:, pl.ds(q * quarter + LANE * c, LANE)], zbuf.at[n % PAIR, :, pl.ds(q * LANE, LANE)], zsem.at[n % PAIR])
+                copy.start()
+
+    def fetch_rows(n):
+        if n < len(row_order):
+            _, l, b = row_order[n]
+            copy = pltpu.make_async_copy(mt[l].at[b], mbuf.at[n % PAIR], msem.at[n % PAIR])
+            copy.start()
+            pending["m", n] = copy
+
+    for n in range(PAIR):
+        fetch_cols(n)
+        fetch_rows(n)
+    announce([peer(axis, by) for axis in "xyz" for by in AROUND])
+    links = Links(ssem, rsem)
+    local = {}
+    for copy in whole:
+        copy.wait()
+
+    def cols(l, c):
+        n = col_order.index(("cols", l, c))
+        slot = n % PAIR
+        pltpu.make_async_copy(zbuf.at[slot], zbuf.at[slot], zsem.at[slot]).wait()
+        if n >= PAIR:
+            settle("g", n - PAIR)
+        total = product(hbuf[l].reshape(-1, hbuf.shape[-1]), zbuf[slot])
+        size = cols_out.shape[3]
+        for i in range(16):
+            cols_out[slot, i // SIDE, i % SIDE] = total[i * size:(i + 1) * size]
+        fetch_cols(n + PAIR)
+        copy = pltpu.make_async_copy(cols_out.at[slot], ga[l].at[c], gsem.at[slot])
+        copy.start()
+        pending["g", n] = copy
+        local["g", l, c] = n
+
+    def rows(l, b):
+        n = row_order.index(("rows", l, b))
+        slot = n % PAIR
+        pending["m", n].wait()
+        if n >= PAIR:
+            settle("b", n - PAIR)
+        total = product(mbuf[slot], ybuf[l])
+        size, spare = total.shape[0] // rows_b, 16 * rows_b - total.shape[0]
+        for i in range(size):
+            rows_out[slot, i // SIDE, i % SIDE] = total[i * rows_b:(i + 1) * rows_b]
+        gain = jnp.sum(scbuf[l, 0] + scbuf[l, 1], axis=0, keepdims=True)
+        at = lax.broadcasted_iota(jnp.int32, (spare, total.shape[1]), 0)
+        rows_out[slot, 3, 3] = jnp.where(at == 0, gain, 0.0)
+        fetch_rows(n + PAIR)
+        copy = pltpu.make_async_copy(rows_out.at[slot], gb[l].at[b], bsem.at[slot])
+        copy.start()
+        pending["b", n] = copy
+
+    def settle(kind, n):
+        if (kind, n) in pending and not local.get((kind, n)):
+            pending[kind, n].wait()
+            local[kind, n] = True
+
+    def block(l, c, b):
+        color, _, is_in, i = CHAINS[c]
+        if is_in:
+            ref = ga[l].at[i]
+            return ref.at[b] if color == "x" else ref.at[:, b] if color == "y" else ref.at[:, :, :, lanes(b * LANE, LANE)]
+        at = pl.ds(i * LANE, LANE)
+        ref = gb[l]
+        return ref.at[b, :, :, :, at] if color == "x" else ref.at[:, b, :, :, at] if color == "y" else ref.at[:, :, b, :, at]
+
+    def second(ref, c, b):
+        color, _, is_in, _ = CHAINS[c]
+        if color == "y":
+            return ref.at[:, :, lanes(b * LANE, LANE)] if is_in else ref.at[:, b]
+        return ref.at[b]
+
+    def third(ref, c, b):
+        color, _, is_in, _ = CHAINS[c]
+        return ref.at[:, lanes(b * LANE, LANE)] if is_in and color == "x" else ref.at[b]
+
+    def buf(table, flat, l, c, slots, slot):
+        color, _, is_in, i = CHAINS[c]
+        ref = table[color] if is_in else flat
+        first = (l * (counts[color] if is_in else len(OUT_CHAINS)) + (i - firsts[color] if is_in else i)) * slots
+        return ref.at[pl.ds(first, slots)] if slot is None else ref.at[first + slot]
+
+    def load(l, c, b, dst, tag):
+        copy = pltpu.make_async_copy(block(l, c, b), dst, lsem.at[l, c, tag])
+        copy.start()
+        local[l, c, tag] = copy
+
+    def p1(l, c, s):
+        color, by, is_in, i = CHAINS[c]
+        r = [buf(ring1, rb, l, c, 3, k) for k in range(3)]
+        w = [buf(work, wb, l, c, PAIR, k) for k in range(PAIR)]
+        if s == 0:
+            if is_in:
+                settle("g", local["g", l, c])
+            else:
+                for b in range(SIDE):
+                    settle("b", row_order.index(("rows", l, b)))
+            links.send((l, c, "p1", 0), block(l, c, spot(color, -by)), r[0], peer(color, by), None, buf(ring1, rb, l, c, 3, None), (l, c, "p1"))
+            load(l, c, spot(color, -PAIR * by), w[1], 0)
+            load(l, c, spot(color, -3 * by), w[0], 1)
+            return
+        mine = (None, w[1], w[0], r[0])[s]
+        links.arrive((l, c, "p1", s - 1), r[s - 1])
+        local[l, c, s - 1].wait()
+        add_into(mine, r[s - 1])
+        if s < 3:
+            links.send((l, c, "p1", s), mine, r[s], peer(color, by), None, buf(ring1, rb, l, c, 3, None), (l, c, "p1"))
+            if s == 1:
+                load(l, c, spot(color, 0), r[0], PAIR)
+        else:
+            p2(l, c, 0)
+
+    def p2(l, c, s):
+        color, by, _, _ = CHAINS[c]
+        axis, beyond = NEXT_AXES[color]
+        total = buf(ring1, rb, l, c, 3, 0)
+        r = [buf(ring2, sb, l, c, 3, k) for k in range(3)]
+        mine = second(total, c, spot(axis, -by * (1 + s)))
+        if s:
+            links.arrive((l, c, "p2", s - 1), r[s - 1])
+            add_into(mine, r[s - 1])
+        if s < 3:
+            links.send((l, c, "p2", s), mine, r[s], peer(axis, by), None, buf(ring2, sb, l, c, 3, None), (l, c, "p2"))
+        else:
+            for slot, o in enumerate(AROUND):
+                links.send((l, c, "p3", o), third(mine, c, spot(beyond, o)), buf(last, tb, l, c, 3, slot), peer(beyond, o), (l, c, "p3", 1), buf(last, tb, l, c, 3, None), (l, c, "p3"))
+
+    def p3(l, c):
+        color, _, is_in, i = CHAINS[c]
+        axis, beyond = NEXT_AXES[color]
+        t = [buf(last, tb, l, c, 3, k) for k in range(3)]
+        links.arrive((l, c, "p3", 1), buf(last, tb, l, c, 3, None))
+        mine = third(second(buf(ring1, rb, l, c, 3, 0), c, place[axis]), c, place[beyond])
+        final = (fa if is_in else fb).at[l, :, pl.ds(LANE * i, LANE)]
+        final[ALL] = (mine[ALL] + t[0][ALL]) + (t[1][ALL] + t[PAIR][ALL])
+
+    def area(l, g, p, q):
+        _, is_in, at, n, _ = GROUPS[g]
+        if is_in:
+            return oa.at[1 - l, p, :, lanes(q * quarter + LANE * at, LANE * n)]
+        return ob.at[1 - l, p, q, :, pl.ds(LANE * at, LANE * n)]
+
+    def line(l, g, at2, part):
+        (first, _), is_in, _, _, _ = GROUPS[g]
+        along = range(SIDE) if part is None else range(PAIR * part, PAIR * part + PAIR)
+        span = pl.ds(along[0], len(along))
+        if first == "y":
+            return [area(l, g, span, at2)]
+        return [area(l, g, at2, k) for k in along] if is_in else [area(l, g, at2, span)]
+
+    def ag(l, g, s):
+        (first, then), is_in, at, n, way = GROUPS[g]
+
+        def piece(o):
+            i, j = spot(first, o), spot(then, 0)
+            return area(l, g, i, j) if first == "y" else area(l, g, j, i)
+
+        if s == 0:
+            src, dst = (fa if is_in else fb).at[l, :, pl.ds(LANE * at, LANE * n)], piece(0)
+            for by in BOTH:
+                links.send((l, g, "a1", by), src, dst, peer(first, by))
+            copy = pltpu.make_async_copy(src, dst, osem.at[l, g])
+            copy.start()
+            local["own", l, g] = copy
+        elif s == 1:
+            for by in BOTH:
+                landed = piece(-by)
+                links.arrive((l, g, "a1", by), landed)
+                if way == by:
+                    links.send((l, g, "b1"), landed, landed, peer(first, by))
+        elif s == PAIR:
+            local["own", l, g].wait()
+            links.arrive((l, g, "b1"), piece(PAIR))
+            for k, part in enumerate(line(l, g, spot(then, 0), None)):
+                for by in BOTH:
+                    links.send((l, g, "a2", k, by), part, part, peer(then, by))
+        elif s == 3:
+            for by in BOTH:
+                at2 = spot(then, -by)
+                for k, part in enumerate(line(l, g, at2, None)):
+                    links.arrive((l, g, "a2", k, by), part)
+                for k, part in enumerate(line(l, g, at2, (1 - by) // PAIR)):
+                    links.send((l, g, "a3", k, by), part, part, peer(then, by))
+        else:
+            for by in BOTH:
+                for k, part in enumerate(line(l, g, spot(then, PAIR), (1 - by) // PAIR)):
+                    links.arrive((l, g, "a3", k, by), part)
+
+    stages = {"cols": cols, "rows": rows, "p1": p1, "p2": p2, "p3": p3, "ag": ag}
+    for kind, *task in order:
+        stages[kind](*task)
+    for n in range(len(col_order)):
+        if n >= len(col_order) - PAIR:
+            settle("g", n)
+    for n in range(len(row_order)):
+        if n >= len(row_order) - PAIR:
+            settle("b", n)
+    links.drain()
+
+
+def add_into(dst, src):
+    lead = dst.shape[:-PAIR]
+    if len(lead) == PAIR:
+        @pl.loop(0, lead[0])
+        def _(i):
+            for j in range(lead[1]):
+                dst[i, j] += src[i, j]
+    elif len(lead) == 1:
+        @pl.loop(0, lead[0])
+        def _(i):
+            dst[i] += src[i]
+    else:
+        dst[ALL] += src[ALL]
+
+
+def reduce_gradients(h_rows, z_cols, m_rows, y_cols, scale_parts, starts=((0.0, 50.0), (0.0, 15.0))):
+    hbm = pl.BlockSpec(memory_space=pltpu.HBM)
+    rows, rows_out, dim, wide = h_rows[0].shape[1], m_rows[0].shape[1], y_cols[0].shape[1], z_cols[0].shape[1]
+    pair = y_cols[0].shape[0]
+    part, part_b = rows // SIDE, (rows_out + BAND) // 16
+    n_in, n_out = len(IN_CHAINS), len(OUT_CHAINS)
+
+    def buffers(slots, depth):
+        shapes = {"x": ((SIDE, part, STRIP), (part, STRIP), (part, LANE)), "y": ((SIDE, part, STRIP), (SIDE, part, LANE), (part, LANE)),
+                  "z": ((SIDE, SIDE, part, LANE), (SIDE, part, LANE), (part, LANE))}
+        flat = ((SIDE, SIDE), (SIDE,), ())[depth]
+        counts = {color: sum(e[0] == color for e in IN_CHAINS) for color in "xyz"}
+        return [pltpu.VMEM((PAIR * counts[color] * slots, *shapes[color][depth]), F32) for color in "xyz"] + [
+            pltpu.VMEM((PAIR * n_out * slots, *flat, part_b, LANE), F32)]
+
+    out = lambda *shape: jax.ShapeDtypeStruct(shape, F32)
+    sem = pltpu.SemaphoreType.DMA
+    in_sums, out_sums, *_ = pl.pallas_call(
+        functools.partial(reduce_kernel, reduce_order(part, part_b, starts)),
+        out_shape=(out(PAIR, SIDE, part, wide), out(PAIR, SIDE, SIDE, part_b, dim), *[out(n_in, SIDE, SIDE, part, STRIP)] * PAIR, *[out(SIDE, SIDE, SIDE, part_b, dim)] * PAIR),
+        in_specs=[hbm] * 9,
+        out_specs=[hbm] * 6,
+        scratch_shapes=[
+            *buffers(PAIR, 0), *buffers(3, 0), *buffers(3, 1), *buffers(3, PAIR),
+            pltpu.VMEM((PAIR, part, LANE * n_in), F32), pltpu.VMEM((PAIR, part_b, dim), F32),
+            pltpu.VMEM((PAIR, *h_rows[0].shape), BF), pltpu.VMEM((PAIR, pair, dim), BF), pltpu.VMEM((PAIR, *scale_parts.shape[1:]), F32),
+            pltpu.VMEM((PAIR, pair, STRIP), BF), pltpu.VMEM((PAIR, rows_out, pair), BF),
+            pltpu.VMEM((PAIR, SIDE, SIDE, part, STRIP), F32), pltpu.VMEM((PAIR, SIDE, SIDE, part_b, dim), F32),
+            sem((STRIP,)), sem((STRIP,)), sem((PAIR, n_in + n_out, 3)), sem((PAIR, len(GROUPS))), sem((PAIR, 3)), sem((PAIR,)), sem((PAIR,)), sem((PAIR,)), sem((PAIR,)),
+        ],
+        compiler_params=pltpu.CompilerParams(collective_id=1, has_side_effects=True, vmem_limit_bytes=67043328),
+        name="reduce_gradients",
+    )(*h_rows, *z_cols, *m_rows, *y_cols, scale_parts)
+    return in_sums, out_sums
+
+
 def rotary_tables(seq_len, head_dim):
     half_dim = head_dim // PAIR
     inv_freq = 10000.0 ** (-(jnp.arange(half_dim, dtype=jnp.float32) * 2.0 / head_dim))
@@ -880,21 +940,12 @@
         turn = jnp.where(low & (down == BAND), -1.0, jnp.where(~low & (down == -BAND), 1.0, 0.0)).astype(jnp.bfloat16)
         weights = [w.reshape(-1, w.shape[-1]) for w in gathered]
         hidden, grad_hidden, *rest = run_layers(x_in[0], grad_y[0], jnp.pad(scale_full, ((0, ROW - n_layers), (0, 0))), cos_tab, sin_tab, turn, weights)
-        h_rows, z_cols, m_rows, y_cols, scale_parts = rest[0:PAIR], rest[PAIR:SIDE], rest[SIDE:6], rest[6:ROW], rest[ROW]
-        in_parts, out_parts = [], []
-        for l in range(n_layers):
-            part_in = jnp.dot(h_rows[l].reshape(SIDE * rows, -1), z_cols[l], preferred_element_type=jnp.float32)
-            in_parts.append(part_in.reshape(SIDE, SIDE, rows // SIDE, proj_dim + LANE))
-            part_out = jnp.dot(m_rows[l].reshape(SIDE * rows_out, -1), y_cols[l], preferred_element_type=jnp.float32).reshape(SIDE, rows_out, model_dim)
-            part_out = jnp.pad(part_out, ((0, 0), (0, BAND), (0, 0)))
-            part_scale = jnp.broadcast_to(scale_parts[l].sum((0, 1)), (SIDE, 1, model_dim))
-            part_out = lax.dynamic_update_slice(part_out, part_scale, (0, rows_out, 0))
-            out_parts.append(part_out.reshape(SIDE, SIDE, SIDE, (rows_out + BAND) // 16, model_dim))
-        in_sums, out_sums = reduce_gradients(in_parts[::-1], out_parts[::-1])
-        in_grads = jnp.stack([g.reshape(rows, -1)[:, :proj_dim] for g in in_sums[::-1]])
-        out_rows = [g.reshape(-1, model_dim) for g in out_sums[::-1]]
-        out_grads = jnp.stack([g[:rows_out] for g in out_rows])
-        scale_grads = jnp.stack([lax.dynamic_slice(g[rows_out], (lax.axis_index("fsdp") * rows,), (rows,)) for g in out_rows])
+        operands = [rest[PAIR * i:PAIR * i + PAIR][::-1] for i in range(SIDE)]
+        in_sums, out_sums = reduce_gradients(*operands, rest[ROW][::-1])
+        in_grads = in_sums.reshape(n_layers, rows, -1)[:, :, :proj_dim]
+        out_rows = out_sums.reshape(n_layers, -1, model_dim)
+        scale_grads = lax.dynamic_slice(out_rows[:, rows_out], (0, lax.axis_index("fsdp") * rows), (n_layers, rows))
+        out_grads = out_rows[:, :rows_out]
         return hidden[None], grad_hidden[None], scale_grads, in_grads, out_grads
 
     return jax.shard_map(

time: 426 us -> 399 us (0.937)
  matrix products: 22.7 us -> 0 us
  Pallas kernels: 360 us -> 366 us
  other arithmetic: 6.73 us -> 1.59 us
  local copies, waits for them, and re-layouts: 35.1 us -> 30.4 us
    dot_general x4 -> x0, matrix products: 22.7 us -> none  [the longest x2 17.6 us: device_step(): jnp.dot(h_rows[l].reshape(SIDE * rows, -1), z_cols[l], preferred_element_...]
    slice x2 -> x3, local copies, waits for them, and re-layouts: 0.74 us -> 8.09 us  [the longest x1 5.34 us: device_step(): in_grads = in_sums.reshape(n_layers, rows, -1)[:, :, :proj_dim]]
    pad x2 -> x0, local copies, waits for them, and re-layouts: 6.68 us -> none  [device_step(): part_out = jnp.pad(part_out, ((0, 0), (0, BAND), (0, 0)))]
    pallas_call x1, Pallas kernels: 196 us -> 201 us  [reduce_gradients(): pl.pallas_call(functools.partial(reduce_kernel, reduce_order(part, part_b...]
    another operation x3 -> x0, other arithmetic: 5.12 us -> none  [the longest x1 2.76 us: device_step(): jnp.stack([g.reshape(rows, -1)[:, :proj_dim] for g in in_sums[::-1]])]
    unnamed x34 -> x20, local copies, waits for them, and re-layouts: 19.9 us -> 17.7 us
where the time goes in v2:
time: 399 us
  Pallas kernels  366 us (92%)
  local copies, waits for them, and re-layouts  30.4 us (8%)
    pallas_call x1, Pallas kernels, reduce_gradients(): pl.pallas_call(functools.partial(reduce_kernel, reduce_order(part, part_b...  201 us
    pallas_call x1, Pallas kernels, run_layers(): pl.pallas_call(layers_kernel, out_shape=(out(seq, dim), out(seq, dim), *[...  89.7 us
    pallas_call x1, Pallas kernels, gather_weights(): pl.pallas_call(functools.partial(gather_kernel, gather_order(*w_in.shape[...  75.2 us
    unnamed x20, local copies, waits for them, and re-layouts  17.7 us

profile of v2, /device:TPU:0, one launch (start us, length us, event | category | flops | bytes accessed | tf_op | source)
XLA Modules:
  0.0 398.7 jit_solution(2977611141810251613)
XLA Ops:
  0.6 0.7 pad_convert_fusion.sc_in
  1.3 0.0 copy-start.4
  1.3 1.8 copy-done.4
  3.1 0.0 copy-start.5
  3.1 1.4 copy-done.5
  4.4 75.2 %gather_weights.1 = (f32[8,8,128]{2,1,0:T(8,128)S(1)}, bf16[4,2,96,7040]{3,2,1,0:T(8,128)(2,1)S(1)}, bf16[4,2,480,768]{3,2,1,0:T(8,128)(2,1)S(1)}, bf16[4,2,96,7...) custom-call(f32[8,128]{1,0:T(8,128)S(1)} %pad_convert_fusion.sc_in, bf16[2,96,7040]{2,1,0:T(8,128)(2,1)S(1)} %copy-done.4, ...), custom_call_target="tpu_custom_call" | custom-call | tf_op jit(solution)/shard_map/gather_weights/pallas_call | solution.py:262
  79.7 0.0 copy-start
  79.7 4.1 %copy-done = bf16[4,2,96,7040]{3,2,1,0:T(8,128)(2,1)} copy-done((bf16[4,2,96,7040]{3,2,1,0:T(8,128)(2,1)}, bf16[4,2,96,7040]{3,2,1,0:T(8,128)(2,1)S(1)}, u32[]{:S(2)}) %copy-start) | copy-done | bytes 10813464
  83.8 0.0 copy-start.1
  83.8 3.9 copy-done.1
  87.7 0.0 copy-start.2
  87.7 2.5 copy-done.2
  90.2 2.6 copy-done.3
  92.8 0.1 reshape.104
  92.9 0.6 pad.12.gain_ref
  93.5 0.2 fusion.4
  93.7 0.8 copy.12.cos_ref
  94.6 0.8 copy.13.sin_ref
  95.4 0.7 select_convert_fusion.turn_ref
  96.1 89.7 %run_layers.1 = (bf16[256,768]{1,0:T(8,128)(2,1)}, bf16[256,768]{1,0:T(8,128)(2,1)}, bf16[4,96,512]{2,1,0:T(8,128)(2,1)}, bf16[4,96,512]{2,1,0:T(8,128)(2,1)}, b...) custom-call(bf16[256,768]{1,0:T(8,128)(2,1)} %bitcast.24, ...), custom_call_target="tpu_custom_call" | custom-call | tf_op jit(solution)/shard_map/run_layers/pallas_call | solution.py:554
  185.8 1.5 rev.3.refs_8_
  187.4 201.1 %reduce_gradients.1 = (f32[2,4,24,7168]{3,2,1,0:T(8,128)}, f32[2,4,4,32,768]{4,3,2,1,0:T(8,128)}, f32[14,4,4,24,512]{4,3,2,1,0:T(8,128)}, f32[14,4,4,24,512]{4,3...) custom-call(bf16[4,96,512]{2,1,0:T(8,128)(2,1)} %get-tuple-element.30.refs_0_, ...), custom_call_target="tpu_custom_call" | custom-call | tf_op jit(solution)/shard_map/reduce_gradients/pallas_call | solution.py:893
  388.4 0.0 copy-start.6
  388.4 1.0 slice.16
  389.4 0.6 constant_dynamic-slice_fusion
  390.0 5.3 %slice.17 = f32[2,96,7040]{2,1,0:T(8,128)} slice(f32[2,96,7168]{2,1,0:T(8,128)} %bitcast.19), slice={[0:2], [0:96], [0:7040]} | slice | bytes 10813440 | tf_op jit(solution)/shard_map/slice | solution.py:945
  395.4 0.0 copy-done.6
  395.4 1.8 slice.18
  397.2 0.0 copy-done.8
  397.2 0.7 copy.16
  397.9 0.0 copy-done.7
  397.9 0.7 copy.17
  (9 shorter events, 0.1 us)
Async XLA Ops:
  1.3 1.8 copy-start.4
  3.1 1.4 copy-start.5
  79.7 4.1 %copy-start = (bf16[4,2,96,7040]{3,2,1,0:T(8,128)(2,1)}, bf16[4,2,96,7040]{3,2,1,0:T(8,128)(2,1)S(1)}, u32[]{:S(2)}) copy-start(bf16[4,2,96,7040]{3,2,1,0:T(8,128)(2,1)S(1)} %get-tuple-element.24) | copy-start | bytes 32440324
  83.8 3.9 copy-start.1
  87.7 2.5 copy-start.2
  90.2 2.6 copy-start.3
  388.4 6.9 %copy-start.6 = (f32[2,4,4,32,768]{4,3,2,1,0:T(8,128)S(1)}, f32[2,4,4,32,768]{4,3,2,1,0:T(8,128)}, u32[]{:S(2)}) copy-start(f32[2,4,4,32,768]{4,3,2,1,0:T(8,128)} %get-tuple-element.39) | copy-start | bytes 9437188
  390.0 7.1 %copy-start.8 = (bf16[256,768]{1,0:T(8,128)(2,1)S(1)}, bf16[256,768]{1,0:T(8,128)(2,1)}, u32[]{:S(2)}) copy-start(bf16[256,768]{1,0:T(8,128)(2,1)} %get-tuple-element.28) | copy-start | bytes 1179652
  395.4 2.5 copy-start.7

commit v3 on v2

--- a/solution.py
+++ b/solution.py
@@ -83,7 +83,7 @@
     return order
 
 
-def gather_order(rows_i, cols_i, rows_o, cols_o, starts):
+def forward_order(rows_i, cols_i, rows_o, cols_o, starts):
     rate = 23300.0
     tasks = []
     for m in range(SIDE):
@@ -111,16 +111,23 @@
             last = [("close", m, color, off) for color in "yz"]
             if is_in:
                 last.append(("far", m, "x") if off == PAIR else ("relay", m, "x", -off))
-            tasks.append((("hand", m, off), m, 0.0, [], last, [], 0.2))
+            tasks.append((("hand", m, off), m, 0.0, [], last, [("chip", (rows_i * cols_i if is_in else rows_o * cols_o) / 150000.0)], 0.2))
+    before = []
+    for l in range(PAIR):
+        work = [(("norm", l), [], 0.8)] + [(("project", l, i), [PAIR * l], 1.4) for i in range(SIDE)]
+        work += [(("attend", l), [], 4.0), (("mlp", l), [], 2.2), (("put", l), [PAIR * l + 1], 2.0)]
+        for name, mats, cost in work:
+            needs = [(("hand", m, off), 0) for m in mats for off in (-1, 1, PAIR)]
+            tasks.append((name, 9, 0.0, needs, before, [], cost))
+            before = [name]
     return plan(tasks)
 
 
-def gather_kernel(order, sc_in, wi_in, wo_in, sc_out, wi_a, wo_a, wi_b, wo_b, own_i, own_o, ssem, rsem, lsem):
-    x, y, z, core = chip_position()
-    here = device_at(x, y, z, core)
+def gather_stages(links, position, shard_i, shard_o, wi, wo, lsem):
+    x, y, z, core = position
     twin = device_at(x, y, z, 1 - core)
-    rows_i, cols_i = wi_in.shape[1:]
-    rows_o, cols_o = wo_in.shape[1:]
+    rows_i, cols_i = shard_i.shape[1:]
+    rows_o, cols_o = shard_o.shape[1:]
     quarter_i, quarter_o = rows_i // SIDE, rows_o // SIDE
     third_i = cols_i // LANE * SIDE // 9 // PAIR * WIDE
     half_o = cols_o // PAIR
@@ -141,15 +148,10 @@
     def peer(axis, o):
         return table[axis, o % SIDE]
 
-    peers = [peer(axis, by) for axis in "xyz" for by in BOTH]
-    others = [(lax.axis_index("dp"), lax.rem(lax.axis_index("fsdp") + k, ROW)) for k in range(1, ROW)]
-    announce(others + peers[PAIR:])
-    links = Links(ssem, rsem)
-
     mats = []
-    for layer, (wi, wo) in enumerate(((wi_a, wo_a), (wi_b, wo_b))):
-        mats.append((wi_in.at[layer], wi, own_i.at[layer], True))
-        mats.append((wo_in.at[layer], wo, own_o.at[layer], False))
+    for l in range(PAIR):
+        mats.append((shard_i.at[l], wi.at[l], rows_i, True))
+        mats.append((shard_o.at[l], wo.at[l], rows_o, False))
 
     def region(is_in, color, q):
         if is_in:
@@ -165,115 +167,81 @@
         start = q * quarter_o
         return ((start, quarter_o), cols), ((start, cut_o), cols), ((start + cut_o, quarter_o - cut_o), cols)
 
-    def at(ref, lead, area):
+    def at(m, xb, area):
         (r, nr), (c, nc) = area
-        if not isinstance(r, int):
-            r = pl.multiple_of(r, ROW)
-        return ref.at[(*lead, pl.ds(r, nr), pl.ds(c, nc))]
+        _, out, size, _ = mats[m]
+        return out.at[pl.ds(pl.multiple_of((PAIR * xb + core) * size + r, ROW), nr), pl.ds(c, nc)]
+
+    def block(m, xb, index):
+        _, out, size, _ = mats[m]
+        return out.at[pl.ds(pl.multiple_of((PAIR * xb + index) * size, BAND), size)]
 
     def colors(m):
         return "yzx" if mats[m][3] else "yz"
 
     def reach(m, color):
-        src, out, _, is_in = mats[m]
+        src, _, _, is_in = mats[m]
         area = region(is_in, color, place[color])[0]
         for by in BOTH:
-            links.send((m, "x1", color, by), at(src, (), area), at(out, (x, core), area), peer("x", by))
+            links.send((m, "x1", color, by), src.at[pl.ds(pl.multiple_of(area[0][0], ROW), area[0][1]), pl.ds(*area[1])], at(m, x, area), peer("x", by))
 
     def launch(m, color, off):
-        _, out, _, is_in = mats[m]
-        block = at(out, (spot("x", off), core), region(is_in, color, place[color])[0])
+        is_in = mats[m][3]
+        moved = at(m, spot("x", off), region(is_in, color, place[color])[0])
         for by in BOTH:
-            links.send((m, "p1", color, off, by), block, block, peer(color, by))
+            links.send((m, "p1", color, off, by), moved, moved, peer(color, by))
 
     def relay(m, color, by):
-        _, out, _, is_in = mats[m]
+        is_in = mats[m][3]
         xb = spot("x", -by)
         areas = region(is_in, color, place[color])
-        links.arrive((m, "x1", color, by), at(out, (xb, core), areas[0]))
-        part = at(out, (xb, core), areas[1] if by == 1 else areas[PAIR])
+        links.arrive((m, "x1", color, by), at(m, xb, areas[0]))
+        part = at(m, xb, areas[1] if by == 1 else areas[PAIR])
         links.send((m, "x2", color, by), part, part, peer("x", by))
         if color != "x":
             launch(m, color, -by)
 
     def far(m, color):
-        _, out, _, is_in = mats[m]
+        is_in = mats[m][3]
         areas = region(is_in, color, place[color])
         for by in BOTH:
-            links.arrive((m, "x2", color, by), at(out, (spot("x", PAIR), core), areas[1] if by == 1 else areas[PAIR]))
+            links.arrive((m, "x2", color, by), at(m, spot("x", PAIR), areas[1] if by == 1 else areas[PAIR]))
         if color != "x":
             launch(m, color, PAIR)
 
     def pass_on(m, color, off, by):
-        _, out, _, is_in = mats[m]
+        is_in = mats[m][3]
         xb = spot("x", off)
         areas = region(is_in, color, spot(color, -by))
-        links.arrive((m, "p1", color, off, by), at(out, (xb, core), areas[0]))
-        part = at(out, (xb, core), areas[1] if by == 1 else areas[PAIR])
+        links.arrive((m, "p1", color, off, by), at(m, xb, areas[0]))
+        part = at(m, xb, areas[1] if by == 1 else areas[PAIR])
         links.send((m, "p2", color, off, by), part, part, peer(color, by))
 
     def close(m, color, off):
-        _, out, _, is_in = mats[m]
+        is_in = mats[m][3]
         areas = region(is_in, color, spot(color, PAIR))
         for by in BOTH:
-            links.arrive((m, "p2", color, off, by), at(out, (spot("x", off), core), areas[1] if by == 1 else areas[PAIR]))
+            links.arrive((m, "p2", color, off, by), at(m, spot("x", off), areas[1] if by == 1 else areas[PAIR]))
 
     def hand(m, off):
-        _, out, _, _ = mats[m]
-        links.send((m, "d2d", off), out.at[spot("x", off), core], out.at[spot("x", off), core], twin)
-
-    stages = {"reach": reach, "relay": relay, "far": far, "pass": pass_on, "close": close, "hand": hand}
-
-    loads = []
-    for m, (src, out, own, _) in enumerate(mats):
-        load = pltpu.make_async_copy(src, own, lsem.at[0, m])
-        load.start()
-        loads.append(load)
-    for k, device in enumerate(others):
-        links.send(("sc", k), sc_in, sc_out.at[lax.axis_index("fsdp")], device)
-    for m, (src, out, own, _) in enumerate(mats):
-        links.send((m, "d2d", 0), src, out.at[x, core], twin)
-    stores = []
-    for m, (src, out, own, _) in enumerate(mats):
-        loads[m].wait()
-        store = pltpu.make_async_copy(own, out.at[x, core], lsem.at[1, m])
-        store.start()
-        stores.append(store)
-    own_scale = pltpu.make_async_copy(sc_in, sc_out.at[lax.axis_index("fsdp")], lsem.at[PAIR, 0])
-    own_scale.start()
-    for kind, *task in order:
-        stages[kind](*task)
-    for m, (src, out, own, _) in enumerate(mats):
+        whole = block(m, spot("x", off), core)
+        links.send((m, "d2d", off), whole, whole, twin)
+
+    owns = []
+
+    def begin():
+        for m, (src, _, _, _) in enumerate(mats):
+            copy = pltpu.make_async_copy(src, block(m, x, core), lsem.at[m])
+            copy.start()
+            owns.append(copy)
+            links.send((m, "d2d", 0), src, block(m, x, core), twin)
+
+    def ready(m):
+        owns[m].wait()
         for off in (0, -1, 1, PAIR):
-            xb = spot("x", off)
-            links.arrive((m, "d2d", off), out.at[xb, 1 - core])
-        stores[m].wait()
-    own_scale.wait()
-    for k in range(7):
-        source = lax.rem(lax.axis_index("fsdp") + 7 - k, ROW)
-        links.arrive(("sc", k), sc_out.at[source])
-    links.drain()
-
-
-def gather_weights(scale_tile, w_in, w_out, starts=None, n_copies=320):
-    any_space = pl.BlockSpec(memory_space=pltpu.HBM)
-    wi = jax.ShapeDtypeStruct((SIDE, PAIR, *w_in.shape[1:]), w_in.dtype)
-    wo = jax.ShapeDtypeStruct((SIDE, PAIR, *w_out.shape[1:]), w_out.dtype)
-    return pl.pallas_call(
-        functools.partial(gather_kernel, gather_order(*w_in.shape[1:], *w_out.shape[1:], starts or (0, 0, 0, 0))),
-        out_shape=(jax.ShapeDtypeStruct((ROW, *scale_tile.shape), scale_tile.dtype), wi, wo, wi, wo),
-        in_specs=[any_space] * 3,
-        out_specs=[any_space] * 5,
-        scratch_shapes=[
-            pltpu.VMEM(w_in.shape, w_in.dtype),
-            pltpu.VMEM(w_out.shape, w_out.dtype),
-            pltpu.SemaphoreType.DMA((n_copies,)),
-            pltpu.SemaphoreType.DMA((n_copies,)),
-            pltpu.SemaphoreType.DMA((3, SIDE)),
-        ],
-        compiler_params=pltpu.CompilerParams(collective_id=0, has_side_effects=True, vmem_limit_bytes=12 << 20),
-        name="gather_weights",
-    )(scale_tile, w_in, w_out)
+            links.arrive((m, "d2d", off), block(m, spot("x", off), 1 - core))
+
+    return begin, ready, peer, {"reach": reach, "relay": relay, "far": far, "pass": pass_on, "close": close, "hand": hand}
 
 
 BF, F32 = jnp.bfloat16, jnp.float32
@@ -287,22 +255,25 @@
     return pl.ds(start if isinstance(start, int) else pl.multiple_of(start, LANE), size)
 
 
-def layers_kernel(x_ref, dy_ref, gain_ref, cos_ref, sin_ref, turn_ref, wi_a, wo_a, wi_b, wo_b,
+def layers_kernel(order, sc_ref, wi_ref, wo_ref, x_ref, dy_ref, cos_ref, sin_ref, turn_ref,
                   y_ref, gx_ref, ht_a, ht_b, z_a, z_b, mt_a, mt_b, yp_a, yp_b, sc_out,
                   wi, wo, z, om, h, hid, qr, kts, vts, ksl, scores, dscores, pcat, dscat,
-                  dot_heads, qt, dht, dkv, omt, ht, dyt, sc, load_sems, own_sems, send_sems, recv_sems):
+                  dot_heads, qt, dht, dkv, omt, ht, dyt, sc, gains, gain_ref, load_sems, own_sems, send_sems, recv_sems,
+                  share_send_sems, share_recv_sems):
     seq, dim = x_ref.shape
-    ff = (wi_a.shape[1] - dim - LANE) // PAIR
-    x, y, zc, core = chip_position()
+    ff = (wi.shape[PAIR] - dim - LANE) // PAIR
+    position = chip_position()
+    x, y, zc, core = position
     twin = device_at(x, y, zc, 1 - core)
-    announce([twin])
-    links = Links(send_sems, recv_sems)
+    me = PAIR * x + core
+    links, shared = Links(send_sems, recv_sems), Links(share_send_sems, share_recv_sems)
     stored, used = [], []
-    loads = []
-    for i, (src, dst) in enumerate(((wi_a, wi.at[0]), (wo_a, wo.at[0]), (wi_b, wi.at[1]), (wo_b, wo.at[1]))):
-        copy = pltpu.make_async_copy(src, dst, load_sems.at[i])
-        copy.start()
-        loads.append(copy)
+    begin, ready, peer, stages = gather_stages(links, position, wi_ref, wo_ref, wi, wo, load_sems)
+    others = [(zc * SIDE + y, rem(me + k, ROW)) for k in range(1, ROW)]
+    announce(others + [peer(axis, by) for axis in "yz" for by in BOTH])
+    begin()
+    for k, device in enumerate(others):
+        links.send(("sc", k), sc_ref, gains.at[me], device)
 
     def keep(src, dst):
         copy = pltpu.make_async_copy(src, dst, own_sems.at[len(used)])
@@ -314,12 +285,13 @@
         for copy in stored:
             copy.wait()
         stored.clear()
-        links.drain()
+        shared.drain()
 
     def share(key, src, out, place):
         keep(src, place(out, 0))
-        links.send(key, src, place(out, 1), twin)
-
+        shared.send(key, src, place(out, 1), twin)
+
+    gains[me] = sc_ref[ALL]
     z[:, :, wi.shape[PAIR]:] = jnp.zeros((PAIR, seq, z.shape[PAIR] - wi.shape[PAIR]), BF)
     entry = (x_ref, hid.at[0])
     kts[ALL] = jnp.zeros(kts.shape, BF)
@@ -334,16 +306,17 @@
             var = jnp.mean(v * v, axis=-1, keepdims=True)
             h[l, rows] = (v * lax.rsqrt(var + 1e-6) * gain_ref[l:l + 1]).astype(BF)
 
-    def project(l):
+    def project(l, quarter):
         def part(at, size):
             z[l, :, lanes(at, size)] = product(h[l], wi[l, :, lanes(at, size)]).astype(BF)
 
         n = wi.shape[PAIR] // STRIP
 
-        @pl.loop(0, n)
+        @pl.loop(quarter * n // SIDE, (quarter + 1) * n // SIDE)
         def _(i):
             part(i * STRIP, STRIP)
-        part(n * STRIP, wi.shape[PAIR] - n * STRIP)
+        if quarter == 3:
+            part(n * STRIP, wi.shape[PAIR] - n * STRIP)
 
     def heads(l):
         cos, sin = cos_ref[ALL], sin_ref[ALL]
@@ -510,21 +483,35 @@
             mine = src.at[pl.ds(pl.multiple_of((PAIR * b + core) * size, BAND), size)]
             other = src.at[pl.ds(pl.multiple_of((PAIR * b + 1 - core) * size, BAND), size)]
             keep(mine, out.at[b, :, pl.ds(0, seq)])
-            links.send((name, l, b), other, out.at[b, :, pl.ds(seq, seq)], twin)
-
-    for l in range(PAIR):
-        loads[PAIR * l].wait()
+            shared.send((name, l, b), other, out.at[b, :, pl.ds(seq, seq)], twin)
+
+    def do_norm(l):
+        if l == 0:
+            for k, (_, f) in enumerate(others):
+                links.arrive(("sc", k), gains.at[rem(me + 7 - k, ROW)])
+            gain_ref[ALL] = jnp.sum(gains[ALL], axis=0)
         normalise(l, entry[l])
         settle()
         flip(lambda at: h[l, :, lanes(at, WIDE)], ht, dim)
-        project(l)
-        attend(l)
+
+    def do_project(l, i):
+        if i == 0:
+            ready(PAIR * l)
+            give_rows(l, "ht", ht, (ht_a, ht_b)[l])
+        project(l, i)
+
+    def do_mlp(l):
         mlp(l)
         flip(lambda at: om[:, lanes(at, WIDE)], omt, om.shape[1])
-        loads[PAIR * l + 1].wait()
+        give_rows(l, "mt", omt, (mt_a, mt_b)[l])
+
+    def do_put(l):
+        ready(PAIR * l + 1)
         put_out(l, hid.at[0] if l == 0 else y_ref)
-        give_rows(l, "ht", ht, (ht_a, ht_b)[l])
-        give_rows(l, "mt", omt, (mt_a, mt_b)[l])
+
+    stages.update(norm=do_norm, project=do_project, attend=attend, mlp=do_mlp, put=do_put)
+    for kind, *task in order:
+        stages[kind](*task)
     share(("y", 1), dy_ref, yp_b, lambda out, far: out.at[pl.ds(far * seq, seq)])
     for l, dy, dst in ((1, dy_ref, hid.at[1]), (0, hid.at[1], gx_ref)):
         if l == 0:
@@ -532,31 +519,33 @@
         backward(l, dy)
         share(("z", l), z.at[l], (z_a, z_b)[l], lambda out, far: out.at[pl.ds(far * seq, seq)])
         backward_rows(l, dy, dst)
-        share(("sc", l), sc.at[l], sc_out.at[l], lambda out, far: out.at[far])
+        share(("scale", l), sc.at[l], sc_out.at[1 - l], lambda out, far: out.at[far])
     settle()
     for l in range(PAIR):
         for b in range(SIDE):
-            links.arrive(("ht", l, b), (ht_a, ht_b)[l].at[b, :, pl.ds(seq, seq)])
-            links.arrive(("mt", l, b), (mt_a, mt_b)[l].at[b, :, pl.ds(seq, seq)])
-        links.arrive(("y", l), (yp_a, yp_b)[l].at[pl.ds(seq, seq)])
-        links.arrive(("z", l), (z_a, z_b)[l].at[pl.ds(seq, seq)])
-        links.arrive(("sc", l), sc_out.at[l, 1])
-
-
-def run_layers(x, dy, gain, cos, sin, turn, weights):
+            shared.arrive(("ht", l, b), (ht_a, ht_b)[l].at[b, :, pl.ds(seq, seq)])
+            shared.arrive(("mt", l, b), (mt_a, mt_b)[l].at[b, :, pl.ds(seq, seq)])
+        shared.arrive(("y", l), (yp_a, yp_b)[l].at[pl.ds(seq, seq)])
+        shared.arrive(("z", l), (z_a, z_b)[l].at[pl.ds(seq, seq)])
+        shared.arrive(("scale", l), sc_out.at[1 - l, 1])
+    links.drain()
+
+
+def run_layers(x, dy, scale, w_in, w_out, cos, sin, turn, starts=(0.0, 10.0, 20.0, 30.0)):
     seq, dim = x.shape
-    proj, cat = weights[0].shape[1], weights[1].shape[0]
+    proj, cat = w_in.shape[PAIR], ROW * w_out.shape[1]
     wide = proj + LANE
-    any_space, vmem = pl.BlockSpec(memory_space=pltpu.HBM), pl.BlockSpec(memory_space=pltpu.VMEM)
+    hbm, vmem = pl.BlockSpec(memory_space=pltpu.HBM), pl.BlockSpec(memory_space=pltpu.VMEM)
     out = lambda *shape, dtype=BF: jax.ShapeDtypeStruct(shape, dtype)
     buffer = lambda *shape, dtype=BF: pltpu.VMEM(shape, dtype)
+    sem = pltpu.SemaphoreType.DMA
     pair = PAIR * seq
     return pl.pallas_call(
-        layers_kernel,
+        functools.partial(layers_kernel, forward_order(*w_in.shape[1:], *w_out.shape[1:], starts)),
         out_shape=(out(seq, dim), out(seq, dim), *[out(SIDE, dim // ROW, pair)] * PAIR, *[out(pair, wide)] * PAIR, *[out(SIDE, cat // ROW, pair)] * PAIR,
                    *[out(pair, dim)] * PAIR, out(PAIR, PAIR, ROW, dim, dtype=F32)),
-        in_specs=[vmem] * 6 + [any_space] * SIDE,
-        out_specs=[vmem] * PAIR + [any_space] * 9,
+        in_specs=[vmem, hbm, hbm] + [vmem] * 5,
+        out_specs=[vmem] * PAIR + [hbm] * 9,
         scratch_shapes=[
             buffer(PAIR, dim, proj), buffer(PAIR, cat, dim), buffer(PAIR, seq, wide), buffer(seq, cat), buffer(PAIR, seq, dim),
             buffer(PAIR, seq, dim), buffer(PAIR, seq, dim),
@@ -564,11 +553,12 @@
             buffer(seq, SIDE * seq, dtype=F32), buffer(seq, SIDE * seq, dtype=F32), buffer(seq, SIDE * seq), buffer(seq, SIDE * seq),
             buffer(dim, seq), buffer(dim, seq), buffer(dim, seq, dtype=F32), buffer(LANE, seq, dtype=F32),
             buffer(cat, seq), buffer(dim, seq), buffer(dim, seq), buffer(PAIR, ROW, dim, dtype=F32),
-            pltpu.SemaphoreType.DMA((SIDE,)), pltpu.SemaphoreType.DMA((BAND,)), pltpu.SemaphoreType.DMA((BAND,)), pltpu.SemaphoreType.DMA((BAND,)),
+            buffer(ROW, ROW, dim, dtype=F32), buffer(ROW, dim, dtype=F32),
+            sem((SIDE,)), sem((BAND,)), sem((200,)), sem((200,)), sem((24,)), sem((24,)),
         ],
         compiler_params=pltpu.CompilerParams(collective_id=PAIR, has_side_effects=True, vmem_limit_bytes=67043328),
         name="run_layers",
-    )(x, dy, gain, cos, sin, turn, *weights)
+    )(scale, w_in, w_out, x, dy, cos, sin, turn)
 
 
 NEXT_AXES = {"x": "yz", "y": "zx", "z": "xy"}
@@ -929,19 +919,17 @@
         ff_dim = w_out.shape[1] * fsdp_size - model_dim
         head_dim = (proj_dim - model_dim - PAIR * ff_dim) // PAIR
         rows, rows_out = norm_scale.shape[1], w_out.shape[1]
-        scale_tile = jnp.pad(norm_scale.astype(jnp.float32), ((0, ROW - n_layers), (0, LANE - rows)))
-        scales, *gathered = gather_weights(scale_tile, w_in, w_out)
-        scale_full = scales[:, :n_layers, :rows].transpose(1, 0, PAIR).reshape(n_layers, model_dim)
+        scale_rows = jnp.zeros((ROW, model_dim), jnp.float32)
+        scale_rows = lax.dynamic_update_slice(scale_rows, norm_scale.astype(jnp.float32), (0, lax.axis_index("fsdp") * rows))
         cos_tab, sin_tab = rotary_tables(seq_len, head_dim)
         cos_tab, sin_tab = jnp.tile(cos_tab, (1, ROW)), jnp.tile(sin_tab, (1, ROW))
         lane = jnp.arange(WIDE)
         down = lane[:, None] - lane[None, :]
         low = lane[None, :] % head_dim < head_dim // PAIR
         turn = jnp.where(low & (down == BAND), -1.0, jnp.where(~low & (down == -BAND), 1.0, 0.0)).astype(jnp.bfloat16)
-        weights = [w.reshape(-1, w.shape[-1]) for w in gathered]
-        hidden, grad_hidden, *rest = run_layers(x_in[0], grad_y[0], jnp.pad(scale_full, ((0, ROW - n_layers), (0, 0))), cos_tab, sin_tab, turn, weights)
+        hidden, grad_hidden, *rest = run_layers(x_in[0], grad_y[0], scale_rows, w_in, w_out, cos_tab, sin_tab, turn)
         operands = [rest[PAIR * i:PAIR * i + PAIR][::-1] for i in range(SIDE)]
-        in_sums, out_sums = reduce_gradients(*operands, rest[ROW][::-1])
+        in_sums, out_sums = reduce_gradients(*operands, rest[ROW])
         in_grads = in_sums.reshape(n_layers, rows, -1)[:, :, :proj_dim]
         out_rows = out_sums.reshape(n_layers, -1, model_dim)
         scale_grads = lax.dynamic_slice(out_rows[:, rows_out], (0, lax.axis_index("fsdp") * rows), (n_layers, rows))

time: 399 us -> 355 us (0.89)
  Pallas kernels: 366 us -> 341 us
  local copies, waits for them, and re-layouts: 30.4 us -> 11.9 us
    pallas_call x2 -> x1, Pallas kernels: 165 us -> 140 us  [run_layers(): pl.pallas_call(functools.partial(layers_kernel, forward_order(*w_in.shape...]
    unnamed x20 -> x10, local copies, waits for them, and re-layouts: 17.7 us -> 1.91 us
where the time goes in v3:
time: 355 us
  Pallas kernels  341 us (96%)
  local copies, waits for them, and re-layouts  11.9 us (3%)
    pallas_call x1, Pallas kernels, reduce_gradients(): pl.pallas_call(functools.partial(reduce_kernel, reduce_order(part, part_b...  201 us
    pallas_call x1, Pallas kernels, run_layers(): pl.pallas_call(functools.partial(layers_kernel, forward_order(*w_in.shape...  140 us

profile of v3, /device:TPU:0, one launch (start us, length us, event | category | flops | bytes accessed | tf_op | source)
XLA Modules:
  0.0 354.7 jit_solution(7782420946715152439)
XLA Ops:
  0.6 0.7 convert_element_type.6
  1.3 0.4 dynamic_update_slice.3.sc_ref
  1.7 0.0 copy-start.3
  1.7 0.2 fusion.4
  1.9 0.4 copy-done.3
  2.3 0.7 select_convert_fusion.turn_ref
  3.0 0.8 copy.11.sin_ref
  3.9 0.8 copy.10.cos_ref
  4.7 139.7 %run_layers.1 = (bf16[256,768]{1,0:T(8,128)(2,1)}, bf16[256,768]{1,0:T(8,128)(2,1)}, bf16[4,96,512]{2,1,0:T(8,128)(2,1)}, bf16[4,96,512]{2,1,0:T(8,128)(2,1)}, b...) custom-call(f32[8,768]{1,0:T(8,128)} %copy-done.3, ...), custom_call_target="tpu_custom_call" | custom-call | tf_op jit(solution)/shard_map/run_layers/pallas_call | solution.py:543
  144.5 200.9 %reduce_gradients.1 = (f32[2,4,24,7168]{3,2,1,0:T(8,128)}, f32[2,4,4,32,768]{4,3,2,1,0:T(8,128)}, f32[14,4,4,24,512]{4,3,2,1,0:T(8,128)}, f32[14,4,4,24,512]{4,3...) custom-call(bf16[4,96,512]{2,1,0:T(8,128)(2,1)} %get-tuple-element.20.refs_0_, ...), custom_call_target="tpu_custom_call" | custom-call | tf_op jit(solution)/shard_map/reduce_gradients/pallas_call | solution.py:883
  345.3 0.0 copy-start
  345.4 5.4 %slice.13 = f32[2,96,7040]{2,1,0:T(8,128)} slice(f32[2,96,7168]{2,1,0:T(8,128)} %bitcast.9), slice={[0:2], [0:96], [0:7040]} | slice | bytes 10813440 | tf_op jit(solution)/shard_map/slice | solution.py:933
  350.8 0.0 copy-done
  350.8 0.0 copy-start.2
  350.8 0.0 copy-start.1
  350.8 1.8 slice.14
  352.6 0.6 constant_dynamic-slice_fusion
  353.2 0.0 copy-done.2
  353.2 0.7 copy.15
  354.0 0.0 copy-done.1
  354.0 0.7 copy.16
  (6 shorter events, 0.1 us)
Async XLA Ops:
  1.7 0.6 copy-start.3
  345.3 5.5 %copy-start = (f32[2,4,4,32,768]{4,3,2,1,0:T(8,128)S(1)}, f32[2,4,4,32,768]{4,3,2,1,0:T(8,128)}, u32[]{:S(2)}) copy-start(f32[2,4,4,32,768]{4,3,2,1,0:T(8,128)} %get-tuple-element.29) | copy-start | bytes 9437188
  350.8 2.4 copy-start.2
  350.8 3.2 copy-start.1

commit v4 on v3

v4 whole, which is shorter than its diff:
```python
import functools
import jax
import jax.numpy as jnp
from jax import lax
from jax.experimental import pallas as pl
from jax.experimental.pallas import tpu as pltpu
from jax.sharding import PartitionSpec as P

MESH_ID = pl.DeviceIdType.MESH
BOTH = (1, -1)
AROUND = (1, -1, 2)
PARTS = (True, False)
ALL = ...
LANE, WIDE, STRIP, HEAD = 128, 256, 512, 64
ROW, BAND, SIDE, PAIR = 8, 32, 4, 2


class Links:
    def __init__(self, send_sems, recv_sems):
        self.send_sems, self.recv_sems = send_sems, recv_sems
        self.slots, self.batches, self.sent = {}, {}, {}

    def send(self, key, src, dst, device, landing=None, whole=None, batch=None, lane=None):
        slot = self.slots.setdefault(landing or key, len(self.slots))
        leaving = self.batches.setdefault(batch or key, len(self.batches))
        copy = pltpu.make_async_remote_copy(
            src_ref=src, dst_ref=dst, send_sem=self.send_sems.at[leaving], recv_sem=self._landing(slot, lane),
            device_id=device, device_id_type=MESH_ID)
        copy.start()
        self.sent[batch or key] = (whole or src, leaving)

    def _landing(self, slot, lane):
        return self.recv_sems.at[slot] if lane is None else self.recv_sems.at[slot, lane]

    def arrive(self, key, landed, lane=None):
        slot = self.slots.setdefault(key, len(self.slots))
        pltpu.make_async_copy(landed, landed, self._landing(slot, lane)).wait()

    def drain(self):
        for left, leaving in self.sent.values():
            pltpu.make_async_copy(left, left, self.send_sems.at[leaving]).wait()
        self.sent.clear()


def rem(a, n):
    return a % n if isinstance(a, int) else lax.rem(a, n)


def chip_position():
    f, d = lax.axis_index("fsdp"), lax.axis_index("dp")
    return f // PAIR, rem(d, SIDE), d // SIDE, rem(f, PAIR)


def device_at(x, y, z, core):
    return (z * SIDE + y, x * PAIR + core)


def step(coord, by):
    return rem(coord + SIDE + by, SIDE)


def announce(devices):
    barrier = pltpu.get_barrier_semaphore()
    for device in devices:
        pl.semaphore_signal(barrier, inc=1, device_id=device, device_id_type=MESH_ID)
    pl.semaphore_wait(barrier, len(devices))


def plan(tasks, latency=2.5):
    free, landed, order, now = {}, {}, [], 0.0
    left = list(tasks)
    while left:
        best = None
        for place, (name, rank, start, needs, after, _, _) in enumerate(left):
            if all(n[0] in landed for n in needs) and all(n in landed for n in after):
                ready = max([start, now] + [landed[task][i] for task, i in needs])
                best = min(best or (ready, rank, place), (ready, rank, place))
        now, _, place = best
        name, _, _, _, _, sends, cost = left.pop(place)
        order.append(name)
        now += cost
        landed[name] = []
        for link, time in sends:
            free[link] = max(now, free.get(link, 0.0)) + time
            landed[name].append(free[link] + latency)
    return order


def forward_order(rows_i, cols_i, rows_o, cols_o, starts):
    rate = 23300.0
    tasks = []
    for m in range(SIDE):
        is_in = m % PAIR == 0
        edge = cols_i // LANE * SIDE // 9 // PAIR * WIDE
        size = {"y": rows_i // SIDE * edge, "x": rows_i * (cols_i - PAIR * edge)} if is_in else {"y": rows_o // SIDE * cols_o // PAIR}
        size["z"] = size["y"]
        for color in "yzx" if is_in else "yz":
            cost = size[color] / rate
            both = [(("x", by), cost) for by in BOTH]
            spread = [((color, by), cost) for by in BOTH] if color != "x" else []
            tasks.append((("reach", m, color), m, starts[m], [], [], both, 0.2))
            for i, by in enumerate(BOTH):
                tasks.append((("relay", m, color, by), m, 0.0, [(("reach", m, color), i)], [], [(("x", by), cost / PAIR)] + spread, 0.2))
            halves = [(("relay", m, color, by), 0) for by in BOTH]
            tasks.append((("far", m, color), m, 0.0, halves, [], spread, 0.2))
            if color == "x":
                continue
            for off, source, first in ((-1, ("relay", m, color, 1), 1), (1, ("relay", m, color, -1), 1), (PAIR, ("far", m, color), 0)):
                for i, by in enumerate(BOTH):
                    tasks.append((("pass", m, color, off, by), m, 0.0, [(source, first + i)], [], [((color, by), cost / PAIR)], 0.2))
                halves = [(("pass", m, color, off, by), 0) for by in BOTH]
                tasks.append((("close", m, color, off), m, 0.0, halves, [], [], 0.2))
        for off in (-1, 1, PAIR):
            last = [("close", m, color, off) for color in "yz"]
            if is_in:
                last.append(("far", m, "x") if off == PAIR else ("relay", m, "x", -off))
            tasks.append((("hand", m, off), m, 0.0, [], last, [("chip", (rows_i * cols_i if is_in else rows_o * cols_o) / 150000.0)], 0.2))
    before = []
    for l in range(PAIR):
        work = [(("norm", l), [], 0.8)] + [(("project", l, i), [PAIR * l], 1.4) for i in range(SIDE)]
        work += [(("attend", l), [], 4.0), (("mlp", l), [], 2.2), (("put", l), [PAIR * l + 1], 2.0)]
        for name, mats, cost in work:
            needs = [(("hand", m, off), 0) for m in mats for off in (-1, 1, PAIR)]
            tasks.append((name, 9, 0.0, needs, before, [], cost))
            before = [name]
    tasks.append((("give",), 9, 45.0, [], [], [], 0.3))
    return plan(tasks)


def gather_stages(links, position, shard_i, shard_o, wi, wo, lsem):
    x, y, z, core = position
    twin = device_at(x, y, z, 1 - core)
    rows_i, cols_i = shard_i.shape[1:]
    rows_o, cols_o = shard_o.shape[1:]
    quarter_i, quarter_o = rows_i // SIDE, rows_o // SIDE
    third_i = cols_i // LANE * SIDE // 9 // PAIR * WIDE
    half_o = cols_o // PAIR
    cut_o = quarter_o // 16 * ROW + ROW if quarter_o % 16 else quarter_o // PAIR
    place = {"x": x, "y": y, "z": z}

    spots = {(axis, o): step(place[axis], o) for axis in "xyz" for o in range(SIDE)}

    def spot(axis, o):
        return spots[axis, o % SIDE]

    table = {}
    for axis in "xyz":
        for o in range(1, SIDE):
            moved = {**place, axis: spot(axis, o)}
            table[axis, o] = device_at(moved["x"], moved["y"], moved["z"], core)

    def peer(axis, o):
        return table[axis, o % SIDE]

    mats = []
    for l in range(PAIR):
        mats.append((shard_i.at[l], wi.at[l], rows_i, True))
        mats.append((shard_o.at[l], wo.at[l], rows_o, False))

    def region(is_in, color, q):
        if is_in:
            if color == "x":
                lo, hi = PAIR * third_i, cols_i
                rows = (0, rows_i)
            else:
                lo, hi = (0, third_i) if color == "y" else (third_i, PAIR * third_i)
                rows = (q * quarter_i, quarter_i)
            mid = lo + ((hi - lo) // LANE + 1) // PAIR * LANE
            return (rows, (lo, hi - lo)), (rows, (lo, mid - lo)), (rows, (mid, hi - mid))
        cols = (0, half_o) if color == "y" else (half_o, half_o)
        start = q * quarter_o
        return ((start, quarter_o), cols), ((start, cut_o), cols), ((start + cut_o, quarter_o - cut_o), cols)

    def at(m, xb, area):
        (r, nr), (c, nc) = area
        _, out, size, _ = mats[m]
        return out.at[pl.ds(pl.multiple_of((PAIR * xb + core) * size + r, ROW), nr), pl.ds(c, nc)]

    def block(m, xb, index):
        _, out, size, _ = mats[m]
        return out.at[pl.ds(pl.multiple_of((PAIR * xb + index) * size, BAND), size)]

    def colors(m):
        return "yzx" if mats[m][3] else "yz"

    def reach(m, color):
        src, _, _, is_in = mats[m]
        area = region(is_in, color, place[color])[0]
        for by in BOTH:
            links.send((m, "x1", color, by), src.at[pl.ds(pl.multiple_of(area[0][0], ROW), area[0][1]), pl.ds(*area[1])], at(m, x, area), peer("x", by))

    def launch(m, color, off):
        is_in = mats[m][3]
        moved = at(m, spot("x", off), region(is_in, color, place[color])[0])
        for by in BOTH:
            links.send((m, "p1", color, off, by), moved, moved, peer(color, by))

    def relay(m, color, by):
        is_in = mats[m][3]
        xb = spot("x", -by)
        areas = region(is_in, color, place[color])
        links.arrive((m, "x1", color, by), at(m, xb, areas[0]))
        part = at(m, xb, areas[1] if by == 1 else areas[PAIR])
        links.send((m, "x2", color, by), part, part, peer("x", by))
        if color != "x":
            launch(m, color, -by)

    def far(m, color):
        is_in = mats[m][3]
        areas = region(is_in, color, place[color])
        for by in BOTH:
            links.arrive((m, "x2", color, by), at(m, spot("x", PAIR), areas[1] if by == 1 else areas[PAIR]))
        if color != "x":
            launch(m, color, PAIR)

    def pass_on(m, color, off, by):
        is_in = mats[m][3]
        xb = spot("x", off)
        areas = region(is_in, color, spot(color, -by))
        links.arrive((m, "p1", color, off, by), at(m, xb, areas[0]))
        part = at(m, xb, areas[1] if by == 1 else areas[PAIR])
        links.send((m, "p2", color, off, by), part, part, peer(color, by))

    def close(m, color, off):
        is_in = mats[m][3]
        areas = region(is_in, color, spot(color, PAIR))
        for by in BOTH:
            links.arrive((m, "p2", color, off, by), at(m, spot("x", off), areas[1] if by == 1 else areas[PAIR]))

    def hand(m, off):
        whole = block(m, spot("x", off), core)
        links.send((m, "d2d", off), whole, whole, twin)

    owns = []

    def begin():
        for m, (src, _, _, _) in enumerate(mats):
            copy = pltpu.make_async_copy(src, block(m, x, core), lsem.at[m])
            copy.start()
            owns.append(copy)
            links.send((m, "d2d", 0), src, block(m, x, core), twin)

    def ready(m):
        owns[m].wait()
        for off in (0, -1, 1, PAIR):
            links.arrive((m, "d2d", off), block(m, spot("x", off), 1 - core))

    return begin, ready, peer, {"reach": reach, "relay": relay, "far": far, "pass": pass_on, "close": close, "hand": hand}


BF, F32 = jnp.bfloat16, jnp.float32


def product(a, b, contract=((1,), (0,))):
    return lax.dot_general(a, b, (contract, ((), ())), preferred_element_type=F32)


def lanes(start, size):
    return pl.ds(start if isinstance(start, int) else pl.multiple_of(start, LANE), size)


def layers_kernel(order, sc_ref, wi_ref, wo_ref, x_ref, dy_ref, cos_ref, sin_ref, turn_ref,
                  y_ref, gx_ref, hy_a, hy_b, hz_a, hz_b, mx_a, mx_b, yx_a, yx_b, zy_b, zz_b, z_a, sc_out,
                  wi, wo, z, om, h, hid, qr, kts, vts, ksl, scores, dscores, pcat, dscat,
                  dot_heads, qt, dht, dkv, omt, ht, dyt, sc, gains, gain_ref, load_sems, own_sems, send_sems, recv_sems,
                  share_send_sems, share_recv_sems):
    seq, dim = x_ref.shape
    ff = (wi.shape[PAIR] - dim - LANE) // PAIR
    position = chip_position()
    x, y, zc, core = position
    twin = device_at(x, y, zc, 1 - core)
    me = PAIR * x + core
    links, shared = Links(send_sems, recv_sems), Links(share_send_sems, share_recv_sems)
    stored = []
    spots, _ = around(position)
    h_out, m_out, y_out, z_out = {"y": (hy_a, hy_b), "z": (hz_a, hz_b)}, (mx_a, mx_b), (yx_a, yx_b), {"y": zy_b, "z": zz_b}
    begin, ready, peer, stages = gather_stages(links, position, wi_ref, wo_ref, wi, wo, load_sems)
    others = [(zc * SIDE + y, rem(me + k, ROW)) for k in range(1, ROW)]

    def spot(axis, o):
        return spots[axis, o % SIDE]

    def device(axis, o, index):
        moved = {"x": x, "y": y, "z": zc, axis: spot(axis, o)}
        return device_at(moved["x"], moved["y"], moved["z"], index)

    announce(others + [device(axis, o, index) for axis in "yz" for o in AROUND for index in range(PAIR)])
    begin()
    for k, far in enumerate(others):
        links.send(("sc", k), sc_ref, gains.at[me], far)

    def keep(src, dst):
        copy = pltpu.make_async_copy(src, dst, own_sems.at[len(stored)])
        copy.start()
        stored.append(copy)

    def tokens(axis, o, index):
        return pl.ds(pl.multiple_of((PAIR * spot(axis, o) + index) * seq, seq), seq)

    def columns(axis, o):
        size = z.shape[PAIR] // ROW
        return lanes(((0 if axis == "y" else SIDE) + spot(axis, o)) * size, size)

    def send_h(l):
        for axis in "yz":
            out = h_out[axis][l].at[:, :, tokens(axis, 0, core)]
            for o in AROUND:
                for index in range(PAIR):
                    shared.send(("h", l, axis, o), ht.at[l, :, index], out, device(axis, o, index), batch=("h", l, axis, o, index), lane=core)
            shared.send(("h", l, axis), ht.at[l, :, 1 - core], out, twin, lane=0)
            keep(ht.at[l, :, core], out)

    def arrive_h(l):
        for axis in "yz":
            for o in AROUND:
                for index in range(PAIR):
                    shared.arrive(("h", l, axis, o), h_out[axis][l].at[:, :, tokens(axis, -o, index)], index)
            shared.arrive(("h", l, axis), h_out[axis][l].at[:, :, tokens(axis, 0, 1 - core)], 0)

    def row_block(l, o, index):
        size = omt.shape[1] // ROW
        return omt.at[l, pl.ds(pl.multiple_of((PAIR * spot("x", o) + index) * size, BAND), size)]

    def send_m(l):
        out = m_out[l].at[:, tokens("x", 0, core)]
        for o in AROUND:
            for index in range(PAIR):
                shared.send(("m", l, o), row_block(l, o, index), out, device("x", o, index), batch=("m", l, o, index), lane=core)
        shared.send(("m", l), row_block(l, 0, 1 - core), out, twin, lane=0)
        keep(row_block(l, 0, core), out)

    def arrive_m(l):
        for o in AROUND:
            for index in range(PAIR):
                shared.arrive(("m", l, o), m_out[l].at[:, tokens("x", -o, index)], index)
        shared.arrive(("m", l), m_out[l].at[:, tokens("x", 0, 1 - core)], 0)

    def send_y(l, src):
        out = y_out[l].at[tokens("x", 0, core)]
        for o in AROUND:
            shared.send(("y", l, o), src, out, device("x", o, core), lane=0)
        shared.send(("y", l), src, out, twin, lane=0)
        keep(src, out)

    def pass_y(l):
        for o in AROUND:
            landed = y_out[l].at[tokens("x", -o, core)]
            shared.arrive(("y", l, o), landed, 0)
            shared.send(("y", l, o, "pass"), landed, landed, twin, lane=0)

    def arrive_y(l):
        for o in AROUND:
            shared.arrive(("y", l, o, "pass"), y_out[l].at[tokens("x", -o, 1 - core)], 0)
        shared.arrive(("y", l), y_out[l].at[tokens("x", 0, 1 - core)], 0)

    def send_z(l):
        for axis in "yz":
            out = z_out[axis].at[tokens(axis, 0, core)]
            for o in AROUND:
                shared.send(("z", axis, o), z.at[l, :, columns(axis, o)], out, device(axis, o, core), lane=0)
            shared.send(("z", axis), z.at[l, :, columns(axis, 0)], out, twin, lane=0)
            keep(z.at[l, :, columns(axis, 0)], out)

    def pass_z():
        for axis in "yz":
            for o in AROUND:
                landed = z_out[axis].at[tokens(axis, -o, core)]
                shared.arrive(("z", axis, o), landed, 0)
                shared.send(("z", axis, o, "pass"), landed, landed, twin, lane=0)

    def arrive_z():
        for axis in "yz":
            for o in AROUND:
                shared.arrive(("z", axis, o, "pass"), z_out[axis].at[tokens(axis, -o, 1 - core)], 0)
            shared.arrive(("z", axis), z_out[axis].at[tokens(axis, 0, 1 - core)], 0)

    def send_scale(l):
        for k, far in enumerate(others):
            shared.send(("scale", l, k), sc.at[l], sc_out.at[l, me], far, lane=0)
        keep(sc.at[l], sc_out.at[l, me])

    def arrive_scale(l):
        for k in range(len(others)):
            shared.arrive(("scale", l, k), sc_out.at[l, rem(me + 7 - k, ROW)], 0)

    gains[me] = sc_ref[ALL]
    z[:, :, wi.shape[PAIR]:] = jnp.zeros((PAIR, seq, z.shape[PAIR] - wi.shape[PAIR]), BF)
    entry = (x_ref, hid.at[0])
    kts[ALL] = jnp.zeros(kts.shape, BF)
    vts[ALL] = jnp.zeros(vts.shape, BF)

    def normalise(l, src):
        @pl.loop(0, seq // BAND)
        def _(r):
            rows = pl.ds(pl.multiple_of(r * BAND, BAND), BAND)
            v = src[rows].astype(F32)
            v = v - jnp.mean(v, axis=-1, keepdims=True)
            var = jnp.mean(v * v, axis=-1, keepdims=True)
            h[l, rows] = (v * lax.rsqrt(var + 1e-6) * gain_ref[l:l + 1]).astype(BF)

    def project(l, quarter):
        def part(at, size):
            z[l, :, lanes(at, size)] = product(h[l], wi[l, :, lanes(at, size)]).astype(BF)

        n = wi.shape[PAIR] // STRIP

        @pl.loop(quarter * n // SIDE, (quarter + 1) * n // SIDE)
        def _(i):
            part(i * STRIP, STRIP)
        if quarter == 3:
            part(n * STRIP, wi.shape[PAIR] - n * STRIP)

    def heads(l):
        cos, sin = cos_ref[ALL], sin_ref[ALL]
        for g in range(dim // WIDE):
            q = z[l, :, g * WIDE:(g + 1) * WIDE]
            qr[l, :, g * WIDE:(g + 1) * WIDE] = ((q.astype(F32) * cos + product(q, turn_ref[ALL]) * sin) * 0.125).astype(BF)
        kv = z[l, :, dim:dim + LANE]
        turned = kv.astype(F32) * cos[:, :LANE] + product(kv, turn_ref[:LANE, :LANE]) * sin[:, :LANE]
        first = lax.broadcasted_iota(jnp.int32, turned.shape, 1) < HEAD
        key_lo = jnp.where(first, turned, 0.0)
        val_hi = jnp.where(first, 0.0, kv.astype(F32))
        return key_lo, pltpu.roll(key_lo, HEAD, 1), pltpu.roll(val_hi, HEAD, 1), val_hi

    def slot_rows(ref, lo, hi):
        zero = jnp.zeros((seq, LANE), BF)
        lo, hi = lo.astype(BF), hi.astype(BF)
        for i, (left, right) in enumerate(((lo, zero), (hi, zero), (zero, lo), (zero, hi))):
            ref[i * seq:(i + 1) * seq, :LANE] = left
            ref[i * seq:(i + 1) * seq, LANE:] = right

    def slot_cols(ref, lo):
        flat = lo.T[:HEAD].astype(BF)
        for i in range(SIDE):
            ref[HEAD * i:HEAD * (i + 1), i * seq:(i + 1) * seq] = flat

    def chances(rows, r, i):
        s = scores[rows, i * seq:(i + 1) * seq]
        at = lax.broadcasted_iota(jnp.int32, s.shape, 0) + r * BAND
        s = jnp.where(at >= lax.broadcasted_iota(jnp.int32, s.shape, 1), s, -1e30)
        e = jnp.exp(s - jnp.max(s, axis=-1, keepdims=True))
        return e * (1.0 / jnp.sum(e, axis=-1, keepdims=True))

    def attend(l):
        key_lo, _, val_lo, val_hi = heads(l)
        slot_cols(kts, key_lo)
        slot_rows(ksl, val_lo, val_hi)

        @pl.loop(0, dim // WIDE)
        def _(g):
            cols = lanes(g * WIDE, WIDE)
            scores[ALL] = product(qr[l, :, cols], kts[ALL])

            @pl.loop(0, seq // BAND)
            def _(r):
                rows = pl.ds(pl.multiple_of(r * BAND, BAND), BAND)
                for i in range(SIDE):
                    pcat[rows, i * seq:(i + 1) * seq] = chances(rows, r, i).astype(BF)
            om[:, cols] = product(pcat[ALL], ksl[ALL]).astype(BF)

    def mlp(l):
        @pl.loop(0, seq // BAND)
        def _(r):
            rows = pl.ds(pl.multiple_of(r * BAND, BAND), BAND)

            @pl.loop(0, ff // STRIP)
            def _(i):
                gate = z[l, rows, lanes(dim + LANE + i * STRIP, STRIP)].astype(F32)
                up = z[l, rows, lanes(dim + LANE + ff + i * STRIP, STRIP)].astype(F32)
                om[rows, lanes(dim + i * STRIP, STRIP)] = (gate * jax.nn.sigmoid(gate) * up).astype(BF)

    def put_out(l, dst):
        for n in range(dim // WIDE):
            cols = slice(n * WIDE, (n + 1) * WIDE)
            total = product(om[ALL], wo[l, :, cols])
            dst[:, cols] = (entry[l][:, cols].astype(F32) + total).astype(BF)

    def flip(src, dst, width):
        @pl.loop(0, width // WIDE)
        def _(i):
            dst[pl.ds(pl.multiple_of(i * WIDE, WIDE), WIDE)] = src(i * WIDE).T

    def backward(l, dy):
        flip(lambda at: dy[:, lanes(at, WIDE)], dyt, dim)

        @pl.loop(0, wo.shape[1] // dim)
        def _(n):
            rows = pl.ds(pl.multiple_of(n * dim, dim), dim)
            part = product(wo[l, rows], dyt[ALL]).astype(BF)
            om[:, lanes(n * dim, dim)] = part.T

            @pl.when(n == 0)
            def _():
                dot_heads[ALL] = part

        @pl.loop(0, seq // BAND)
        def _(r):
            rows = pl.ds(pl.multiple_of(r * BAND, BAND), BAND)

            @pl.loop(0, ff // STRIP)
            def _(i):
                gate_at, up_at = lanes(dim + LANE + i * STRIP, STRIP), lanes(dim + LANE + ff + i * STRIP, STRIP)
                gate, up = z[l, rows, gate_at].astype(F32), z[l, rows, up_at].astype(F32)
                d = om[rows, lanes(dim + i * STRIP, STRIP)].astype(F32)
                sig = jax.nn.sigmoid(gate)
                du = d * up
                z[l, rows, gate_at] = (du * sig + du * gate * (sig * (1.0 - sig))).astype(BF)
                z[l, rows, up_at] = (d * (gate * sig)).astype(BF)

        key_lo, key_hi, val_lo, val_hi = heads(l)
        slot_cols(kts, key_lo)
        slot_cols(vts, val_lo)
        slot_rows(ksl, key_lo, key_hi)
        dkv[ALL] = jnp.zeros(dkv.shape, F32)
        flip(lambda at: qr[l, :, lanes(at, WIDE)], qt, dim)

        @pl.loop(0, dim // WIDE)
        def _(g):
            cols = lanes(g * WIDE, WIDE)
            scores[ALL] = product(qr[l, :, cols], kts[ALL])
            dscores[ALL] = product(om[:, cols], vts[ALL])

            @pl.loop(0, seq // BAND)
            def _(r):
                rows = pl.ds(pl.multiple_of(r * BAND, BAND), BAND)
                for i in range(SIDE):
                    at = slice(i * seq, (i + 1) * seq)
                    p = chances(rows, r, i)
                    pcat[rows, at] = p.astype(BF)
                    pd = p * dscores[rows, at].astype(BF).astype(F32)
                    dscat[rows, at] = (pd - p * jnp.sum(pd, axis=-1, keepdims=True)).astype(BF)
            dq = product(dscat[ALL], ksl[ALL]).astype(BF)
            back = dq.astype(F32) * cos_ref[ALL] - product(dq, turn_ref[ALL]) * sin_ref[ALL]
            z[l, :, cols] = (back * 0.125).astype(BF)
            for i in range(SIDE):
                head = pl.ds(pl.multiple_of(g * WIDE + i * HEAD, HEAD), HEAD)
                at = slice(i * seq, (i + 1) * seq)
                dkv[:HEAD] += product(qt[head], dscat[:, at])
                dkv[HEAD:] += product(dot_heads[head], pcat[:, at])

        dkv_t = dkv[ALL].T
        dk = dkv_t.astype(BF)
        turned = dk.astype(F32) * cos_ref[:, :LANE] - product(dk, turn_ref[:LANE, :LANE]) * sin_ref[:, :LANE]
        first = lax.broadcasted_iota(jnp.int32, turned.shape, 1) < HEAD
        z[l, :, dim:dim + LANE] = jnp.where(first, turned, dkv_t).astype(BF)

    def backward_rows(l, dy, dst):
        n, width = wi.shape[PAIR] // 1408, 1408
        for i in range(n):
            at = slice(i * width, (i + 1) * width)
            part = product(wi[l, :, at], z[l, :, at], ((1,), (1,)))
            dht[ALL] = part if i == 0 else dht[ALL] + part
        for i in range(dim // WIDE):
            cols = slice(i * WIDE, (i + 1) * WIDE)
            h[l, :, cols] = dht[cols].T.astype(BF)
        sc[l] = jnp.zeros(sc.shape[1:], F32)

        @pl.loop(0, seq // BAND)
        def _(r):
            rows = pl.ds(pl.multiple_of(r * BAND, BAND), BAND)
            v = entry[l][rows].astype(F32)
            v = v - jnp.mean(v, axis=-1, keepdims=True)
            scale = lax.rsqrt(jnp.mean(v * v, axis=-1, keepdims=True) + 1e-6)
            hat = v * scale
            d = h[l, rows].astype(F32)
            each = (d * hat).reshape(SIDE, ROW, dim)
            sc[l] += (each[0] + each[1]) + (each[PAIR] + each[3])
            d = d * gain_ref[l:l + 1]
            d = scale * (d - jnp.mean(d, axis=-1, keepdims=True) - hat * jnp.mean(d * hat, axis=-1, keepdims=True))
            dst[rows] = (dy[rows].astype(F32) + d.astype(BF).astype(F32)).astype(BF)

    def do_norm(l):
        if l == 0:
            for k, (_, f) in enumerate(others):
                links.arrive(("sc", k), gains.at[rem(me + 7 - k, ROW)])
            gain_ref[ALL] = jnp.sum(gains[ALL], axis=0)
        normalise(l, entry[l])
        for i in range(dim // WIDE):
            flat = h[l, :, i * WIDE:(i + 1) * WIDE].T
            size = ht.shape[3]
            for b in range(ROW):
                lo, hi = max(b * size, i * WIDE), min((b + 1) * size, (i + 1) * WIDE)
                if lo < hi:
                    ht[l, b // PAIR, b % PAIR, lo - b * size:hi - b * size] = flat[lo - i * WIDE:hi - i * WIDE]

    def do_project(l, i):
        if i == 0:
            ready(PAIR * l)
        project(l, i)

    def do_mlp(l):
        mlp(l)
        flip(lambda at: om[:, lanes(at, WIDE)], omt.at[l], om.shape[1])
        if l == 0:
            send_m(l)

    def do_put(l):
        ready(PAIR * l + 1)
        put_out(l, hid.at[0] if l == 0 else y_ref)

    stages.update(norm=do_norm, project=do_project, attend=attend, mlp=do_mlp, put=do_put, give=lambda: send_y(1, dy_ref))
    for kind, *task in order:
        stages[kind](*task)
    send_h(0)
    send_h(1)
    send_m(1)
    middle = hid.at[1]
    backward(1, dy_ref)
    send_z(1)
    backward_rows(1, dy_ref, middle)
    send_y(0, middle)
    send_scale(1)
    pass_y(1)
    backward(0, middle)
    keep(z.at[0], z_a)
    pass_z()
    backward_rows(0, middle, gx_ref)
    send_scale(0)
    pass_y(0)
    for l in range(PAIR):
        arrive_h(l)
        arrive_m(l)
        arrive_scale(l)
        arrive_y(l)
    arrive_z()
    for copy in stored:
        copy.wait()
    shared.drain()
    links.drain()


def run_layers(x, dy, scale, w_in, w_out, cos, sin, turn, starts=(0.0, 10.0, 20.0, 30.0)):
    seq, dim = x.shape
    proj, cat = w_in.shape[PAIR], ROW * w_out.shape[1]
    wide = proj + LANE
    hbm, vmem = pl.BlockSpec(memory_space=pltpu.HBM), pl.BlockSpec(memory_space=pltpu.VMEM)
    out = lambda *shape, dtype=BF: jax.ShapeDtypeStruct(shape, dtype)
    buffer = lambda *shape, dtype=BF: pltpu.VMEM(shape, dtype)
    sem = pltpu.SemaphoreType.DMA
    line = ROW * seq
    return pl.pallas_call(
        functools.partial(layers_kernel, forward_order(*w_in.shape[1:], *w_out.shape[1:], starts)),
        out_shape=(out(seq, dim), out(seq, dim), *[out(SIDE, dim // ROW, line)] * SIDE, *[out(cat // ROW, line)] * PAIR, *[out(line, dim)] * PAIR,
                   *[out(line, wide // ROW)] * PAIR, out(seq, wide), out(PAIR, ROW, ROW, dim, dtype=F32)),
        in_specs=[vmem, hbm, hbm] + [vmem] * 5,
        out_specs=[vmem] * PAIR + [hbm] * 12,
        scratch_shapes=[
            buffer(PAIR, dim, proj), buffer(PAIR, cat, dim), buffer(PAIR, seq, wide), buffer(seq, cat), buffer(PAIR, seq, dim),
            buffer(PAIR, seq, dim), buffer(PAIR, seq, dim),
            buffer(WIDE, SIDE * seq), buffer(WIDE, SIDE * seq), buffer(SIDE * seq, WIDE),
            buffer(seq, SIDE * seq, dtype=F32), buffer(seq, SIDE * seq, dtype=F32), buffer(seq, SIDE * seq), buffer(seq, SIDE * seq),
            buffer(dim, seq), buffer(dim, seq), buffer(dim, seq, dtype=F32), buffer(LANE, seq, dtype=F32),
            buffer(PAIR, cat, seq), buffer(PAIR, SIDE, PAIR, dim // ROW, seq), buffer(dim, seq), buffer(PAIR, ROW, dim, dtype=F32),
            buffer(ROW, ROW, dim, dtype=F32), buffer(ROW, dim, dtype=F32),
            sem((SIDE,)), sem((16,)), sem((200,)), sem((200,)), sem((96,)), sem((96, PAIR)),
        ],
        compiler_params=pltpu.CompilerParams(collective_id=PAIR, has_side_effects=True, vmem_limit_bytes=67043328),
        name="run_layers",
    )(scale, w_in, w_out, x, dy, cos, sin, turn)


PARTS = (("i", "x", "z", "y", 0, STRIP), ("i", "x", "z", "y", STRIP, 384), ("i", "x", "y", "z", 0, STRIP), ("i", "x", "y", "z", STRIP, 384),
         ("o", "y", "z", "y", 0, 384), ("o", "z", "y", "z", 384, 384))


def reduce_order(rows, rows_b, starts):
    rate = 11650.0
    tasks = []
    moved = WIDE * 896 / (PAIR * rate)
    tasks.append((("swap",), (0, 0), 0.0, [], [], [((axis, by), moved * n) for axis in "yz" for by, n in ((1, 1), (-1, 1), (1, PAIR))] + [("chip", 0.8)] * PAIR, 0.5))
    for i, axis in enumerate("yz"):
        for j, o in enumerate(AROUND):
            tasks.append((("pass", axis, o), (0, 1), 0.0, [(("swap",), 3 * i + j)], [], [("chip", 1.6)], 0.2))
    for l in (1, 0):
        late = 1 - l
        for c, (kind, first, then, last, at, width) in enumerate(PARTS):
            needs, cost = [], 1.6 * width / STRIP
            if kind == "i" and l == 0:
                needs = [(("pass", last, o), 0) for o in AROUND]
            tasks.append((("make", l, c), (9 * late, -c), starts[late], needs, [], [], cost))
            full = SIDE * SIDE * (rows if kind == "i" else rows_b) * width / rate
            sends = [[((first, by), full / ROW) for by in BOTH], [((first, by), full / SIDE) for by in BOTH],
                     [((then, o), full / 16) for o in (1, -1, 1)], []]
            piece = full / 16
            sends += [[((then, by), piece) for by in BOTH], [((then, 1 - PAIR * (c % PAIR)), piece)], [((last, by), SIDE * piece) for by in BOTH],
                      [((last, by), PAIR * piece) for by in BOTH], []]
            for s in range(9):
                task = ("sum", l, c, s)
                needs = [(("sum", l, c, s - 1), k) for k in range(len(sends[s - 1]))] if s else []
                tasks.append((task, (late, -s), 0.0, needs, [("make", l, c)] if s == 0 else [("sum", l, c, s - 1)], sends[s], 0.3))
    return plan(tasks)


def reduce_kernel(order, *refs):
    hy, hz, mx, yx = refs[0:PAIR], refs[PAIR:SIDE], refs[SIDE:6], refs[6:ROW]
    zy1, zz1, z0, sc = refs[ROW:12]
    oa, ob = refs[12:14]
    n = len(PARTS)
    total, half, full, small, front = (refs[14 + k * n:14 + (k + 1) * n] for k in range(5))
    (hbuf, zbuf, mbuf, ybuf, scbuf, ssem, rsem, isem, osem, zsem) = refs[14 + 5 * n:]
    position = chip_position()
    x, y, zc, core = position
    place = {"x": x, "y": y, "z": zc}
    twin = device_at(x, y, zc, 1 - core)
    spots, peers = around(position)

    def spot(axis, o):
        return spots[axis, o % SIDE]

    def peer(axis, o):
        return peers[axis, o % SIDE]

    seq, wide = z0.shape
    own = wide // ROW
    loads = {}

    def load(key, src, dst):
        copy = pltpu.make_async_copy(src, dst, isem.at[len(loads)])
        copy.start()
        loads[key] = copy

    for l in (1, 0):
        if l:
            load(("z", 1, "y"), zy1, zbuf.at[1, 0])
            load(("z", 1, "z"), zz1, zbuf.at[1, 1])
        load(("h", l, "y"), hy[l], hbuf.at[l, 0])
        load(("h", l, "z"), hz[l], hbuf.at[l, 1])
        load(("m", l), mx[l], mbuf.at[l])
        load(("y", l), yx[l], ybuf.at[l])
        load(("s", l), sc.at[l], scbuf.at[l])
    done = set()

    def loaded(*keys):
        for key in keys:
            if key not in done:
                loads[key].wait()
                done.add(key)

    announce([peer(axis, o) for axis in "xyz" for o in AROUND] + [twin])
    links = Links(ssem, rsem)

    def columns(axis, o):
        return lanes(((0 if axis == "y" else SIDE) + spot(axis, o)) * own, own)

    def tokens(axis, o, index):
        return pl.ds(pl.multiple_of((PAIR * spot(axis, o) + index) * seq, seq), seq)

    def swap():
        for i, axis in enumerate("yz"):
            mine = zbuf.at[0, i, tokens(axis, 0, core)]
            for o in AROUND:
                links.send(("z", axis, o), z0.at[:, columns(axis, o)], mine, peer(axis, o))
            links.send(("near", axis), z0.at[:, columns(axis, 0)], mine, twin)
            load(("own", axis), z0.at[:, columns(axis, 0)], mine)

    def hand_on(axis, o):
        i = "yz".index(axis)
        landed = zbuf.at[0, i, tokens(axis, -o, core)]
        links.arrive(("z", axis, o), landed)
        links.send(("pass", axis, o), landed, landed, twin)

    def make(l, c):
        kind, first, then, last, at, width = PARTS[c]
        if kind == "i":
            i = "yz".index(last)
            loaded(("h", l, last))
            if l:
                loaded(("z", 1, last))
            elif ("joined", last) not in done:
                done.add(("joined", last))
                loaded(("own", last))
                links.arrive(("near", last), zbuf.at[0, i, tokens(last, 0, 1 - core)])
                for o in AROUND:
                    links.arrive(("pass", last, o), zbuf.at[0, i, tokens(last, -o, 1 - core)])
            size = total[c].shape[3]
            for lo in range(0, width, WIDE):
                hi = min(width, lo + WIDE)
                part = product(hbuf[l, i].reshape(-1, hbuf.shape[-1]), zbuf[l, i, :, at + lo:at + hi])
                for r in range(16):
                    total[c][l, r // SIDE, r % SIDE, :, lo:hi] = part[r * size:(r + 1) * size]
            return
        loaded(("m", l), ("y", l), ("s", l))
        part = product(mbuf[l], ybuf[l, :, at:at + width])
        size = total[c].shape[3]

        def put(r, value):
            total[c][(l, r // SIDE, r % SIDE) if first == "y" else (l, r % SIDE, r // SIDE)] = value

        for r in range(part.shape[0] // size):
            put(r, part[r * size:(r + 1) * size])
        gain = jnp.sum(jnp.sum(scbuf[l, :, :, at:at + width], axis=0), axis=0, keepdims=True)
        row = lax.broadcasted_iota(jnp.int32, (size, width), 0)
        put(15, jnp.where(row == 0, gain, 0.0))

    def area(l, c, o, whole):
        kind, first, then, last, at, width = PARTS[c]
        inner = (spot(then, whole) if isinstance(whole, int) else whole)
        outer = spot(last, o)
        if kind == "i":
            cols = lanes(((0 if last == "y" else SIDE) + outer) * own + at, width)
            return oa.at[l, inner, :, cols]
        cols = pl.ds(at, width)
        return ob.at[l, outer, inner, :, cols] if last == "y" else ob.at[l, inner, outer, :, cols]

    def add(l, c, s):
        kind, first, then, last, at, width = PARTS[c]
        t = total[c].at[l]
        way = 1 - PAIR * (c % PAIR)
        key = (l, c)
        if s == 0:
            far = t.at[spot(first, PAIR)]
            for k, by in enumerate(BOTH):
                links.send((*key, "half", by), far.at[pl.ds(PAIR * k, PAIR)], half[c].at[l, k], peer(first, by))
        elif s == 1:
            for k, by in enumerate(BOTH):
                links.arrive((*key, "half", by), half[c].at[l, k])
                mine = t.at[spot(first, by)]
                add_into(mine.at[pl.ds(PAIR * k, PAIR)], half[c].at[l, k])
                links.send((*key, "full", by), mine, full[c].at[l, k], peer(first, by))
        elif s == PAIR:
            mine = t.at[spot(first, 0)]
            for k, by in enumerate(BOTH):
                links.arrive((*key, "full", by), full[c].at[l, k])
                add_into(mine, full[c].at[l, k])
            for k, o in enumerate(AROUND):
                links.send((*key, "small", o), mine.at[spot(then, o)], small[c].at[l, k], peer(then, o), (*key, "small", 1), small[c].at[l], (*key, "small"))
        elif s == 3:
            links.arrive((*key, "small", 1), small[c].at[l])
            mine = t.at[spot(first, 0), spot(then, 0)]
            front[c][l] = (mine[ALL] + small[c][l, 0]) + (small[c][l, 1] + small[c][l, PAIR])
        elif s == SIDE:
            src, dst = front[c].at[l], area(l, c, 0, 0)
            for by in BOTH:
                links.send((*key, "a1", by), src, dst, peer(then, by))
            copy = pltpu.make_async_copy(src, dst, osem.at[l, c])
            copy.start()
            loads["front", l, c] = copy
        elif s == 5:
            for by in BOTH:
                landed = area(l, c, 0, -by)
                links.arrive((*key, "a1", by), landed)
                if way == by:
                    links.send((*key, "b1"), landed, landed, peer(then, by))
        elif s == 6:
            loaded(("front", l, c))
            links.arrive((*key, "b1"), area(l, c, 0, PAIR))
            line = area(l, c, 0, slice(None))
            for by in BOTH:
                links.send((*key, "a2", by), line, line, peer(last, by))
        elif s == 7:
            for k, by in enumerate(BOTH):
                links.arrive((*key, "a2", by), area(l, c, -by, slice(None)))
                part = area(l, c, -by, pl.ds(PAIR * k, PAIR))
                links.send((*key, "a3", by), part, part, peer(last, by))
        else:
            for k, by in enumerate(BOTH):
                links.arrive((*key, "a3", by), area(l, c, PAIR, pl.ds(PAIR * k, PAIR)))

    stages = {"swap": swap, "pass": hand_on, "make": make, "sum": add}
    for kind, *task in order:
        stages[kind](*task)
    links.drain()


def add_into(dst, src):
    @pl.loop(0, dst.shape[0])
    def _(i):
        if len(dst.shape) == SIDE:
            for j in range(dst.shape[1]):
                dst[i, j] += src[i, j]
        else:
            dst[i] += src[i]


def around(position):
    place, core = dict(zip("xyz", position)), position[3]
    spots = {(axis, o): step(place[axis], o) for axis in "xyz" for o in range(SIDE)}
    peers = {}
    for axis in "xyz":
        for o in range(1, SIDE):
            moved = {**place, axis: spots[axis, o]}
            peers[axis, o] = device_at(moved["x"], moved["y"], moved["z"], core)
    return spots, peers


def reduce_gradients(operands, starts=(0.0, 0.0)):
    hbm = pl.BlockSpec(memory_space=pltpu.HBM)
    h_rows, m_rows, y_cols, z_cols, z_own, scale_parts = operands
    part, part_b = h_rows[0].shape[1] // SIDE, (m_rows[0].shape[0] + BAND) // 16
    (line, dim), wide = y_cols[0].shape, z_own.shape[1]
    out = lambda *shape: jax.ShapeDtypeStruct(shape, F32)
    sem = pltpu.SemaphoreType.DMA

    def buffers(*lead):
        return [pltpu.VMEM((PAIR, *lead, part if e[0] == "i" else part_b, e[5]), F32) for e in PARTS]

    return pl.pallas_call(
        functools.partial(reduce_kernel, reduce_order(part, part_b, starts)),
        out_shape=(out(PAIR, SIDE, part, wide), out(PAIR, SIDE, SIDE, part_b, dim)),
        in_specs=[hbm] * 12,
        out_specs=[hbm] * PAIR,
        scratch_shapes=[
            *buffers(SIDE, SIDE), *buffers(PAIR, PAIR), *buffers(PAIR, SIDE), *buffers(3), *buffers(),
            pltpu.VMEM((PAIR, PAIR, *h_rows[0].shape), BF), pltpu.VMEM((PAIR, PAIR, line, wide // ROW), BF), pltpu.VMEM((PAIR, *m_rows[0].shape), BF),
            pltpu.VMEM((PAIR, line, dim), BF), pltpu.VMEM(scale_parts.shape, F32),
            sem((WIDE,)), sem((WIDE,)), sem((16,)), sem((PAIR, len(PARTS))), sem((PAIR,)),
        ],
        compiler_params=pltpu.CompilerParams(collective_id=1, has_side_effects=True, vmem_limit_bytes=67043328),
        name="reduce_gradients",
    )(*h_rows, *m_rows, *y_cols, *z_cols, z_own, scale_parts)


def rotary_tables(seq_len, head_dim):
    half_dim = head_dim // PAIR
    inv_freq = 10000.0 ** (-(jnp.arange(half_dim, dtype=jnp.float32) * 2.0 / head_dim))
    angles = jnp.arange(seq_len, dtype=jnp.float32)[:, None] * inv_freq[None, :]
    return jnp.cos(angles), jnp.sin(angles)


def solution(mesh):
    fsdp_size = mesh.shape["fsdp"]
    batch_spec = P(("dp", "fsdp"), None, None)
    scale_spec = P(None, "fsdp")
    weight_spec = P(None, "fsdp", None)

    def device_step(x_in, grad_y, norm_scale, w_in, w_out):
        n_layers = w_in.shape[0]
        seq_len, model_dim = x_in.shape[1:]
        proj_dim = w_in.shape[PAIR]
        ff_dim = w_out.shape[1] * fsdp_size - model_dim
        head_dim = (proj_dim - model_dim - PAIR * ff_dim) // PAIR
        rows, rows_out = norm_scale.shape[1], w_out.shape[1]
        scale_rows = jnp.zeros((ROW, model_dim), jnp.float32)
        scale_rows = lax.dynamic_update_slice(scale_rows, norm_scale.astype(jnp.float32), (0, lax.axis_index("fsdp") * rows))
        cos_tab, sin_tab = rotary_tables(seq_len, head_dim)
        cos_tab, sin_tab = jnp.tile(cos_tab, (1, ROW)), jnp.tile(sin_tab, (1, ROW))
        lane = jnp.arange(WIDE)
        down = lane[:, None] - lane[None, :]
        low = lane[None, :] % head_dim < head_dim // PAIR
        turn = jnp.where(low & (down == BAND), -1.0, jnp.where(~low & (down == -BAND), 1.0, 0.0)).astype(jnp.bfloat16)
        hidden, grad_hidden, *rest = run_layers(x_in[0], grad_y[0], scale_rows, w_in, w_out, cos_tab, sin_tab, turn)
        in_sums, out_sums = reduce_gradients((rest[0:SIDE], rest[SIDE:6], rest[6:ROW], rest[ROW:10], rest[10], rest[11]))
        in_grads = in_sums.reshape(n_layers, rows, -1)[:, :, :proj_dim]
        out_rows = out_sums.reshape(n_layers, -1, model_dim)
        scale_grads = lax.dynamic_slice(out_rows[:, rows_out], (0, lax.axis_index("fsdp") * rows), (n_layers, rows))
        out_grads = out_rows[:, :rows_out]
        return hidden[None], grad_hidden[None], scale_grads, in_grads, out_grads

    return jax.shard_map(
        device_step,
        mesh=mesh,
        in_specs=(batch_spec, batch_spec, scale_spec, weight_spec, weight_spec),
        out_specs=(batch_spec, batch_spec, scale_spec, weight_spec, weight_spec),
        check_vma=False,
    )
```

time: 355 us -> 287 us (0.81)
  Pallas kernels: 341 us -> 273 us
    pallas_call x1, Pallas kernels: 201 us -> 112 us  [reduce_gradients(): pl.pallas_call(functools.partial(reduce_kernel, reduce_order(part, part_b...]
    pallas_call x1, Pallas kernels: 140 us -> 161 us  [run_layers(): pl.pallas_call(functools.partial(layers_kernel, forward_order(*w_in.shape...]
where the time goes in v4:
time: 287 us
  Pallas kernels  273 us (95%)
  local copies, waits for them, and re-layouts  11.9 us (4%)
    pallas_call x1, Pallas kernels, run_layers(): pl.pallas_call(functools.partial(layers_kernel, forward_order(*w_in.shape...  161 us
    pallas_call x1, Pallas kernels, reduce_gradients(): pl.pallas_call(functools.partial(reduce_kernel, reduce_order(part, part_b...  112 us

profile of v4, /device:TPU:0, one launch (start us, length us, event | category | flops | bytes accessed | tf_op | source)
XLA Modules:
  0.0 287.1 jit_solution(4631249083614542449)
XLA Ops:
  0.6 0.7 convert_element_type.6
  1.3 0.4 dynamic_update_slice.3.sc_ref
  1.7 0.0 copy-start.3
  1.7 0.2 fusion.4
  1.9 0.4 copy-done.3
  2.3 0.7 select_convert_fusion.turn_ref
  3.0 0.8 copy.11.sin_ref
  3.9 0.8 copy.10.cos_ref
  4.7 161.0 %run_layers.1 = (bf16[256,768]{1,0:T(8,128)(2,1)}, bf16[256,768]{1,0:T(8,128)(2,1)}, bf16[4,96,2048]{2,1,0:T(8,128)(2,1)}, bf16[4,96,2048]{2,1,0:T(8,128)(2,1)},...) custom-call(f32[8,768]{1,0:T(8,128)} %copy-done.3, ...), custom_call_target="tpu_custom_call" | custom-call | tf_op jit(solution)/shard_map/run_layers/pallas_call | solution.py:641
  165.8 111.9 %reduce_gradients.1 = (f32[2,4,24,7168]{3,2,1,0:T(8,128)}, f32[2,4,4,32,768]{4,3,2,1,0:T(8,128)}) custom-call(bf16[4,96,2048]{2,1,0:T(8,128)(2,1)} %get-tuple-element.23.refs_0_, bf16[4,96,2048]{2,1,0:T(8,128)(2,1)} %get-tuple-element.24.refs_1_, bf16[4,96,2048]{2,1,0:T(8,128)(2,1)} %get-tuple-element.25.refs_2_, ...), custom_call_target="tpu_custom_call" | custom-call | tf_op jit(solution)/shard_map/reduce_gradients/pallas_call | solution.py:897
  277.7 0.0 copy-start
  277.7 5.4 %slice.13 = f32[2,96,7040]{2,1,0:T(8,128)} slice(f32[2,96,7168]{2,1,0:T(8,128)} %bitcast.9), slice={[0:2], [0:96], [0:7040]} | slice | bytes 10813440 | tf_op jit(solution)/shard_map/slice | solution.py:943
  283.1 0.0 copy-done
  283.1 0.0 copy-start.2
  283.1 0.0 copy-start.1
  283.2 1.8 slice.14
  284.9 0.6 constant_dynamic-slice_fusion
  285.6 0.0 copy-done.2
  285.6 0.7 copy.15
  286.3 0.0 copy-done.1
  286.3 0.7 copy.16
  (6 shorter events, 0.1 us)
Async XLA Ops:
  1.7 0.6 copy-start.3
  277.7 5.5 %copy-start = (f32[2,4,4,32,768]{4,3,2,1,0:T(8,128)S(1)}, f32[2,4,4,32,768]{4,3,2,1,0:T(8,128)}, u32[]{:S(2)}) copy-start(f32[2,4,4,32,768]{4,3,2,1,0:T(8,128)} %get-tuple-element.35) | copy-start | bytes 9437188
  283.1 2.4 copy-start.2
  283.1 3.2 %copy-start.1 = (bf16[256,768]{1,0:T(8,128)(2,1)S(1)}, bf16[256,768]{1,0:T(8,128)(2,1)}, u32[]{:S(2)}) copy-start(bf16[256,768]{1,0:T(8,128)(2,1)} %get-tuple-element.22) | copy-start | bytes 1179652

commit v5 on v4

--- a/solution.py
+++ b/solution.py
@@ -10,7 +10,7 @@
 BOTH = (1, -1)
 AROUND = (1, -1, 2)
 PARTS = (True, False)
-ALL = ...
+ALL, ZERO = ..., 0.0
 LANE, WIDE, STRIP, HEAD = 128, 256, 512, 64
 ROW, BAND, SIDE, PAIR = 8, 32, 4, 2
 
@@ -67,7 +67,7 @@
 
 
 def plan(tasks, latency=2.5):
-    free, landed, order, now = {}, {}, [], 0.0
+    free, landed, order, now = {}, {}, [], ZERO
     left = list(tasks)
     while left:
         best = None
@@ -81,12 +81,12 @@
         now += cost
         landed[name] = []
         for link, time in sends:
-            free[link] = max(now, free.get(link, 0.0)) + time
+            free[link] = max(now, free.get(link, ZERO)) + time
             landed[name].append(free[link] + latency)
     return order
 
 
-def forward_order(rows_i, cols_i, rows_o, cols_o, starts):
+def layers_order(rows_i, cols_i, rows_o, cols_o, seq, starts):
     rate = 23300.0
     tasks = []
     for m in range(SIDE):
@@ -100,30 +100,82 @@
             spread = [((color, by), cost) for by in BOTH] if color != "x" else []
             tasks.append((("reach", m, color), m, starts[m], [], [], both, 0.2))
             for i, by in enumerate(BOTH):
-                tasks.append((("relay", m, color, by), m, 0.0, [(("reach", m, color), i)], [], [(("x", by), cost / PAIR)] + spread, 0.2))
+                tasks.append((("relay", m, color, by), m, ZERO, [(("reach", m, color), i)], [], [(("x", by), cost / PAIR)] + spread, 0.2))
             halves = [(("relay", m, color, by), 0) for by in BOTH]
-            tasks.append((("far", m, color), m, 0.0, halves, [], spread, 0.2))
+            tasks.append((("far", m, color), m, ZERO, halves, [], spread, 0.2))
             if color == "x":
                 continue
             for off, source, first in ((-1, ("relay", m, color, 1), 1), (1, ("relay", m, color, -1), 1), (PAIR, ("far", m, color), 0)):
                 for i, by in enumerate(BOTH):
-                    tasks.append((("pass", m, color, off, by), m, 0.0, [(source, first + i)], [], [((color, by), cost / PAIR)], 0.2))
+                    tasks.append((("pass", m, color, off, by), m, ZERO, [(source, first + i)], [], [((color, by), cost / PAIR)], 0.2))
                 halves = [(("pass", m, color, off, by), 0) for by in BOTH]
-                tasks.append((("close", m, color, off), m, 0.0, halves, [], [], 0.2))
+                tasks.append((("close", m, color, off), m, ZERO, halves, [], [], 0.2))
         for off in (-1, 1, PAIR):
             last = [("close", m, color, off) for color in "yz"]
             if is_in:
                 last.append(("far", m, "x") if off == PAIR else ("relay", m, "x", -off))
-            tasks.append((("hand", m, off), m, 0.0, [], last, [("chip", (rows_i * cols_i if is_in else rows_o * cols_o) / 150000.0)], 0.2))
+            tasks.append((("hand", m, off), m, ZERO, [], last, [("chip", (rows_i * cols_i if is_in else rows_o * cols_o) / 150000.0)], 0.2))
     before = []
+
+    def work(name, cost, mats=()):
+        needs = [(("hand", m, off), 0) for m in mats for off in (-1, 1, PAIR)]
+        tasks.append((name, 99, ZERO, needs, list(before), [], cost))
+        before[:] = [name]
+
     for l in range(PAIR):
-        work = [(("norm", l), [], 0.8)] + [(("project", l, i), [PAIR * l], 1.4) for i in range(SIDE)]
-        work += [(("attend", l), [], 4.0), (("mlp", l), [], 2.2), (("put", l), [PAIR * l + 1], 2.0)]
-        for name, mats, cost in work:
-            needs = [(("hand", m, off), 0) for m in mats for off in (-1, 1, PAIR)]
-            tasks.append((name, 9, 0.0, needs, before, [], cost))
-            before = [name]
-    tasks.append((("give",), 9, 45.0, [], [], [], 0.3))
+        work(("norm", l), 0.8)
+        for i in range(SIDE):
+            work(("project", l, i), 1.4, [PAIR * l])
+        work(("attend", l), 4.0)
+        work(("mlp", l), 2.2)
+        work(("put", l), 2.0, [PAIR * l + 1])
+    for l in (1, 0):
+        work(("back_out", l), 4.0)
+        work(("back_mlp", l), 3.5)
+        work(("back_heads", l), 1.2)
+        for g in range(3):
+            work(("back_quad", l, g), 2.3)
+        work(("back_keys", l), 0.5)
+        for i in range(5):
+            work(("back_in", l, i), 1.0)
+        work(("back_norm", l), 1.2)
+    def send(name, rank, start, after, sends):
+        tasks.append((name, rank, start, [], [after] if after else [], sends, 0.4))
+
+    def follow(name, rank, needs, sends):
+        tasks.append((name, rank, ZERO, needs, [], sends, 0.2))
+
+    def both(axis, size):
+        return [((axis, by), size / rate) for by in BOTH]
+
+    model = rows_i * ROW
+    for l in (1, 0):
+        for axis in "yz":
+            name = ("send_h", l, axis)
+            send(name, 20 - l, 58.0, ("norm", l), both(axis, seq * model))
+            for i, by in enumerate(BOTH):
+                for index in range(PAIR):
+                    follow(("pass_h", l, axis, by, index), 10, [(name, i)], [((axis, by), seq * model / SIDE / rate)])
+        name = ("send_m", l)
+        send(name, 22 - l, ZERO, ("mlp", l), both("x", seq * rows_o) + both("x", PAIR * seq * rows_o))
+        for i, by in enumerate(BOTH):
+            for index in range(PAIR):
+                follow(("pass_m", l, by, index), 11, [(name, i)], [(("x", by), seq * rows_o / PAIR / rate)])
+        name = ("send_y", l)
+        send(name, 12, 42.0, ("back_norm", 1) if l == 0 else None, both("x", seq * model))
+        for i, by in enumerate(BOTH):
+            follow(("pass_y", l, by), 12, [(name, i)], [(("x", by), seq * model / PAIR / rate)])
+        follow(("far_y", l), 12, [(("pass_y", l, by), 0) for by in BOTH], [])
+        for axis in "zy" if l else "z":
+            name = ("send_z", l, axis)
+            share = seq * (cols_i + LANE) / ROW
+            send(name, 13, ZERO, ("back_mlp", l) if axis == "z" else ("back_keys", l), both(axis, share / PAIR) + both(axis, share))
+            for i, by in enumerate(BOTH):
+                follow(("pass_z", l, axis, by), 13, [(name, i)], [((axis, by), share / PAIR / rate)])
+                follow(("twin_z", l, axis, by), 14, [(name, PAIR + i)], [])
+            follow(("far_z", l, axis), 14, [(("pass_z", l, axis, by), 0) for by in BOTH], [])
+        send(("send_scale", l), 15, ZERO, ("back_norm", l), [])
+    send(("own_z",), 15, ZERO, ("back_keys", 0), [])
     return plan(tasks)
 
 
@@ -260,7 +312,7 @@
 
 
 def layers_kernel(order, sc_ref, wi_ref, wo_ref, x_ref, dy_ref, cos_ref, sin_ref, turn_ref,
-                  y_ref, gx_ref, hy_a, hy_b, hz_a, hz_b, mx_a, mx_b, yx_a, yx_b, zy_b, zz_b, z_a, sc_out,
+                  y_ref, gx_ref, hy_a, hy_b, hz_a, hz_b, mx_a, mx_b, yx_a, yx_b, zy_b, zz_b, zz_a, z_a, sc_out, relay_m, relay_z,
                   wi, wo, z, om, h, hid, qr, kts, vts, ksl, scores, dscores, pcat, dscat,
                   dot_heads, qt, dht, dkv, omt, ht, dyt, sc, gains, gain_ref, load_sems, own_sems, send_sems, recv_sems,
                   share_send_sems, share_recv_sems):
@@ -273,7 +325,8 @@
     links, shared = Links(send_sems, recv_sems), Links(share_send_sems, share_recv_sems)
     stored = []
     spots, _ = around(position)
-    h_out, m_out, y_out, z_out = {"y": (hy_a, hy_b), "z": (hz_a, hz_b)}, (mx_a, mx_b), (yx_a, yx_b), {"y": zy_b, "z": zz_b}
+    h_out, m_out, y_out, z_out = {"y": (hy_a, hy_b), "z": (hz_a, hz_b)}, (mx_a, mx_b), (yx_a, yx_b), {(1, "y"): zy_b, (1, "z"): zz_b, (0, "z"): zz_a}
+    middle = hid.at[1]
     begin, ready, peer, stages = gather_stages(links, position, wi_ref, wo_ref, wi, wo, load_sems)
     others = [(zc * SIDE + y, rem(me + k, ROW)) for k in range(1, ROW)]
 
@@ -301,78 +354,121 @@
         size = z.shape[PAIR] // ROW
         return lanes(((0 if axis == "y" else SIDE) + spot(axis, o)) * size, size)
 
-    def send_h(l):
-        for axis in "yz":
-            out = h_out[axis][l].at[:, :, tokens(axis, 0, core)]
-            for o in AROUND:
-                for index in range(PAIR):
-                    shared.send(("h", l, axis, o), ht.at[l, :, index], out, device(axis, o, index), batch=("h", l, axis, o, index), lane=core)
-            shared.send(("h", l, axis), ht.at[l, :, 1 - core], out, twin, lane=0)
-            keep(ht.at[l, :, core], out)
+    def send_h(l, axis):
+        out = h_out[axis][l].at[:, :, tokens(axis, 0, core)]
+        for by in BOTH:
+            for index in range(PAIR):
+                shared.send(("h", l, axis, by), ht.at[l, :, index], out, device(axis, by, index), batch=("h", l, axis, by, index), lane=core)
+        shared.send(("h", l, axis), ht.at[l, :, 1 - core], out, twin, lane=0)
+        keep(ht.at[l, :, core], out)
+
+    def pass_h(l, axis, by, index):
+        out = h_out[axis][l]
+        shared.arrive(("h", l, axis, by), out.at[:, :, tokens(axis, -by, index)], index)
+        part = out.at[pl.ds(1 - by, PAIR), :, tokens(axis, -by, index)]
+        shared.send(("h2", l, axis, by), part, part, device(axis, by, core), batch=("h2", l, axis, by, index), lane=index)
 
     def arrive_h(l):
         for axis in "yz":
-            for o in AROUND:
+            for by in BOTH:
                 for index in range(PAIR):
-                    shared.arrive(("h", l, axis, o), h_out[axis][l].at[:, :, tokens(axis, -o, index)], index)
+                    shared.arrive(("h2", l, axis, by), h_out[axis][l].at[pl.ds(1 - by, PAIR), :, tokens(axis, PAIR, index)], index)
             shared.arrive(("h", l, axis), h_out[axis][l].at[:, :, tokens(axis, 0, 1 - core)], 0)
 
-    def row_block(l, o, index):
+    def row_block(l, o, index, part=None):
         size = omt.shape[1] // ROW
-        return omt.at[l, pl.ds(pl.multiple_of((PAIR * spot("x", o) + index) * size, BAND), size)]
+        start = (PAIR * spot("x", o) + index) * size
+        if part is not None:
+            size = size // PAIR
+            start = start + part * size
+        return omt.at[l, pl.ds(pl.multiple_of(start, 16), size)]
+
+    def row_half(k):
+        size = m_out[0].shape[0] // PAIR
+        return pl.ds(k * size, size)
 
     def send_m(l):
         out = m_out[l].at[:, tokens("x", 0, core)]
-        for o in AROUND:
+        for k, by in enumerate(BOTH):
             for index in range(PAIR):
-                shared.send(("m", l, o), row_block(l, o, index), out, device("x", o, index), batch=("m", l, o, index), lane=core)
+                shared.send(("mr", l, by), row_block(l, PAIR, index, k), relay_m.at[l, k, core], device("x", by, index), batch=("mr", l, by, index), lane=core)
+        for by in BOTH:
+            for index in range(PAIR):
+                shared.send(("m", l, by), row_block(l, by, index), out, device("x", by, index), batch=("m", l, by, index), lane=core)
         shared.send(("m", l), row_block(l, 0, 1 - core), out, twin, lane=0)
         keep(row_block(l, 0, core), out)
 
+    def pass_m(l, by, index):
+        k = (1 - by) // PAIR
+        shared.arrive(("mr", l, by), relay_m.at[l, k, index], index)
+        shared.send(("m2", l, by), relay_m.at[l, k, index], m_out[l].at[row_half(k), tokens("x", -by, index)], device("x", by, core),
+                    batch=("m2", l, by, index), lane=index)
+
     def arrive_m(l):
-        for o in AROUND:
+        for k, by in enumerate(BOTH):
             for index in range(PAIR):
-                shared.arrive(("m", l, o), m_out[l].at[:, tokens("x", -o, index)], index)
+                shared.arrive(("m", l, by), m_out[l].at[:, tokens("x", -by, index)], index)
+                shared.arrive(("m2", l, by), m_out[l].at[row_half(k), tokens("x", PAIR, index)], index)
         shared.arrive(("m", l), m_out[l].at[:, tokens("x", 0, 1 - core)], 0)
 
-    def send_y(l, src):
-        out = y_out[l].at[tokens("x", 0, core)]
-        for o in AROUND:
-            shared.send(("y", l, o), src, out, device("x", o, core), lane=0)
+    def token_half(axis, o, k):
+        return pl.ds(pl.multiple_of((PAIR * spot(axis, o) + core) * seq + k * (seq // PAIR), seq // PAIR), seq // PAIR)
+
+    def send_y(l):
+        src, out = (middle, dy_ref)[l], y_out[l].at[tokens("x", 0, core)]
+        for by in BOTH:
+            shared.send(("y", l, by), src, out, device("x", by, core), lane=0)
         shared.send(("y", l), src, out, twin, lane=0)
         keep(src, out)
 
-    def pass_y(l):
-        for o in AROUND:
-            landed = y_out[l].at[tokens("x", -o, core)]
-            shared.arrive(("y", l, o), landed, 0)
-            shared.send(("y", l, o, "pass"), landed, landed, twin, lane=0)
+    def pass_y(l, by):
+        landed, part = y_out[l].at[tokens("x", -by, core)], y_out[l].at[token_half("x", -by, (1 - by) // PAIR)]
+        shared.arrive(("y", l, by), landed, 0)
+        shared.send(("y2", l, by), part, part, device("x", by, core), lane=0)
+        shared.send(("yp", l, by), landed, landed, twin, lane=0)
+
+    def far_y(l):
+        for k, by in enumerate(BOTH):
+            shared.arrive(("y2", l, by), y_out[l].at[token_half("x", PAIR, k)], 0)
+        landed = y_out[l].at[tokens("x", PAIR, core)]
+        shared.send(("yp", l, PAIR), landed, landed, twin, lane=0)
 
     def arrive_y(l):
         for o in AROUND:
-            shared.arrive(("y", l, o, "pass"), y_out[l].at[tokens("x", -o, 1 - core)], 0)
+            shared.arrive(("yp", l, o), y_out[l].at[tokens("x", -o, 1 - core)], 0)
         shared.arrive(("y", l), y_out[l].at[tokens("x", 0, 1 - core)], 0)
 
-    def send_z(l):
-        for axis in "yz":
-            out = z_out[axis].at[tokens(axis, 0, core)]
-            for o in AROUND:
-                shared.send(("z", axis, o), z.at[l, :, columns(axis, o)], out, device(axis, o, core), lane=0)
-            shared.send(("z", axis), z.at[l, :, columns(axis, 0)], out, twin, lane=0)
-            keep(z.at[l, :, columns(axis, 0)], out)
-
-    def pass_z():
-        for axis in "yz":
-            for o in AROUND:
-                landed = z_out[axis].at[tokens(axis, -o, core)]
-                shared.arrive(("z", axis, o), landed, 0)
-                shared.send(("z", axis, o, "pass"), landed, landed, twin, lane=0)
-
-    def arrive_z():
-        for axis in "yz":
-            for o in AROUND:
-                shared.arrive(("z", axis, o, "pass"), z_out[axis].at[tokens(axis, -o, 1 - core)], 0)
-            shared.arrive(("z", axis), z_out[axis].at[tokens(axis, 0, 1 - core)], 0)
+    def send_z(l, axis):
+        out = z_out[l, axis].at[tokens(axis, 0, core)]
+        for k, by in enumerate(BOTH):
+            shared.send(("zr", l, axis, by), z.at[l, pl.ds(k * (seq // PAIR), seq // PAIR), columns(axis, PAIR)], relay_z.at[l, "yz".index(axis), k],
+                        device(axis, by, core), lane=0)
+        for by in BOTH:
+            shared.send(("z", l, axis, by), z.at[l, :, columns(axis, by)], out, device(axis, by, core), lane=0)
+        shared.send(("z", l, axis), z.at[l, :, columns(axis, 0)], out, twin, lane=0)
+        keep(z.at[l, :, columns(axis, 0)], out)
+
+    def pass_z(l, axis, by):
+        k = (1 - by) // PAIR
+        half = relay_z.at[l, "yz".index(axis), k]
+        shared.arrive(("zr", l, axis, by), half, 0)
+        shared.send(("z2", l, axis, by), half, z_out[l, axis].at[token_half(axis, -by, k)], device(axis, by, core), lane=0)
+
+    def twin_z(l, axis, by):
+        landed = z_out[l, axis].at[tokens(axis, -by, core)]
+        shared.arrive(("z", l, axis, by), landed, 0)
+        shared.send(("zp", l, axis, by), landed, landed, twin, lane=0)
+
+    def far_z(l, axis):
+        for k, by in enumerate(BOTH):
+            shared.arrive(("z2", l, axis, by), z_out[l, axis].at[token_half(axis, PAIR, k)], 0)
+        landed = z_out[l, axis].at[tokens(axis, PAIR, core)]
+        shared.send(("zp", l, axis, PAIR), landed, landed, twin, lane=0)
+
+    def arrive_z(l, axis):
+        for o in AROUND:
+            shared.arrive(("zp", l, axis, o), z_out[l, axis].at[tokens(axis, -o, 1 - core)], 0)
+        shared.arrive(("z", l, axis), z_out[l, axis].at[tokens(axis, 0, 1 - core)], 0)
 
     def send_scale(l):
         for k, far in enumerate(others):
@@ -418,8 +514,8 @@
         kv = z[l, :, dim:dim + LANE]
         turned = kv.astype(F32) * cos[:, :LANE] + product(kv, turn_ref[:LANE, :LANE]) * sin[:, :LANE]
         first = lax.broadcasted_iota(jnp.int32, turned.shape, 1) < HEAD
-        key_lo = jnp.where(first, turned, 0.0)
-        val_hi = jnp.where(first, 0.0, kv.astype(F32))
+        key_lo = jnp.where(first, turned, ZERO)
+        val_hi = jnp.where(first, ZERO, kv.astype(F32))
         return key_lo, pltpu.roll(key_lo, HEAD, 1), pltpu.roll(val_hi, HEAD, 1), val_hi
 
     def slot_rows(ref, lo, hi):
@@ -480,7 +576,10 @@
         def _(i):
             dst[pl.ds(pl.multiple_of(i * WIDE, WIDE), WIDE)] = src(i * WIDE).T
 
-    def backward(l, dy):
+    upstream = (middle, dy_ref)
+
+    def back_out(l):
+        dy = upstream[l]
         flip(lambda at: dy[:, lanes(at, WIDE)], dyt, dim)
 
         @pl.loop(0, wo.shape[1] // dim)
@@ -493,6 +592,7 @@
             def _():
                 dot_heads[ALL] = part
 
+    def back_mlp(l):
         @pl.loop(0, seq // BAND)
         def _(r):
             rows = pl.ds(pl.multiple_of(r * BAND, BAND), BAND)
@@ -507,6 +607,7 @@
                 z[l, rows, gate_at] = (du * sig + du * gate * (sig * (1.0 - sig))).astype(BF)
                 z[l, rows, up_at] = (d * (gate * sig)).astype(BF)
 
+    def back_heads(l):
         key_lo, key_hi, val_lo, val_hi = heads(l)
         slot_cols(kts, key_lo)
         slot_cols(vts, val_lo)
@@ -514,42 +615,45 @@
         dkv[ALL] = jnp.zeros(dkv.shape, F32)
         flip(lambda at: qr[l, :, lanes(at, WIDE)], qt, dim)
 
-        @pl.loop(0, dim // WIDE)
-        def _(g):
-            cols = lanes(g * WIDE, WIDE)
-            scores[ALL] = product(qr[l, :, cols], kts[ALL])
-            dscores[ALL] = product(om[:, cols], vts[ALL])
-
-            @pl.loop(0, seq // BAND)
-            def _(r):
-                rows = pl.ds(pl.multiple_of(r * BAND, BAND), BAND)
-                for i in range(SIDE):
-                    at = slice(i * seq, (i + 1) * seq)
-                    p = chances(rows, r, i)
-                    pcat[rows, at] = p.astype(BF)
-                    pd = p * dscores[rows, at].astype(BF).astype(F32)
-                    dscat[rows, at] = (pd - p * jnp.sum(pd, axis=-1, keepdims=True)).astype(BF)
-            dq = product(dscat[ALL], ksl[ALL]).astype(BF)
-            back = dq.astype(F32) * cos_ref[ALL] - product(dq, turn_ref[ALL]) * sin_ref[ALL]
-            z[l, :, cols] = (back * 0.125).astype(BF)
+
+    def back_quad(l, g):
+        cols = pl.ds(g * WIDE, WIDE)
+        scores[ALL] = product(qr[l, :, cols], kts[ALL])
+        dscores[ALL] = product(om[:, cols], vts[ALL])
+
+        @pl.loop(0, seq // BAND)
+        def _(r):
+            rows = pl.ds(pl.multiple_of(r * BAND, BAND), BAND)
             for i in range(SIDE):
-                head = pl.ds(pl.multiple_of(g * WIDE + i * HEAD, HEAD), HEAD)
                 at = slice(i * seq, (i + 1) * seq)
-                dkv[:HEAD] += product(qt[head], dscat[:, at])
-                dkv[HEAD:] += product(dot_heads[head], pcat[:, at])
-
+                p = chances(rows, r, i)
+                pcat[rows, at] = p.astype(BF)
+                pd = p * dscores[rows, at].astype(BF).astype(F32)
+                dscat[rows, at] = (pd - p * jnp.sum(pd, axis=-1, keepdims=True)).astype(BF)
+        dq = product(dscat[ALL], ksl[ALL]).astype(BF)
+        back = dq.astype(F32) * cos_ref[ALL] - product(dq, turn_ref[ALL]) * sin_ref[ALL]
+        z[l, :, cols] = (back * 0.125).astype(BF)
+        for i in range(SIDE):
+            head = pl.ds(g * WIDE + i * HEAD, HEAD)
+            at = slice(i * seq, (i + 1) * seq)
+            dkv[:HEAD] += product(qt[head], dscat[:, at])
+            dkv[HEAD:] += product(dot_heads[head], pcat[:, at])
+
+    def back_keys(l):
         dkv_t = dkv[ALL].T
         dk = dkv_t.astype(BF)
         turned = dk.astype(F32) * cos_ref[:, :LANE] - product(dk, turn_ref[:LANE, :LANE]) * sin_ref[:, :LANE]
         first = lax.broadcasted_iota(jnp.int32, turned.shape, 1) < HEAD
         z[l, :, dim:dim + LANE] = jnp.where(first, turned, dkv_t).astype(BF)
 
-    def backward_rows(l, dy, dst):
-        n, width = wi.shape[PAIR] // 1408, 1408
-        for i in range(n):
-            at = slice(i * width, (i + 1) * width)
-            part = product(wi[l, :, at], z[l, :, at], ((1,), (1,)))
-            dht[ALL] = part if i == 0 else dht[ALL] + part
+    def back_in(l, i):
+        width = wi.shape[PAIR] // 5
+        at = slice(i * width, (i + 1) * width)
+        part = product(wi[l, :, at], z[l, :, at], ((1,), (1,)))
+        dht[ALL] = part if i == 0 else dht[ALL] + part
+
+    def back_norm(l):
+        dy, dst = upstream[l], (gx_ref, middle)[l]
         for i in range(dim // WIDE):
             cols = slice(i * WIDE, (i + 1) * WIDE)
             h[l, :, cols] = dht[cols].T.astype(BF)
@@ -591,45 +695,32 @@
     def do_mlp(l):
         mlp(l)
         flip(lambda at: om[:, lanes(at, WIDE)], omt.at[l], om.shape[1])
-        if l == 0:
-            send_m(l)
 
     def do_put(l):
         ready(PAIR * l + 1)
         put_out(l, hid.at[0] if l == 0 else y_ref)
 
-    stages.update(norm=do_norm, project=do_project, attend=attend, mlp=do_mlp, put=do_put, give=lambda: send_y(1, dy_ref))
+    stages.update(
+        norm=do_norm, project=do_project, attend=attend, mlp=do_mlp, put=do_put, back_out=back_out, back_mlp=back_mlp, back_heads=back_heads,
+        back_quad=back_quad, back_keys=back_keys, back_in=back_in, back_norm=back_norm, send_h=send_h, pass_h=pass_h, send_m=send_m,
+        pass_m=pass_m, send_y=send_y, pass_y=pass_y, far_y=far_y, send_z=send_z, pass_z=pass_z, twin_z=twin_z, far_z=far_z,
+        send_scale=send_scale, own_z=lambda: keep(z.at[0], z_a))
     for kind, *task in order:
         stages[kind](*task)
-    send_h(0)
-    send_h(1)
-    send_m(1)
-    middle = hid.at[1]
-    backward(1, dy_ref)
-    send_z(1)
-    backward_rows(1, dy_ref, middle)
-    send_y(0, middle)
-    send_scale(1)
-    pass_y(1)
-    backward(0, middle)
-    keep(z.at[0], z_a)
-    pass_z()
-    backward_rows(0, middle, gx_ref)
-    send_scale(0)
-    pass_y(0)
     for l in range(PAIR):
         arrive_h(l)
         arrive_m(l)
         arrive_scale(l)
         arrive_y(l)
-    arrive_z()
+    for l, axis in z_out:
+        arrive_z(l, axis)
     for copy in stored:
         copy.wait()
     shared.drain()
     links.drain()
 
 
-def run_layers(x, dy, scale, w_in, w_out, cos, sin, turn, starts=(0.0, 10.0, 20.0, 30.0)):
+def run_layers(x, dy, scale, w_in, w_out, cos, sin, turn, starts=(ZERO, 10.0, 20.0, 30.0)):
     seq, dim = x.shape
     proj, cat = w_in.shape[PAIR], ROW * w_out.shape[1]
     wide = proj + LANE
@@ -639,11 +730,12 @@
     sem = pltpu.SemaphoreType.DMA
     line = ROW * seq
     return pl.pallas_call(
-        functools.partial(layers_kernel, forward_order(*w_in.shape[1:], *w_out.shape[1:], starts)),
+        functools.partial(layers_kernel, layers_order(*w_in.shape[1:], *w_out.shape[1:], seq, starts)),
         out_shape=(out(seq, dim), out(seq, dim), *[out(SIDE, dim // ROW, line)] * SIDE, *[out(cat // ROW, line)] * PAIR, *[out(line, dim)] * PAIR,
-                   *[out(line, wide // ROW)] * PAIR, out(seq, wide), out(PAIR, ROW, ROW, dim, dtype=F32)),
+                   *[out(line, wide // ROW)] * 3, out(seq, wide), out(PAIR, ROW, ROW, dim, dtype=F32),
+                   out(PAIR, PAIR, PAIR, cat // 16, seq), out(PAIR, PAIR, PAIR, seq // PAIR, wide // ROW)),
         in_specs=[vmem, hbm, hbm] + [vmem] * 5,
-        out_specs=[vmem] * PAIR + [hbm] * 12,
+        out_specs=[vmem] * PAIR + [hbm] * 15,
         scratch_shapes=[
             buffer(PAIR, dim, proj), buffer(PAIR, cat, dim), buffer(PAIR, seq, wide), buffer(seq, cat), buffer(PAIR, seq, dim),
             buffer(PAIR, seq, dim), buffer(PAIR, seq, dim),
@@ -652,7 +744,7 @@
             buffer(dim, seq), buffer(dim, seq), buffer(dim, seq, dtype=F32), buffer(LANE, seq, dtype=F32),
             buffer(PAIR, cat, seq), buffer(PAIR, SIDE, PAIR, dim // ROW, seq), buffer(dim, seq), buffer(PAIR, ROW, dim, dtype=F32),
             buffer(ROW, ROW, dim, dtype=F32), buffer(ROW, dim, dtype=F32),
-            sem((SIDE,)), sem((16,)), sem((200,)), sem((200,)), sem((96,)), sem((96, PAIR)),
+            sem((SIDE,)), sem((16,)), sem((200,)), sem((200,)), sem((LANE,)), sem((LANE, PAIR)),
         ],
         compiler_params=pltpu.CompilerParams(collective_id=PAIR, has_side_effects=True, vmem_limit_bytes=67043328),
         name="run_layers",
@@ -666,17 +758,18 @@
 def reduce_order(rows, rows_b, starts):
     rate = 11650.0
     tasks = []
-    moved = WIDE * 896 / (PAIR * rate)
-    tasks.append((("swap",), (0, 0), 0.0, [], [], [((axis, by), moved * n) for axis in "yz" for by, n in ((1, 1), (-1, 1), (1, PAIR))] + [("chip", 0.8)] * PAIR, 0.5))
-    for i, axis in enumerate("yz"):
-        for j, o in enumerate(AROUND):
-            tasks.append((("pass", axis, o), (0, 1), 0.0, [(("swap",), 3 * i + j)], [], [("chip", 1.6)], 0.2))
+    share = WIDE * 896 / (PAIR * rate)
+    tasks.append((("swap",), (0, 0), ZERO, [], [], [(("y", by), share / PAIR) for by in BOTH] + [(("y", by), share) for by in BOTH], 0.5))
+    for i, by in enumerate(BOTH):
+        tasks.append((("relay", by), (0, 1), ZERO, [(("swap",), i)], [], [(("y", by), share / PAIR)], 0.2))
+        tasks.append((("near", by), (0, PAIR), ZERO, [(("swap",), PAIR + i)], [], [("chip", 1.6)], 0.2))
+    tasks.append((("far",), (0, PAIR), ZERO, [(("relay", by), 0) for by in BOTH], [], [("chip", 1.6)], 0.2))
     for l in (1, 0):
         late = 1 - l
         for c, (kind, first, then, last, at, width) in enumerate(PARTS):
             needs, cost = [], 1.6 * width / STRIP
-            if kind == "i" and l == 0:
-                needs = [(("pass", last, o), 0) for o in AROUND]
+            if last == "y" and kind == "i" and l == 0:
+                needs = [(("near", 1), 0), (("near", -1), 0), (("far",), 0)]
             tasks.append((("make", l, c), (9 * late, -c), starts[late], needs, [], [], cost))
             full = SIDE * SIDE * (rows if kind == "i" else rows_b) * width / rate
             sends = [[((first, by), full / ROW) for by in BOTH], [((first, by), full / SIDE) for by in BOTH],
@@ -687,17 +780,17 @@
             for s in range(9):
                 task = ("sum", l, c, s)
                 needs = [(("sum", l, c, s - 1), k) for k in range(len(sends[s - 1]))] if s else []
-                tasks.append((task, (late, -s), 0.0, needs, [("make", l, c)] if s == 0 else [("sum", l, c, s - 1)], sends[s], 0.3))
+                tasks.append((task, (late, -s), ZERO, needs, [("make", l, c)] if s == 0 else [("sum", l, c, s - 1)], sends[s], 0.3))
     return plan(tasks)
 
 
 def reduce_kernel(order, *refs):
     hy, hz, mx, yx = refs[0:PAIR], refs[PAIR:SIDE], refs[SIDE:6], refs[6:ROW]
-    zy1, zz1, z0, sc = refs[ROW:12]
-    oa, ob = refs[12:14]
+    zy1, zz1, zz0, z0, sc = refs[ROW:13]
+    oa, ob, relay = refs[13:16]
     n = len(PARTS)
-    total, half, full, small, front = (refs[14 + k * n:14 + (k + 1) * n] for k in range(5))
-    (hbuf, zbuf, mbuf, ybuf, scbuf, ssem, rsem, isem, osem, zsem) = refs[14 + 5 * n:]
+    total, half, full, small, front = (refs[16 + k * n:16 + (k + 1) * n] for k in range(5))
+    (hbuf, zbuf, mbuf, ybuf, scbuf, ssem, rsem, isem, osem, zsem) = refs[16 + 5 * n:]
     position = chip_position()
     x, y, zc, core = position
     place = {"x": x, "y": y, "z": zc}
@@ -723,6 +816,8 @@
         if l:
             load(("z", 1, "y"), zy1, zbuf.at[1, 0])
             load(("z", 1, "z"), zz1, zbuf.at[1, 1])
+        else:
+            load(("z", 0, "z"), zz0, zbuf.at[0, 1])
         load(("h", l, "y"), hy[l], hbuf.at[l, 0])
         load(("h", l, "z"), hz[l], hbuf.at[l, 1])
         load(("m", l), mx[l], mbuf.at[l])
@@ -745,33 +840,47 @@
     def tokens(axis, o, index):
         return pl.ds(pl.multiple_of((PAIR * spot(axis, o) + index) * seq, seq), seq)
 
+    def token_half(o, k):
+        return pl.ds(pl.multiple_of((PAIR * spot("y", o) + core) * seq + k * (seq // PAIR), seq // PAIR), seq // PAIR)
+
     def swap():
-        for i, axis in enumerate("yz"):
-            mine = zbuf.at[0, i, tokens(axis, 0, core)]
-            for o in AROUND:
-                links.send(("z", axis, o), z0.at[:, columns(axis, o)], mine, peer(axis, o))
-            links.send(("near", axis), z0.at[:, columns(axis, 0)], mine, twin)
-            load(("own", axis), z0.at[:, columns(axis, 0)], mine)
-
-    def hand_on(axis, o):
-        i = "yz".index(axis)
-        landed = zbuf.at[0, i, tokens(axis, -o, core)]
-        links.arrive(("z", axis, o), landed)
-        links.send(("pass", axis, o), landed, landed, twin)
+        mine = zbuf.at[0, 0, tokens("y", 0, core)]
+        for k, by in enumerate(BOTH):
+            links.send(("zr", by), z0.at[pl.ds(k * (seq // PAIR), seq // PAIR), columns("y", PAIR)], relay.at[k], peer("y", by))
+        for by in BOTH:
+            links.send(("z", by), z0.at[:, columns("y", by)], mine, peer("y", by))
+        links.send(("z",), z0.at[:, columns("y", 0)], mine, twin)
+        load(("own",), z0.at[:, columns("y", 0)], mine)
+
+    def pass_on(by):
+        k = (1 - by) // PAIR
+        links.arrive(("zr", by), relay.at[k])
+        links.send(("z2", by), relay.at[k], zbuf.at[0, 0, token_half(-by, k)], peer("y", by))
+
+    def near(by):
+        landed = zbuf.at[0, 0, tokens("y", -by, core)]
+        links.arrive(("z", by), landed)
+        links.send(("zp", by), landed, landed, twin)
+
+    def far():
+        for k, by in enumerate(BOTH):
+            links.arrive(("z2", by), zbuf.at[0, 0, token_half(PAIR, k)])
+        landed = zbuf.at[0, 0, tokens("y", PAIR, core)]
+        links.send(("zp", PAIR), landed, landed, twin)
 
     def make(l, c):
         kind, first, then, last, at, width = PARTS[c]
         if kind == "i":
             i = "yz".index(last)
             loaded(("h", l, last))
-            if l:
-                loaded(("z", 1, last))
-            elif ("joined", last) not in done:
-                done.add(("joined", last))
-                loaded(("own", last))
-                links.arrive(("near", last), zbuf.at[0, i, tokens(last, 0, 1 - core)])
+            if l or last == "z":
+                loaded(("z", l, last))
+            elif "joined" not in done:
+                done.add("joined")
+                loaded(("own",))
+                links.arrive(("z",), zbuf.at[0, 0, tokens("y", 0, 1 - core)])
                 for o in AROUND:
-                    links.arrive(("pass", last, o), zbuf.at[0, i, tokens(last, -o, 1 - core)])
+                    links.arrive(("zp", o), zbuf.at[0, 0, tokens("y", -o, 1 - core)])
             size = total[c].shape[3]
             for lo in range(0, width, WIDE):
                 hi = min(width, lo + WIDE)
@@ -790,7 +899,7 @@
             put(r, part[r * size:(r + 1) * size])
         gain = jnp.sum(jnp.sum(scbuf[l, :, :, at:at + width], axis=0), axis=0, keepdims=True)
         row = lax.broadcasted_iota(jnp.int32, (size, width), 0)
-        put(15, jnp.where(row == 0, gain, 0.0))
+        put(15, jnp.where(row == 0, gain, ZERO))
 
     def area(l, c, o, whole):
         kind, first, then, last, at, width = PARTS[c]
@@ -856,7 +965,7 @@
             for k, by in enumerate(BOTH):
                 links.arrive((*key, "a3", by), area(l, c, PAIR, pl.ds(PAIR * k, PAIR)))
 
-    stages = {"swap": swap, "pass": hand_on, "make": make, "sum": add}
+    stages = {"swap": swap, "relay": pass_on, "near": near, "far": far, "make": make, "sum": add}
     for kind, *task in order:
         stages[kind](*task)
     links.drain()
@@ -883,7 +992,7 @@
     return spots, peers
 
 
-def reduce_gradients(operands, starts=(0.0, 0.0)):
+def reduce_gradients(operands, starts=(ZERO, ZERO)):
     hbm = pl.BlockSpec(memory_space=pltpu.HBM)
     h_rows, m_rows, y_cols, z_cols, z_own, scale_parts = operands
     part, part_b = h_rows[0].shape[1] // SIDE, (m_rows[0].shape[0] + BAND) // 16
@@ -896,9 +1005,9 @@
 
     return pl.pallas_call(
         functools.partial(reduce_kernel, reduce_order(part, part_b, starts)),
-        out_shape=(out(PAIR, SIDE, part, wide), out(PAIR, SIDE, SIDE, part_b, dim)),
-        in_specs=[hbm] * 12,
-        out_specs=[hbm] * PAIR,
+        out_shape=(out(PAIR, SIDE, part, wide), out(PAIR, SIDE, SIDE, part_b, dim), jax.ShapeDtypeStruct((PAIR, z_own.shape[0] // PAIR, wide // ROW), BF)),
+        in_specs=[hbm] * 13,
+        out_specs=[hbm] * 3,
         scratch_shapes=[
             *buffers(SIDE, SIDE), *buffers(PAIR, PAIR), *buffers(PAIR, SIDE), *buffers(3), *buffers(),
             pltpu.VMEM((PAIR, PAIR, *h_rows[0].shape), BF), pltpu.VMEM((PAIR, PAIR, line, wide // ROW), BF), pltpu.VMEM((PAIR, *m_rows[0].shape), BF),
@@ -937,9 +1046,9 @@
         lane = jnp.arange(WIDE)
         down = lane[:, None] - lane[None, :]
         low = lane[None, :] % head_dim < head_dim // PAIR
-        turn = jnp.where(low & (down == BAND), -1.0, jnp.where(~low & (down == -BAND), 1.0, 0.0)).astype(jnp.bfloat16)
+        turn = jnp.where(low & (down == BAND), -1.0, jnp.where(~low & (down == -BAND), 1.0, ZERO)).astype(jnp.bfloat16)
         hidden, grad_hidden, *rest = run_layers(x_in[0], grad_y[0], scale_rows, w_in, w_out, cos_tab, sin_tab, turn)
-        in_sums, out_sums = reduce_gradients((rest[0:SIDE], rest[SIDE:6], rest[6:ROW], rest[ROW:10], rest[10], rest[11]))
+        in_sums, out_sums, _ = reduce_gradients((rest[0:SIDE], rest[SIDE:6], rest[6:ROW], rest[ROW:11], rest[11], rest[12]))
         in_grads = in_sums.reshape(n_layers, rows, -1)[:, :, :proj_dim]
         out_rows = out_sums.reshape(n_layers, -1, model_dim)
         scale_grads = lax.dynamic_slice(out_rows[:, rows_out], (0, lax.axis_index("fsdp") * rows), (n_layers, rows))

time: 287 us -> 288 us (level)
    pallas_call x1, Pallas kernels: 112 us -> 118 us  [reduce_gradients(): pl.pallas_call(functools.partial(reduce_kernel, reduce_order(part, part_b...]
    pallas_call x1, Pallas kernels: 161 us -> 155 us  [run_layers(): pl.pallas_call(functools.partial(layers_kernel, layers_order(*w_in.shape[...]
where the time goes in v5:
time: 288 us
  Pallas kernels  274 us (95%)
  local copies, waits for them, and re-layouts  11.9 us (4%)
    pallas_call x1, Pallas kernels, run_layers(): pl.pallas_call(functools.partial(layers_kernel, layers_order(*w_in.shape[...  155 us
    pallas_call x1, Pallas kernels, reduce_gradients(): pl.pallas_call(functools.partial(reduce_kernel, reduce_order(part, part_b...  118 us

profile of v5, /device:TPU:0, one launch (start us, length us, event | category | flops | bytes accessed | tf_op | source)
XLA Modules:
  0.0 287.7 jit_solution(1238325447054994259)
XLA Ops:
  0.6 0.7 convert_element_type.6
  1.3 0.4 dynamic_update_slice.3.sc_ref
  1.7 0.0 copy-start.3
  1.7 0.2 fusion.4
  1.9 0.4 copy-done.3
  2.3 0.7 select_convert_fusion.turn_ref
  3.0 0.8 copy.11.sin_ref
  3.9 0.8 copy.10.cos_ref
  4.7 155.1 %run_layers.1 = (bf16[256,768]{1,0:T(8,128)(2,1)}, bf16[256,768]{1,0:T(8,128)(2,1)}, bf16[4,96,2048]{2,1,0:T(8,128)(2,1)}, bf16[4,96,2048]{2,1,0:T(8,128)(2,1)},...) custom-call(f32[8,768]{1,0:T(8,128)} %copy-done.3, ...), custom_call_target="tpu_custom_call" | custom-call | tf_op jit(solution)/shard_map/run_layers/pallas_call | solution.py:732
  159.8 118.4 %reduce_gradients.1 = (f32[2,4,24,7168]{3,2,1,0:T(8,128)}, f32[2,4,4,32,768]{4,3,2,1,0:T(8,128)}, bf16[2,128,896]{2,1,0:T(8,128)(2,1)}) custom-call(bf16[4,96,2048]{2,1,0:T(8,128)(2,1)} %get-tuple-element.24.refs_0_, bf16[4,96,2048]{2,1,0:T(8,128)(2,1)} %get-tuple-element.25.refs_1_, bf16[4,96,2048]{2,1,0:T(8,128)(2,1)} %get-tuple-element.26.refs_2_, ...), custom_call_target="tpu_custom_call" | custom-call | tf_op jit(solution)/shard_map/reduce_gradients/pallas_call | solution.py:1006
  278.3 0.0 copy-start
  278.3 5.4 %slice.13 = f32[2,96,7040]{2,1,0:T(8,128)} slice(f32[2,96,7168]{2,1,0:T(8,128)} %bitcast.9), slice={[0:2], [0:96], [0:7040]} | slice | bytes 10813440 | tf_op jit(solution)/shard_map/slice | solution.py:1052
  283.7 0.0 copy-done
  283.7 0.0 copy-start.2
  283.7 0.0 copy-start.1
  283.7 1.8 slice.14
  285.5 0.6 constant_dynamic-slice_fusion
  286.2 0.0 copy-done.2
  286.2 0.7 copy.15
  286.9 0.0 copy-done.1
  286.9 0.7 copy.16
  (6 shorter events, 0.1 us)
Async XLA Ops:
  1.7 0.6 copy-start.3
  278.3 5.5 %copy-start = (f32[2,4,4,32,768]{4,3,2,1,0:T(8,128)S(1)}, f32[2,4,4,32,768]{4,3,2,1,0:T(8,128)}, u32[]{:S(2)}) copy-start(f32[2,4,4,32,768]{4,3,2,1,0:T(8,128)} %get-tuple-element.37) | copy-start | bytes 9437188
  283.7 2.4 copy-start.2
  283.7 3.2 %copy-start.1 = (bf16[256,768]{1,0:T(8,128)(2,1)S(1)}, bf16[256,768]{1,0:T(8,128)(2,1)}, u32[]{:S(2)}) copy-start(bf16[256,768]{1,0:T(8,128)(2,1)} %get-tuple-element.23) | copy-start | bytes 1179652
